TPU v7x, 128 devices: a whole 4x4x4 slice. The times are simulated.
128 devices in a mesh: dom: 128 (over y, z, x, core).
Axes of the slice: x: 4, y: 4, z: 4, core: 2. Of those that a mesh axis runs over, the one named last changes fastest.
Arguments:
- features: bfloat16 [65536, 512], P('dom'), may hold values from -6 to 6
- weights: bfloat16 [3, 512, 512], replicated, may hold values from -0.078125 to 0.078125
- halo_send: int32 [128, 128, 4], P('dom'), may hold values from 0 to 511
- nbr_index: int32 [65536, 2, 8], P('dom'), may hold values from 0 to 1023
- tile_count: int32 [128], P('dom'), may hold values from 1 to 16, as said below
- edge_ends: int32 [2048, 2, 256], P('dom'), may hold values from 0 to 511
- neg_ids: int32 [1024], P('dom'), may hold values from 0 to 511
Outputs:
- weight_grad: float32 [3, 512, 512], replicated
- mean_loss: float32 [], replicated
- pre_grad: bfloat16 [65536, 512], P('dom')
Inputs may be any that keep to these rules, and one draw needn't show every extreme that they name: `nbr_index`: an entry below 512 names a row of the node's own partition; an entry 512 + q * 4 + k names slot k of the halo from partition q. `tile_count`: partition 128 - 1 holds 16 tiles; every other partition holds at most 8. `edge_ends`: tile slots at or past a partition's tile_count hold no edges. `neg_ids`: entry j names a row of partition j // 8.
All inputs are finite; a program needn't handle non-finite values.
Results may differ from a plain program's by a relative error of at most 0.0012.
The roundings to bfloat16 on the way count: a program that leaves them out, or rounds other values in their place, can miss the bound.
Values may be sent and summed in bfloat16 or wider, within the bound.
No kernel may reach another device: no remote copies, remote signals or barrier semaphores. Data moves between devices by JAX's collectives and lax.ppermute only.
A program may use at most 64 MiB of HBM per device.

v0:
```python
import jax
import jax.numpy as jnp
from jax import lax
from jax.experimental import pallas as pl
from jax.experimental.pallas import tpu as pltpu
from jax.sharding import Mesh
from jax.sharding import PartitionSpec as P

DOM = ("dom_0", "dom_1", "dom_2", "dom_3")
FAR = ("dom_0", "dom_1", "dom_2")
NEAR = ("dom_3",)
H = 512
RELS = 2
FAN = 8
TILE = 256
NODE_DEV = 512
NEG = 1024
NEG_DEV = 8
N_DOM = 128
HALO_PEER = 4
CHIPS = 64
GROUP = 4
HALF = 256
F32 = jnp.float32
BF16 = jnp.bfloat16
F16 = jnp.float16
SPAN = 60000.0
TINY = 1e-30
NT = (((1,), (1,)), ((), ()))
TN = (((0,), (0,)), ((), ()))
FROM_HBM = "hbm"


def swap(x, axes):
    return lax.all_to_all(x, axes, split_axis=0, concat_axis=0, tiled=True)


def core_swap(x):
    return lax.ppermute(x, "dom_3", [(0, 1), (1, 0)])


def dot(a, b):
    return jnp.dot(a, b, preferred_element_type=F32)


def split_two(x):
    high = x.astype(BF16)
    return high, (x - high.astype(F32)).astype(BF16)


def vmem():
    return pl.BlockSpec(memory_space=pltpu.VMEM)


def whole(shape):
    return pl.BlockSpec(shape, lambda i: (0,) * len(shape))


def weight_at(k):
    return pl.BlockSpec((1, H, H), lambda i: (k, 0, 0))


def smem():
    return pl.BlockSpec(memory_space=pltpu.SMEM)


def near_memory(x):
    return pltpu.with_memory_space_constraint(x, pltpu.VMEM)


def hbm(shape, kind):
    return pltpu.HBM(shape, kind)


def call(body, outs, specs, scratch=(), args=()):
    given = []
    for spec, x in zip(specs, args):
        if spec is FROM_HBM:
            x = pltpu.with_memory_space_constraint(x, pltpu.HBM)
        elif spec.memory_space == pltpu.VMEM and x.dtype != jnp.int32:
            x = near_memory(x)
        given.append(x)
    return pl.pallas_call(
        body,
        out_shape=[pltpu.VMEM(*o) if isinstance(o, tuple) else o for o in outs],
        grid=(1,),
        in_specs=[whole(x.shape) if spec is FROM_HBM else spec for spec, x in zip(specs, args)],
        out_specs=[vmem() if isinstance(o, tuple) else whole(o.shape) for o in outs],
        scratch_shapes=list(scratch),
        compiler_params=pltpu.CompilerParams(vmem_limit_bytes=28 << 20),
    )(*given)


def halo_body(send_ref, features_ref, out_ref):
    node = lax.broadcasted_iota(jnp.int32, (NODE_DEV, N_DOM), 0)
    own = features_ref[...]
    for k in range(HALO_PEER):
        hit = jnp.where(node == send_ref[k : k + 1, :], 1.0, 0.0).astype(BF16)
        out_ref[:, k, :] = lax.dot_general(hit, own, TN, preferred_element_type=F32).astype(BF16)


def counts_body(features_ref, w_ref, nbr_ref, halo_count_ref, own_sum_ref, pre_ref, own_count_ref):
    rows = 32
    lanes = lax.broadcasted_iota(jnp.int32, (rows, NODE_DEV), 1)

    def chunk(step, _):
        at = pl.ds(pl.multiple_of(step * rows, rows), rows)
        for r in range(RELS):
            index = nbr_ref[at, r * FAN : (r + 1) * FAN]
            for half in range(2):
                total = jnp.zeros((rows, NODE_DEV), F32)
                for k in range(FAN):
                    hit = lanes == (index[:, k : k + 1] - half * NODE_DEV)
                    total = total + jnp.where(hit, 1.0, 0.0)
                if half == 0:
                    own_count_ref[r, at, :] = total.astype(BF16)
                else:
                    halo_count_ref[r, at, :] = total.astype(BF16)
        return 0

    lax.fori_loop(0, NODE_DEV // rows, chunk, 0)
    own = features_ref[...]
    for r in range(RELS):
        own_sum_ref[r] = dot(own_count_ref[r], own)
    pre_ref[...] = dot(own, w_ref[0])


def layer_body(neg_ids_ref, halo_count_ref, halo_ref, own_sum_ref, pre_ref, first_ref, second_ref, means_ref, embed_ref, picked_ref):
    halo = halo_ref[...]
    preact = pre_ref[...]
    for r, w_ref in enumerate((first_ref, second_ref)):
        total = own_sum_ref[r] + dot(halo_count_ref[r], halo)
        mean = (total * (1.0 / FAN)).astype(BF16)
        means_ref[r] = mean
        preact = preact + dot(mean, w_ref[0])
    embed = preact.astype(BF16)
    embed_ref[...] = embed
    picked = dot(chosen_rows(neg_ids_ref), embed)[:NEG_DEV]
    picked_ref[...] = jnp.broadcast_to(picked[None], (CHIPS, NEG_DEV, H)).astype(BF16)


def soft_parts(x):
    small = jnp.exp(-jnp.abs(x))
    bottom = 1.0 / (1.0 + small)
    sigmoid = jnp.where(x >= 0, bottom, small * bottom)
    log_one = jnp.where(small < 1e-3, small * (1.0 - 0.5 * small), jnp.log(1.0 + small))
    return sigmoid, jnp.maximum(x, 0.0) + log_one


def largest(x):
    return jnp.max(jnp.max(jnp.abs(x), axis=0, keepdims=True), axis=1, keepdims=True)


def notes_of(values):
    lane = lax.broadcasted_iota(jnp.int32, (NEG_DEV, 128), 1)
    note = jnp.zeros((NEG_DEV, 128), F32)
    for place, value in enumerate(values):
        note = jnp.where(lane == place, value, note)
    return note


def positive_body(count_ref, embed_ref, ends_ref, features_ref, means_ref, grad_ref, note_ref, turned_ref, sources_ref, spread_ref, pairs_ref):
    tiles = count_ref[0]
    pairs_ref[...] = jnp.zeros((NODE_DEV, NODE_DEV), F32)
    node = lax.broadcasted_iota(jnp.int32, (NODE_DEV, TILE), 0)

    def group(step, _):
        sources, targets = [], []
        for j in range(GROUP):
            t = step * GROUP + j
            source = jnp.where(t < tiles, ends_ref[t, 0:1, :], -1)
            sources.append(jnp.where(node == source, 1.0, 0.0).astype(BF16))
            targets.append(jnp.where(node == ends_ref[t, 1:2, :], 1.0, 0.0).astype(BF16))
        pairs_ref[...] += lax.dot_general(
            jnp.concatenate(sources, axis=1), jnp.concatenate(targets, axis=1), NT, preferred_element_type=F32
        )
        return 0

    lax.fori_loop(0, (tiles + (GROUP - 1)) // GROUP, group, 0)
    embed = embed_ref[...]
    pairs = pairs_ref[...]
    sources = jnp.sum(pairs, axis=1, keepdims=True)
    sources_ref[...] = jnp.broadcast_to(sources, (NODE_DEV, 128))
    high, low = split_two(embed.astype(F32) * sources)
    spread_ref[:, 0:H] = high
    spread_ref[:, H:] = low
    scores = lax.dot_general(embed, embed, NT, preferred_element_type=F32)
    sigmoid, softplus = soft_parts(-scores)
    loss = jnp.sum(jnp.sum(pairs * softplus, axis=0, keepdims=True), axis=1, keepdims=True)
    widest = largest(features_ref[...].astype(F32))
    for r in range(RELS):
        widest = jnp.maximum(widest, largest(means_ref[r].astype(F32)))
    high, low = split_two(-((pairs + pairs.T) * sigmoid))
    base = dot(high, embed) + dot(low, embed)
    grad_ref[...] = base
    note_ref[...] = notes_of((loss, tiles.astype(F32), widest, NODE_DEV * largest(base)))
    turned_ref[0:H, :] = features_ref[...].T
    for r in range(RELS):
        turned_ref[(r + 1) * H : (r + 2) * H, :] = means_ref[r].T


def scored(embed, rows, sources, spread):
    scores = lax.dot_general(embed, rows, NT, preferred_element_type=F32)
    sigmoid, softplus = soft_parts(scores)
    per_source = jnp.sum(softplus, axis=1, keepdims=True)
    loss = jnp.sum(per_source * sources, axis=0, keepdims=True) * (1.0 / NEG)
    weight = (sigmoid * (1.0 / NEG)).astype(BF16)
    parts = lax.dot_general(weight, spread, TN, preferred_element_type=F32)
    return weight, loss, parts[:, :H] + parts[:, H:]


def near_body(embed_ref, rows_ref, spread_ref, sources_ref, note_in_ref, weight_ref, part_ref, note_ref):
    rows = rows_ref[...]
    weight, loss, part = scored(embed_ref[...], rows, sources_ref[:, 0:1], spread_ref[...])
    weight_ref[...] = weight
    part_ref[...] = part.astype(part_ref.dtype)
    note = note_in_ref[...]
    lane = lax.broadcasted_iota(jnp.int32, note.shape, 1)
    note = note + jnp.where(lane == 0, loss, 0.0)
    tallest = jnp.maximum(note, jnp.where(lane == 4, largest(rows.astype(F32)), 0.0))
    note = jnp.where(lane == 4, tallest, note)
    note_ref[...] = jnp.where(lane == 5, jnp.maximum(note, largest(part)), note)


def rest_body(near_weight_ref, near_rows_ref, weight_ref, rows_ref, sources_ref, base_ref, grad_ref):
    total = dot(near_weight_ref[...], near_rows_ref[...]) + dot(weight_ref[...], rows_ref[...])
    grad_ref[...] = base_ref[...] + sources_ref[:, 0:1] * total


def shared_note(note_ref):
    loss, tiles, widest, base, tallest, part = (note_ref[0:1, i : i + 1] for i in range(6))
    return loss, tiles, widest * (base + TILE * tiles * tallest), NEG_DEV * widest, part


def merge_body(part_ref, arrived_ref, own_note_ref, other_note_ref, send_ref):
    total = part_ref[...] + arrived_ref[...].astype(F32)
    send_ref[:, :, 0:H] = total.reshape(CHIPS, NEG_DEV, H).astype(BF16)
    both = zip(shared_note(own_note_ref), shared_note(other_note_ref))
    loss, tiles, known, wide, part = (own + other for own, other in both)
    first = loss.astype(BF16).astype(F32)
    second = (loss - first).astype(BF16).astype(F32)
    note = notes_of((first, second, (loss - first) - second, tiles, known, wide, part))
    send_ref[:, :, H:] = jnp.broadcast_to(note[None], (CHIPS, NEG_DEV, 128)).astype(BF16)


def chosen_rows(neg_ids_ref):
    row = lax.broadcasted_iota(jnp.int32, (16, NODE_DEV), 0)
    lane = lax.broadcasted_iota(jnp.int32, (16, NODE_DEV), 1)
    chosen = jnp.zeros((16, NODE_DEV), F32)
    for i in range(NEG_DEV):
        chosen = jnp.where((row == i) & (lane == neg_ids_ref[i]), 1.0, chosen)
    return chosen.astype(BF16)


def half_at(core):
    return pl.ds(pl.multiple_of(core * HALF, HALF), HALF)


def known_body(neg_ids_ref, core_ref, grad_ref, turned_ref, own_ref, other_ref, chosen_ref, pre_ref):
    node = lax.broadcasted_iota(jnp.int32, (NODE_DEV, H), 0)
    grad = grad_ref[...]
    for i in range(NEG_DEV):
        grad = jnp.where(node == neg_ids_ref[i], 0.0, grad)
    pre_ref[...] = grad.astype(BF16)
    turned = turned_ref[...]
    chosen = lax.dot_general(chosen_rows(neg_ids_ref), turned, NT, preferred_element_type=F32)
    chosen_ref[...] = chosen.astype(BF16)
    other_ref[...] = dot(turned, pre_ref[:, half_at(1 - core_ref[0])])
    own_ref[...] = dot(turned, pre_ref[:, half_at(core_ref[0])])


def outer_body(neg_ids_ref, core_ref, arrived_ref, grad_ref, pre_ref, own_ref, other_ref, note_ref, sum_ref, row_ref):
    total = jnp.sum(arrived_ref[...].astype(F32), axis=0)
    note_ref[...] = total[:, H:]
    sum_ref[...] = grad_ref[...]
    for i in range(NEG_DEV):
        at = pl.ds(neg_ids_ref[i], 1)
        sum_ref[at, :] += total[i : i + 1, 0:H]
    row_ref[...] = jnp.zeros((16, H), F32)
    for i in range(NEG_DEV):
        fresh = jnp.bool_(True)
        for j in range(i):
            fresh = fresh & (neg_ids_ref[j] != neg_ids_ref[i])
        row = sum_ref[pl.ds(neg_ids_ref[i], 1), :]
        row_ref[i : i + 1, :] = jnp.where(fresh, row, 0.0)
    pre_ref[...] = sum_ref[...].astype(BF16)
    own_ref[...] = row_ref[:, half_at(core_ref[0])].astype(BF16)
    other_ref[...] = row_ref[:, half_at(1 - core_ref[0])].astype(BF16)


def update_body(known_ref, own_chosen_ref, other_chosen_ref, own_row_ref, other_row_ref, note_ref, out_ref):
    chosen = jnp.concatenate([own_chosen_ref[...], other_chosen_ref[...]], axis=0)
    rows = jnp.concatenate([own_row_ref[...], other_row_ref[...]], axis=0)
    extra = lax.dot_general(chosen, rows, TN, preferred_element_type=F32)
    out_ref[...] = (known_ref[...] + extra) * scale_of(note_ref)


def scale_of(note_ref):
    known, wide, part = (note_ref[0:1, i : i + 1] for i in (4, 5, 6))
    return SPAN / (known + wide * part + TINY)


def factor_of(note_ref):
    return 1.0 / scale_of(note_ref) / (note_ref[0:1, 3:4] * TILE)


def first_half_body(core_ref, half_ref, note_ref, weight_ref, loss_ref):
    note = note_ref[0:1, :]
    loss = note[:, 0:1] + note[:, 1:2] + note[:, 2:3]
    loss_ref[...] = loss / (note[:, 3:4] * TILE)
    weight_ref[...] = (half_ref[...] * factor_of(note_ref)).reshape(RELS + 1, H, HALF)


def second_half_body(core_ref, half_ref, note_ref, begun_ref, weight_ref):
    weight_ref[...] = (half_ref[...] * factor_of(note_ref)).reshape(RELS + 1, H, HALF)


def halves(body, which, extra, alias):
    whole = jax.ShapeDtypeStruct((RELS + 1, H, H), F32)
    block = pl.BlockSpec((RELS + 1, H, HALF), lambda i, core: (0, 0, which(core[0])))
    scalar = pl.BlockSpec((1, 1), lambda i, core: (0, 0))
    full = vmem()
    note = vmem()
    return pl.pallas_call(
        body,
        out_shape=[whole, jax.ShapeDtypeStruct((1, 1), F32)][: 1 + extra],
        grid_spec=pltpu.PrefetchScalarGridSpec(
            num_scalar_prefetch=1,
            grid=(1,),
            in_specs=[full, note] + [pl.BlockSpec(memory_space=pl.ANY)] * len(alias),
            out_specs=[block, scalar][: 1 + extra],
        ),
        input_output_aliases=alias,
        compiler_params=pltpu.CompilerParams(vmem_limit_bytes=28 << 20),
    )


def on_device(features, weights, halo_send, nbr_index, tile_count, edge_ends, neg_ids):
    square = (NODE_DEV, H)
    tall = ((RELS + 1) * H, HALF)
    core = lax.axis_index(NEAR).astype(jnp.int32).reshape(1)
    core, halo_send = lax.optimization_barrier((core, halo_send))
    (outgoing,) = call(halo_body, [hbm((N_DOM, HALO_PEER, H), BF16)], [vmem(), whole((NODE_DEV, H))], (), (halo_send[0].T, features))
    incoming = swap(outgoing, DOM)
    neighbours = nbr_index.reshape(NODE_DEV, RELS * FAN)
    halo_count, own_sum, pre = call(
        counts_body,
        [hbm((RELS, NODE_DEV, 512), BF16), hbm((RELS, *square), F32), hbm(square, F32)],
        [FROM_HBM, weight_at(0), vmem()],
        [pltpu.VMEM((RELS, NODE_DEV, NODE_DEV), BF16)],
        (features, weights, neighbours),
    )
    means, embed, picked = call(
        layer_body,
        [hbm((RELS, *square), BF16), (square, BF16), hbm((CHIPS, NEG_DEV, H), BF16)],
        [smem(), FROM_HBM, vmem(), FROM_HBM, FROM_HBM, weight_at(1), weight_at(2)],
        (),
        (neg_ids, halo_count, incoming.reshape(512, H), own_sum, pre, weights, weights),
    )
    near_rows = swap(picked, FAR).reshape(square)
    base, note, turned, sources, spread = call(
        positive_body,
        [hbm(square, F32), ((8, 128), F32), hbm(((RELS + 1) * H, NODE_DEV), BF16), ((NODE_DEV, 128), F32), ((NODE_DEV, 2 * H), BF16)],
        [smem(), vmem(), vmem(), FROM_HBM, FROM_HBM],
        [pltpu.VMEM((NODE_DEV, NODE_DEV), F32)],
        (tile_count, embed, edge_ends, features, means),
    )
    near_rows, note = lax.optimization_barrier((near_rows, note))
    other_rows = core_swap(near_rows)
    near_weight, near_part, note = call(
        near_body,
        [(square, BF16), (square, F32), ((8, 128), F32)],
        [vmem()] * 5,
        (),
        (embed, near_rows, spread, sources, note),
    )
    weight, other_part, note = call(
        near_body,
        [(square, BF16), (square, BF16), ((8, 128), F32)],
        [vmem()] * 5,
        (),
        (embed, other_rows, spread, sources, note),
    )
    other_note = core_swap(note)
    part_arrived = core_swap(other_part)
    (grad,) = call(
        rest_body,
        [(square, F32)],
        [vmem()] * 5 + [FROM_HBM],
        (),
        (near_weight, near_rows, weight, other_rows, sources, base),
    )
    part_arrived, grad = lax.optimization_barrier((part_arrived, grad))
    (outgoing_grad,) = call(
        merge_body,
        [hbm((CHIPS, NEG_DEV, H + 128), BF16)],
        [vmem()] * 4,
        (),
        (near_part, part_arrived, note, other_note),
    )
    outgoing_grad, grad = lax.optimization_barrier((outgoing_grad, grad))
    arrived = swap(outgoing_grad, FAR)
    known_own, known_other, chosen = call(
        known_body,
        [(tall, F32), (tall, F32), ((16, (RELS + 1) * H), BF16)],
        [smem(), smem(), vmem(), FROM_HBM],
        [pltpu.VMEM(square, BF16)],
        (neg_ids, core, grad, turned),
    )
    other_chosen = core_swap(chosen)
    known = known_own + core_swap(known_other)
    arrived, known, other_chosen = lax.optimization_barrier((arrived, known, other_chosen))
    pre_grad, own_row, send_row, note = call(
        outer_body,
        [hbm(square, BF16), ((16, HALF), BF16), ((16, HALF), BF16), ((NEG_DEV, 128), F32)],
        [smem(), smem(), vmem(), vmem()],
        [pltpu.VMEM(square, F32), pltpu.VMEM((16, H), F32)],
        (neg_ids, core, arrived, grad),
    )
    (partial,) = call(
        update_body,
        [(tall, F32)],
        [vmem()] * 6,
        (),
        (known, chosen, other_chosen, own_row, core_swap(send_row), note),
    )
    chunks = (CHIPS, 24, HALF)
    mine = jnp.sum(swap(partial.astype(F16).reshape(chunks), FAR).astype(F32), axis=0).astype(F16)
    half = swap(jnp.broadcast_to(mine, chunks), FAR).reshape(tall)
    other_half = core_swap(half).astype(F32)
    half = half.astype(F32)
    note = near_memory(note)
    begun, mean_loss = halves(first_half_body, lambda c: c, 1, {})(core, near_memory(half), note)
    (begun, other_half) = lax.optimization_barrier((begun, other_half))
    (weight_grad,) = halves(second_half_body, lambda c: 1 - c, 0, {3: 0})(core, near_memory(other_half), note, begun)
    return weight_grad, mean_loss.reshape(()), pre_grad


def solution(mesh):
    torus = Mesh(mesh.devices.reshape(4, 4, 4, 2), DOM)
    in_specs = (
        P(DOM, None),
        P(),
        P(DOM, None, None),
        P(DOM, None, None),
        P(DOM),
        P(DOM, None, None),
        P(DOM),
    )
    out_specs = (P(), P(), P(DOM, None))
    return jax.shard_map(on_device, mesh=torus, in_specs=in_specs, out_specs=out_specs, check_vma=False)
```

profile of v0, /device:TPU:1, one launch (start us, length us, event | category | flops | bytes accessed | tf_op | source)
XLA Modules:
  0.0 134.0 jit_solution(7076995651706042644)
XLA Ops:
  0.7 1.1 copy-done.1
  1.8 0.7 copy-done.5
  2.5 1.4 %shard_map.95 = bf16[128,4,512]{2,1,0:T(4,128)(2,1)} custom-call(s32[4,128]{1,0:T(4,128)S(1)} %bitcast.13, bf16[512,512]{1,0:T(8,128)(2,1)S(1)} %copy-done.1), custom_call_target="tpu_custom_call" | custom-call | tf_op jit(solution)/shard_map/pallas_call | solution.py:83
  3.9 11.5 %all-to-all-start = ((bf16[128,4,512]{2,1,0:T(4,128)(2,1)}), bf16[128,4,512]{2,1,0:T(4,128)(2,1)S(1)}, u32[]{:S(2)}, u32[]{:S(2)}) async-start(bf16[128,4,512]{2,1,0:T(4,128)(2,1)} %shard_map.95), calls=%async_computation | async-start | bytes 1048576 | tf_op jit(solution)/shard_map/all_to_all | solution.py:35
  15.6 8.4 %shard_map.94 = (bf16[2,512,512]{2,1,0:T(8,128)(2,1)}, f32[2,512,512]{2,1,0:T(8,128)}, f32[512,512]{1,0:T(8,128)}) custom-call(bf16[512,512]{1,0:T(8,128)(2,1)} %features_ref.5, bf16[3,512,512]{2,1,0:T(8,128)(2,1)S(1)} %copy-done, s32[512,16]{1,0:T(8,128)S(1)} %copy.12.nbr_ref), custom_call_target="tpu_custom_call" | custom-call | tf_op jit(solution)/shard_map/pallas_call | solution.py:83
  24.0 5.0 %all-to-all-done = bf16[128,4,512]{2,1,0:T(4,128)(2,1)S(1)} async-done(((bf16[128,4,512]{2,1,0:T(4,128)(2,1)}), bf16[128,4,512]{2,1,0:T(4,128)(2,1)S(1)}, u32[]{:S(2)}, u32[]{:S(2)}) %all-to-all-start) | async-done | bytes 524320 | tf_op jit(solution)/shard_map/all_to_all | solution.py:35
  29.2 4.4 %shard_map.96 = (bf16[2,512,512]{2,1,0:T(8,128)(2,1)}, bf16[512,512]{1,0:T(8,128)(2,1)S(1)}, bf16[64,8,512]{2,1,0:T(8,128)(2,1)}) custom-call(s32[8]{0:T(128)S(1)} %copy-done.4, bf16[2,512,512]{2,1,0:T(8,128)(2,1)} %get-tuple-element.43.halo_count_ref, bf16[512,512]{1,0:T(8,128)(2,1)S(1)} %reshape.29.halo_ref, f32[2,512,512]{2,1,0:T(8,128)} %get-tuple-element.45.own_sum_ref, ...), custom_call_target="tpu_custom_call" | custom-call | tf_op jit(solution)/shard_map/pallas_call | solution.py:83
  33.6 5.5 %all-to-all-start.1 = ((bf16[64,8,512]{2,1,0:T(8,128)(2,1)}), bf16[64,8,512]{2,1,0:T(8,128)(2,1)S(1)}, u32[]{:S(2)}, u32[]{:S(2)}) async-start(bf16[64,8,512]{2,1,0:T(8,128)(2,1)} %get-tuple-element.48), calls=%async_computation.1 | async-start | bytes 1048576 | tf_op jit(solution)/shard_map/all_to_all | solution.py:35
  39.7 5.7 %shard_map.97 = (f32[512,512]{1,0:T(8,128)}, f32[8,128]{1,0:T(8,128)S(1)}, bf16[1536,512]{1,0:T(8,128)(2,1)}, f32[512,128]{1,0:T(8,128)S(1)}, bf16[512,1024]{1,0:T(8,128)(2,1)S(1)}) custom-call(s32[1]{0:T(128)S(6)} %copy.14.count_ref, bf16[512,512]{1,0:T(8,128)(2,1)S(1)} %get-tuple-element.47.embed_ref, s32[16,2,256]{2,1,0:T(2,128)S(1)} %copy-done.3, ...), custom_call_target="tpu_custom_call" | custom-call | tf_op jit(solution)/shard_map/pallas_call | solution.py:83
  45.4 6.1 %all-to-all-done.1 = bf16[64,8,512]{2,1,0:T(8,128)(2,1)S(1)} async-done(((bf16[64,8,512]{2,1,0:T(8,128)(2,1)}), bf16[64,8,512]{2,1,0:T(8,128)(2,1)S(1)}, u32[]{:S(2)}, u32[]{:S(2)}) %all-to-all-start.1) | async-done | bytes 524320 | tf_op jit(solution)/shard_map/all_to_all | solution.py:35
  51.5 2.0 %collective-permute-start = (bf16[512,512]{1,0:T(8,128)(2,1)S(1)}, bf16[512,512]{1,0:T(8,128)(2,1)S(1)}, u32[]{:S(2)}, u32[]{:S(2)}) collective-permute-start(bf16[512,512]{1,0:T(8,128)(2,1)S(1)} %bitcast.10), channel_id=1, source_target_pairs={{0,1},{1,0},{2,3},{3,2},{4,5},{5,4},{6,7},{7,6},{8,9},{9,8},{10,11... | collective-permute-start | bytes 1572872 | tf_op jit(solution)/shard_map/ppermute | solution.py:39
  53.5 1.8 %shard_map.98 = (bf16[512,512]{1,0:T(8,128)(2,1)S(1)}, f32[512,512]{1,0:T(8,128)S(1)}, f32[8,128]{1,0:T(8,128)S(1)}) custom-call(bf16[512,512]{1,0:T(8,128)(2,1)S(1)} %get-tuple-element.47.embed_ref, bf16[512,512]{1,0:T(8,128)(2,1)S(1)} %bitcast.11, bf16[512,1024]{1,0:T(8,128)(2,1)S(1)} %get-tuple-element.52.spread_ref, ...), custom_call_target="tpu_custom_call" | custom-call | tf_op jit(solution)/shard_map/pallas_call | solution.py:83
  55.3 1.8 %shard_map.99 = (bf16[512,512]{1,0:T(8,128)(2,1)S(1)}, bf16[512,512]{1,0:T(8,128)(2,1)S(1)}, f32[8,128]{1,0:T(8,128)S(1)}) custom-call(bf16[512,512]{1,0:T(8,128)(2,1)S(1)} %get-tuple-element.47.embed_ref, bf16[512,512]{1,0:T(8,128)(2,1)S(1)} %collective-permute-done.rows_ref, bf16[512,1024]{1,0:T(8,128)(2,1)S(1)} %get-tuple-element.52.spread_ref, ...), custom_call_target="tpu_custom_call" | custom-call | tf_op jit(solution)/shard_map/pallas_call | solution.py:83
  57.2 0.4 collective-permute-start.2
  57.7 1.9 %shard_map.100.grad_ref = f32[512,512]{1,0:T(8,128)S(1)} custom-call(bf16[512,512]{1,0:T(8,128)(2,1)S(1)} %get-tuple-element.58.near_weight_ref, bf16[512,512]{1,0:T(8,128)(2,1)S(1)} %bitcast.12, bf16[512,512]{1,0:T(8,128)(2,1)S(1)} %get-tuple-element.59.weight_ref, bf16[512,512]{1,0:T(8,128)(2,1)S(1)} %collective-permute-done.rows_ref, ...), custom_call_target="tpu_custom_call" | custom-call | tf_op jit(solution)/shard_map/pallas_call | solution.py:83
  59.6 1.4 %shard_map.101 = bf16[64,8,640]{2,1,0:T(8,128)(2,1)} custom-call(f32[512,512]{1,0:T(8,128)S(1)} %get-tuple-element.55.part_ref, bf16[512,512]{1,0:T(8,128)(2,1)S(1)} %collective-permute-done.1.arrived_ref, f32[8,128]{1,0:T(8,128)S(1)} %get-tuple-element.62.own_note_ref, f32[8,128]{1,0:T(8,128)S(1)} %collective-permute-done.2.other_note_ref), custom_call_target="tpu_custom_call" | custom-call | tf_op jit(solution)/shard_map/pallas_call | solution.py:83
  61.0 3.5 %shard_map.102 = (f32[1536,256]{1,0:T(8,128)S(1)}, f32[1536,256]{1,0:T(8,128)S(1)}, bf16[16,1536]{1,0:T(8,128)(2,1)S(1)}) custom-call(s32[8]{0:T(128)S(1)} %copy-done.4, s32[1]{0:T(128)} %bitcast.core_ref, f32[512,512]{1,0:T(8,128)S(1)} %shard_map.100.grad_ref, bf16[1536,512]{1,0:T(8,128)(2,1)} %get-tuple-element.66.turned_ref), custom_call_target="tpu_custom_call" | custom-call | tf_op jit(solution)/shard_map/pallas_call | solution.py:83
  64.5 1.1 copy-done.2
  65.6 0.3 collective-permute-start.3
  65.9 4.6 %all-to-all-start.2 = ((bf16[64,8,640]{2,1,0:T(8,128)(2,1)}), bf16[64,8,640]{2,1,0:T(8,128)(2,1)S(1)}, u32[]{:S(2)}, u32[]{:S(2)}) async-start(bf16[64,8,640]{2,1,0:T(8,128)(2,1)} %shard_map.101), calls=%async_computation.2 | async-start | bytes 1310720 | tf_op jit(solution)/shard_map/all_to_all | solution.py:35
  70.5 0.3 collective-permute-start.4
  70.8 2.1 %add.3.known_ref = f32[1536,256]{1,0:T(8,128)S(1)} add(f32[1536,256]{1,0:T(8,128)} %copy-done.2, f32[1536,256]{1,0:T(8,128)} %collective-permute-done.3) | non-fusion elementwise | flops 393216 | bytes 4718592 | tf_op jit(solution)/shard_map/add | solution.py:411
  72.9 11.8 %all-to-all-done.2.arrived_ref = bf16[64,8,640]{2,1,0:T(8,128)(2,1)S(1)} async-done(((bf16[64,8,640]{2,1,0:T(8,128)(2,1)}), bf16[64,8,640]{2,1,0:T(8,128)(2,1)S(1)}, u32[]{:S(2)}, u32[]{:S(2)}) %all-to-all-start.2) | async-done | bytes 655392 | tf_op jit(solution)/shard_map/all_to_all | solution.py:35
  84.8 1.5 %shard_map.103 = (bf16[512,512]{1,0:T(8,128)(2,1)}, bf16[16,256]{1,0:T(8,128)(2,1)S(1)}, bf16[16,256]{1,0:T(8,128)(2,1)S(1)}, f32[8,128]{1,0:T(8,128)S(1)}) custom-call(s32[8]{0:T(128)S(1)} %copy-done.4, s32[1]{0:T(128)} %bitcast.core_ref, bf16[64,8,640]{2,1,0:T(8,128)(2,1)S(1)} %all-to-all-done.2.arrived_ref, f32[512,512]{1,0:T(8,128)S(1)} %shard_map.100.grad_ref), custom_call_target="tpu_custom_call" | custom-call | tf_op jit(solution)/shard_map/pallas_call | solution.py:83
  86.3 1.5 %collective-permute-start.5 = (bf16[16,256]{1,0:T(8,128)(2,1)S(1)}, bf16[16,256]{1,0:T(8,128)(2,1)S(1)}, u32[]{:S(2)}, u32[]{:S(2)}) collective-permute-start(bf16[16,256]{1,0:T(8,128)(2,1)S(1)} %get-tuple-element.74), channel_id=1, source_target_pairs={{0,1},{1,0},{2,3},{3,2},{4,5},{5,4},{6,7},{7,6},{8,9},{9,8},{10,11... | collective-permute-start | bytes 24584 | tf_op jit(solution)/shard_map/ppermute | solution.py:39
  87.8 0.8 collective-permute-done.5.other_row_ref
  88.7 0.6 shard_map.104
  89.4 19.4 %all_to_all.25 = f16[64,24,256]{2,1,0:T(8,128)(2,1)S(1)} all-to-all(f16[64,24,256]{2,1,0:T(8,128)(2,1)S(1)} %bitcast.15), channel_id=1, replica_groups=mesh['dom_0'=4,'dom_1'=4,'dom_2'=4,'dom_3'=2] {'dom_0','dom_1','dom_2'}, dimensions={0} | all-to-all | bytes 1572864 | tf_op jit(solution)/shard_map/all_to_all | solution.py:35
  109.0 18.5 %all_to_all.26 = f16[64,24,256]{2,1,0:T(8,128)(2,1)S(1)} all-to-all(f16[64,24,256]{2,1,0:T(8,128)(2,1)S(1)} %broadcast_in_dim.3), channel_id=1, replica_groups=mesh['dom_0'=4,'dom_1'=4,'dom_2'=4,'dom_3'=2] {'dom_0','dom_1','dom_2'}, dimensions={0} | all-to-all | bytes 1572864 | tf_op jit(solution)/shard_map/all_to_all | solution.py:35
  127.5 2.9 %collective-permute-start.6 = (f16[1536,256]{1,0:T(8,128)(2,1)S(1)}, f16[1536,256]{1,0:T(8,128)(2,1)S(1)}, u32[]{:S(2)}, u32[]{:S(2)}) collective-permute-start(f16[1536,256]{1,0:T(8,128)(2,1)S(1)} %bitcast.14), channel_id=1, source_target_pairs={{0,1},{1,0},{2,3},{3,2},{4,5},{5,4},{6,7},{7,6},{8,9},{9,8},{10,11... | collective-permute-start | bytes 2359304 | tf_op jit(solution)/shard_map/ppermute | solution.py:39
  130.6 1.5 %shard_map.105 = (f32[3,512,512]{2,1,0:T(8,128)}, f32[1,1]{1,0:T(1,128)}) custom-call(s32[1]{0:T(128)} %bitcast.core_ref, f32[1536,256]{1,0:T(8,128)S(1)} %bitcast_convert_fusion.half_ref, f32[8,128]{1,0:T(8,128)S(1)} %get-tuple-element.75.note_ref), custom_call_target="tpu_custom_call" | custom-call | tf_op jit(solution)/shard_map/pallas_call | solution.py:433
  132.4 1.5 %shard_map.106 = f32[3,512,512]{2,1,0:T(8,128)} custom-call(s32[1]{0:T(128)} %bitcast.core_ref, f32[1536,256]{1,0:T(8,128)S(1)} %convert_element_type.19.half_ref, f32[8,128]{1,0:T(8,128)S(1)} %get-tuple-element.75.note_ref, f32[3,512,512]{2,1,0:T(8,128)} %get-tuple-element.78.begun_ref), custom_call_target="tpu_custom_call", output_to_operand_aliasing={{}: (3, {})} | custom-call | tf_op jit(solution)/shard_map/pallas_call | solution.py:435
  (26 shorter events, 1.3 us)
Async XLA Ops:
  0.6 14.9 %copy-start = (bf16[3,512,512]{2,1,0:T(8,128)(2,1)S(1)}, bf16[3,512,512]{2,1,0:T(8,128)(2,1)}, u32[]{:S(2)}) copy-start(bf16[3,512,512]{2,1,0:T(8,128)(2,1)} %second_ref.1) | copy-start | bytes 4718596
  0.6 1.2 copy-start.1
  1.8 0.7 copy-start.5
  2.5 12.9 %copy-start.6 = (s32[512,2,8]{0,2,1:T(8,128)S(1)}, s32[512,2,8]{0,2,1:T(8,128)}, u32[]{:S(2)}) copy-start(s32[512,2,8]{0,2,1:T(8,128)} %param.10) | copy-start | bytes 98308
  3.9 25.1 %all-to-all-start = ((bf16[128,4,512]{2,1,0:T(4,128)(2,1)}), bf16[128,4,512]{2,1,0:T(4,128)(2,1)S(1)}, u32[]{:S(2)}, u32[]{:S(2)}) async-start(bf16[128,4,512]{2,1,0:T(4,128)(2,1)} %shard_map.95), calls=%async_computation | async-start | bytes 1048576 | tf_op jit(solution)/shard_map/all_to_all | solution.py:35
  15.6 13.6 %copy-start.4 = (s32[8]{0:T(128)S(1)}, s32[8]{0:T(128)}, u32[]{:S(2)}) copy-start(s32[8]{0:T(128)} %neg_ids_ref.5) | copy-start | bytes 100
  29.2 10.6 %copy-start.3 = (s32[16,2,256]{2,1,0:T(2,128)S(1)}, s32[16,2,256]{2,1,0:T(2,128)}, u32[]{:S(2)}) copy-start(s32[16,2,256]{2,1,0:T(2,128)} %ends_ref.1) | copy-start | bytes 98308
  33.6 18.0 %all-to-all-start.1 = ((bf16[64,8,512]{2,1,0:T(8,128)(2,1)}), bf16[64,8,512]{2,1,0:T(8,128)(2,1)S(1)}, u32[]{:S(2)}, u32[]{:S(2)}) async-start(bf16[64,8,512]{2,1,0:T(8,128)(2,1)} %get-tuple-element.48), calls=%async_computation.1 | async-start | bytes 1048576 | tf_op jit(solution)/shard_map/all_to_all | solution.py:35
  51.5 3.8 %collective-permute-start = (bf16[512,512]{1,0:T(8,128)(2,1)S(1)}, bf16[512,512]{1,0:T(8,128)(2,1)S(1)}, u32[]{:S(2)}, u32[]{:S(2)}) collective-permute-start(bf16[512,512]{1,0:T(8,128)(2,1)S(1)} %bitcast.10), channel_id=1, source_target_pairs={{0,1},{1,0},{2,3},{3,2},{4,5},{5,4},{6,7},{7,6},{8,9},{9,8},{10,11... | collective-permute-start | bytes 1572872 | tf_op jit(solution)/shard_map/ppermute | solution.py:39
  57.1 2.5 %collective-permute-start.1 = (bf16[512,512]{1,0:T(8,128)(2,1)S(1)}, bf16[512,512]{1,0:T(8,128)(2,1)S(1)}, u32[]{:S(2)}, u32[]{:S(2)}) collective-permute-start(bf16[512,512]{1,0:T(8,128)(2,1)S(1)} %get-tuple-element.57), channel_id=1, source_target_pairs={{0,1},{1,0},{2,3},{3,2},{4,5},{5,4},{6,7},{7,6},{8,9},{9,8},{10,11... | collective-permute-start | bytes 1572872 | tf_op jit(solution)/shard_map/ppermute | solution.py:39
  57.2 2.4 %collective-permute-start.2 = (f32[8,128]{1,0:T(8,128)S(1)}, f32[8,128]{1,0:T(8,128)S(1)}, u32[]{:S(2)}, u32[]{:S(2)}) collective-permute-start(f32[8,128]{1,0:T(8,128)S(1)} %get-tuple-element.62.own_note_ref), channel_id=1, source_target_pairs={{0,1},{1,0},{2,3},{3,2},{4,5},{5,4},{6,7},{7,6},{8,9},{9,8},{10,11... | collective-permute-start | bytes 12296 | tf_op jit(solution)/shard_map/ppermute | solution.py:39
  64.4 1.1 copy-start.2
  65.6 5.2 %collective-permute-start.3 = (f32[1536,256]{1,0:T(8,128)S(1)}, f32[1536,256]{1,0:T(8,128)}, u32[]{:S(2)}, u32[]{:S(2)}) collective-permute-start(f32[1536,256]{1,0:T(8,128)S(1)} %get-tuple-element.68), channel_id=1, source_target_pairs={{0,1},{1,0},{2,3},{3,2},{4,5},{5,4},{6,7},{7,6},{8,9},{9,8},{10,11... | collective-permute-start | bytes 4718600 | tf_op jit(solution)/shard_map/ppermute | solution.py:39
  65.9 18.9 %all-to-all-start.2 = ((bf16[64,8,640]{2,1,0:T(8,128)(2,1)}), bf16[64,8,640]{2,1,0:T(8,128)(2,1)S(1)}, u32[]{:S(2)}, u32[]{:S(2)}) async-start(bf16[64,8,640]{2,1,0:T(8,128)(2,1)} %shard_map.101), calls=%async_computation.2 | async-start | bytes 1310720 | tf_op jit(solution)/shard_map/all_to_all | solution.py:35
  70.5 2.4 %collective-permute-start.4 = (bf16[16,1536]{1,0:T(8,128)(2,1)S(1)}, bf16[16,1536]{1,0:T(8,128)(2,1)S(1)}, u32[]{:S(2)}, u32[]{:S(2)}) collective-permute-start(bf16[16,1536]{1,0:T(8,128)(2,1)S(1)} %get-tuple-element.69.own_chosen_ref), channel_id=1, source_target_pairs={{0,1},{1,0},{2,3},{3,2},{4,5},{5,4},{6,7},{7,6},{8,9},{9,8},{10,11... | collective-permute-start | bytes 147464 | tf_op jit(solution)/shard_map/ppermute | solution.py:39
  86.3 2.4 %collective-permute-start.5 = (bf16[16,256]{1,0:T(8,128)(2,1)S(1)}, bf16[16,256]{1,0:T(8,128)(2,1)S(1)}, u32[]{:S(2)}, u32[]{:S(2)}) collective-permute-start(bf16[16,256]{1,0:T(8,128)(2,1)S(1)} %get-tuple-element.74), channel_id=1, source_target_pairs={{0,1},{1,0},{2,3},{3,2},{4,5},{5,4},{6,7},{7,6},{8,9},{9,8},{10,11... | collective-permute-start | bytes 24584 | tf_op jit(solution)/shard_map/ppermute | solution.py:39
  127.5 4.8 %collective-permute-start.6 = (f16[1536,256]{1,0:T(8,128)(2,1)S(1)}, f16[1536,256]{1,0:T(8,128)(2,1)S(1)}, u32[]{:S(2)}, u32[]{:S(2)}) collective-permute-start(f16[1536,256]{1,0:T(8,128)(2,1)S(1)} %bitcast.14), channel_id=1, source_target_pairs={{0,1},{1,0},{2,3},{3,2},{4,5},{5,4},{6,7},{7,6},{8,9},{9,8},{10,11... | collective-permute-start | bytes 2359304 | tf_op jit(solution)/shard_map/ppermute | solution.py:39
where the time goes:
time: 135 us; the launch traced here: 134 us
  blocking collectives  37.9 us (28%)
  Pallas kernels  35.4 us (26%)
  starting transfers between devices  29.1 us (22%)
  waiting for transfers between devices  24.1 us (18%)
  local copies, waits for them, and re-layouts  3.3 us (2%)
  other arithmetic  2.67 us (2%)
  between operations  1.48 us (1%)
    all_to_all x2, blocking collectives, swap(): return lax.all_to_all(x, axes, split_axis=0, concat_axis=0, tiled=True)  37.9 us
    pallas_call x11, Pallas kernels, call(): pl.pallas_call(body, out_shape=[pltpu.VMEM(*o) if isinstance(o, tuple) el...  32.4 us
    all_to_all x3, waiting for transfers between devices, swap(): return lax.all_to_all(x, axes, split_axis=0, concat_axis=0, tiled=True)  23 us
    all_to_all x3, starting transfers between devices, swap(): return lax.all_to_all(x, axes, split_axis=0, concat_axis=0, tiled=True)  21.6 us
    ppermute x7, starting transfers between devices, core_swap(): return lax.ppermute(x, 'dom_3', [(0, 1), (1, 0)])  7.51 us
    unnamed x14, local copies, waits for them, and re-layouts  2.99 us
  transfers between devices with their start and end apart: 10, of which 5 were waited for; matrix products, arithmetic and copies ran while one was open for 2% of the time, Pallas kernels for 14%

commit v1 on v0

--- a/solution.py
+++ b/solution.py
@@ -125,18 +125,44 @@
     pre_ref[...] = dot(own, w_ref[0])
 
 
-def layer_body(neg_ids_ref, halo_count_ref, halo_ref, own_sum_ref, pre_ref, first_ref, second_ref, means_ref, embed_ref, picked_ref):
-    halo = halo_ref[...]
-    preact = pre_ref[...]
-    for r, w_ref in enumerate((first_ref, second_ref)):
-        total = own_sum_ref[r] + dot(halo_count_ref[r], halo)
-        mean = (total * (1.0 / FAN)).astype(BF16)
-        means_ref[r] = mean
-        preact = preact + dot(mean, w_ref[0])
-    embed = preact.astype(BF16)
-    embed_ref[...] = embed
-    picked = dot(chosen_rows(neg_ids_ref), embed)[:NEG_DEV]
-    picked_ref[...] = jnp.broadcast_to(picked[None], (CHIPS, NEG_DEV, H)).astype(BF16)
+def layer_body(neg_ids_ref, halo_count_ref, halo_ref, own_sum_ref, pre_ref, w_ref, mean_ref, embed_ref, picked_ref, total_ref):
+    r = pl.program_id(0)
+    total = own_sum_ref[0] + dot(halo_count_ref[0], halo_ref[...])
+    mean = (total * (1.0 / FAN)).astype(BF16)
+    mean_ref[0] = mean
+    part = dot(mean, w_ref[0])
+
+    @pl.when(r == 0)
+    def _():
+        total_ref[...] = pre_ref[...] + part
+
+    @pl.when(r == RELS - 1)
+    def _():
+        embed = (total_ref[...] + part).astype(BF16)
+        embed_ref[...] = embed
+        picked = dot(chosen_rows(neg_ids_ref), embed)[:NEG_DEV]
+        picked_ref[...] = jnp.broadcast_to(picked[None], (CHIPS, NEG_DEV, H)).astype(BF16)
+
+
+def layer(neg_ids, halo_count, halo, own_sum, pre, weights):
+    per_relation = pl.BlockSpec((1, NODE_DEV, H), lambda r: (r, 0, 0))
+    from_hbm = lambda x: pltpu.with_memory_space_constraint(x, pltpu.HBM)
+    return pl.pallas_call(
+        layer_body,
+        out_shape=[hbm((RELS, NODE_DEV, H), BF16), pltpu.VMEM((NODE_DEV, H), BF16), hbm((CHIPS, NEG_DEV, H), BF16)],
+        grid=(RELS,),
+        in_specs=[
+            smem(),
+            per_relation,
+            vmem(),
+            per_relation,
+            pl.BlockSpec((NODE_DEV, H), lambda r: (0, 0)),
+            pl.BlockSpec((1, H, H), lambda r: (r + 1, 0, 0)),
+        ],
+        out_specs=[per_relation, vmem(), pl.BlockSpec((CHIPS, NEG_DEV, H), lambda r: (0, 0, 0))],
+        scratch_shapes=[pltpu.VMEM((NODE_DEV, H), F32)],
+        compiler_params=pltpu.CompilerParams(vmem_limit_bytes=28 << 20),
+    )(neg_ids, from_hbm(halo_count), near_memory(halo), from_hbm(own_sum), from_hbm(pre), from_hbm(weights))
 
 
 def soft_parts(x):
@@ -159,10 +185,18 @@
     return note
 
 
-def positive_body(count_ref, embed_ref, ends_ref, features_ref, means_ref, grad_ref, note_ref, turned_ref, sources_ref, spread_ref, pairs_ref):
-    tiles = count_ref[0]
+def positive_body(count_ref, embed_ref, ends_ref, features_ref, means_ref, grad_ref, note_ref, sources_ref, spread_ref, pairs_ref, sigmoid_ref, softplus_ref):
+    embed = embed_ref[...]
+    scores = lax.dot_general(embed, embed, NT, preferred_element_type=F32)
+    sigmoid, softplus = soft_parts(-scores)
+    sigmoid_ref[...] = sigmoid
+    softplus_ref[...] = softplus
     pairs_ref[...] = jnp.zeros((NODE_DEV, NODE_DEV), F32)
     node = lax.broadcasted_iota(jnp.int32, (NODE_DEV, TILE), 0)
+    widest = largest(features_ref[...].astype(F32))
+    for r in range(RELS):
+        widest = jnp.maximum(widest, largest(means_ref[r].astype(F32)))
+    tiles = count_ref[0]
 
     def group(step, _):
         sources, targets = [], []
@@ -177,26 +211,17 @@
         return 0
 
     lax.fori_loop(0, (tiles + (GROUP - 1)) // GROUP, group, 0)
-    embed = embed_ref[...]
     pairs = pairs_ref[...]
     sources = jnp.sum(pairs, axis=1, keepdims=True)
     sources_ref[...] = jnp.broadcast_to(sources, (NODE_DEV, 128))
     high, low = split_two(embed.astype(F32) * sources)
     spread_ref[:, 0:H] = high
     spread_ref[:, H:] = low
-    scores = lax.dot_general(embed, embed, NT, preferred_element_type=F32)
-    sigmoid, softplus = soft_parts(-scores)
-    loss = jnp.sum(jnp.sum(pairs * softplus, axis=0, keepdims=True), axis=1, keepdims=True)
-    widest = largest(features_ref[...].astype(F32))
-    for r in range(RELS):
-        widest = jnp.maximum(widest, largest(means_ref[r].astype(F32)))
-    high, low = split_two(-((pairs + pairs.T) * sigmoid))
+    loss = jnp.sum(jnp.sum(pairs * softplus_ref[...], axis=0, keepdims=True), axis=1, keepdims=True)
+    high, low = split_two(-((pairs + pairs.T) * sigmoid_ref[...]))
     base = dot(high, embed) + dot(low, embed)
     grad_ref[...] = base
     note_ref[...] = notes_of((loss, tiles.astype(F32), widest, NODE_DEV * largest(base)))
-    turned_ref[0:H, :] = features_ref[...].T
-    for r in range(RELS):
-        turned_ref[(r + 1) * H : (r + 2) * H, :] = means_ref[r].T
 
 
 def scored(embed, rows, sources, spread):
@@ -256,17 +281,21 @@
     return pl.ds(pl.multiple_of(core * HALF, HALF), HALF)
 
 
-def known_body(neg_ids_ref, core_ref, grad_ref, turned_ref, own_ref, other_ref, chosen_ref, pre_ref):
+def known_body(neg_ids_ref, core_ref, grad_ref, features_ref, means_ref, own_ref, other_ref, chosen_ref):
     node = lax.broadcasted_iota(jnp.int32, (NODE_DEV, H), 0)
     grad = grad_ref[...]
     for i in range(NEG_DEV):
         grad = jnp.where(node == neg_ids_ref[i], 0.0, grad)
-    pre_ref[...] = grad.astype(BF16)
-    turned = turned_ref[...]
-    chosen = lax.dot_general(chosen_rows(neg_ids_ref), turned, NT, preferred_element_type=F32)
-    chosen_ref[...] = chosen.astype(BF16)
-    other_ref[...] = dot(turned, pre_ref[:, half_at(1 - core_ref[0])])
-    own_ref[...] = dot(turned, pre_ref[:, half_at(core_ref[0])])
+    pre = grad.astype(BF16)
+    picks = chosen_rows(neg_ids_ref)
+    swapped = core_ref[0] == 1
+    for r, rows in enumerate((features_ref[...], means_ref[0], means_ref[1])):
+        at = pl.ds(r * H, H)
+        both = lax.dot_general(rows, pre, TN, preferred_element_type=F32)
+        first, second = both[:, :HALF], both[:, HALF:]
+        own_ref[at, :] = jnp.where(swapped, second, first)
+        other_ref[at, :] = jnp.where(swapped, first, second)
+        chosen_ref[:, at] = dot(picks, rows).astype(BF16)
 
 
 def outer_body(neg_ids_ref, core_ref, arrived_ref, grad_ref, pre_ref, own_ref, other_ref, note_ref, sum_ref, row_ref):
@@ -340,29 +369,23 @@
     tall = ((RELS + 1) * H, HALF)
     core = lax.axis_index(NEAR).astype(jnp.int32).reshape(1)
     core, halo_send = lax.optimization_barrier((core, halo_send))
-    (outgoing,) = call(halo_body, [hbm((N_DOM, HALO_PEER, H), BF16)], [vmem(), whole((NODE_DEV, H))], (), (halo_send[0].T, features))
+    (outgoing,) = call(halo_body, [hbm((N_DOM, HALO_PEER, H), BF16)], [FROM_HBM, FROM_HBM], (), (halo_send[0].T, features))
     incoming = swap(outgoing, DOM)
     neighbours = nbr_index.reshape(NODE_DEV, RELS * FAN)
     halo_count, own_sum, pre = call(
         counts_body,
         [hbm((RELS, NODE_DEV, 512), BF16), hbm((RELS, *square), F32), hbm(square, F32)],
-        [FROM_HBM, weight_at(0), vmem()],
+        [FROM_HBM, weight_at(0), FROM_HBM],
         [pltpu.VMEM((RELS, NODE_DEV, NODE_DEV), BF16)],
         (features, weights, neighbours),
     )
-    means, embed, picked = call(
-        layer_body,
-        [hbm((RELS, *square), BF16), (square, BF16), hbm((CHIPS, NEG_DEV, H), BF16)],
-        [smem(), FROM_HBM, vmem(), FROM_HBM, FROM_HBM, weight_at(1), weight_at(2)],
-        (),
-        (neg_ids, halo_count, incoming.reshape(512, H), own_sum, pre, weights, weights),
-    )
+    means, embed, picked = layer(neg_ids, halo_count, incoming.reshape(512, H), own_sum, pre, weights)
     near_rows = swap(picked, FAR).reshape(square)
-    base, note, turned, sources, spread = call(
+    base, note, sources, spread = call(
         positive_body,
-        [hbm(square, F32), ((8, 128), F32), hbm(((RELS + 1) * H, NODE_DEV), BF16), ((NODE_DEV, 128), F32), ((NODE_DEV, 2 * H), BF16)],
-        [smem(), vmem(), vmem(), FROM_HBM, FROM_HBM],
-        [pltpu.VMEM((NODE_DEV, NODE_DEV), F32)],
+        [hbm(square, F32), ((8, 128), F32), ((NODE_DEV, 128), F32), ((NODE_DEV, 2 * H), BF16)],
+        [smem(), vmem(), FROM_HBM, FROM_HBM, FROM_HBM],
+        [pltpu.VMEM(square, F32)] * 3,
         (tile_count, embed, edge_ends, features, means),
     )
     near_rows, note = lax.optimization_barrier((near_rows, note))
@@ -393,7 +416,7 @@
     part_arrived, grad = lax.optimization_barrier((part_arrived, grad))
     (outgoing_grad,) = call(
         merge_body,
-        [hbm((CHIPS, NEG_DEV, H + 128), BF16)],
+        [((CHIPS, NEG_DEV, H + 128), BF16)],
         [vmem()] * 4,
         (),
         (near_part, part_arrived, note, other_note),
@@ -403,9 +426,9 @@
     known_own, known_other, chosen = call(
         known_body,
         [(tall, F32), (tall, F32), ((16, (RELS + 1) * H), BF16)],
-        [smem(), smem(), vmem(), FROM_HBM],
-        [pltpu.VMEM(square, BF16)],
-        (neg_ids, core, grad, turned),
+        [smem(), smem(), vmem(), FROM_HBM, FROM_HBM],
+        (),
+        (neg_ids, core, grad, features, means),
     )
     other_chosen = core_swap(chosen)
     known = known_own + core_swap(known_other)

time: 135 us -> 135 us (level)
    pallas_call x0 -> x1, Pallas kernels: none -> 5.01 us  [layer(): pl.pallas_call(layer_body, out_shape=[hbm((RELS, NODE_DEV, H), BF16), plt...]
    pallas_call x11 -> x10, Pallas kernels: 32.4 us -> 28.1 us  [call(): pl.pallas_call(body, out_shape=[pltpu.VMEM(*o) if isinstance(o, tuple) el...]
    unnamed x14 -> x8, local copies, waits for them, and re-layouts: 2.99 us -> 1.16 us
where the time goes in v1:
time: 135 us; the launch traced here: 134 us
  blocking collectives  37.9 us (28%)
  Pallas kernels  36.2 us (27%)
  starting transfers between devices  29.9 us (22%)
  waiting for transfers between devices  23.8 us (18%)
  other arithmetic  2.67 us (2%)
  local copies, waits for them, and re-layouts  2.19 us (2%)
  between operations  1.42 us (1%)
    all_to_all x2, blocking collectives, swap(): return lax.all_to_all(x, axes, split_axis=0, concat_axis=0, tiled=True)  37.9 us
    pallas_call x10, Pallas kernels, call(): pl.pallas_call(body, out_shape=[pltpu.VMEM(*o) if isinstance(o, tuple) el...  28.1 us
    all_to_all x3, waiting for transfers between devices, swap(): return lax.all_to_all(x, axes, split_axis=0, concat_axis=0, tiled=True)  22.8 us
    all_to_all x3, starting transfers between devices, swap(): return lax.all_to_all(x, axes, split_axis=0, concat_axis=0, tiled=True)  22.4 us
    ppermute x7, starting transfers between devices, core_swap(): return lax.ppermute(x, 'dom_3', [(0, 1), (1, 0)])  7.51 us
    pallas_call x1, Pallas kernels, layer(): pl.pallas_call(layer_body, out_shape=[hbm((RELS, NODE_DEV, H), BF16), plt...  5.01 us
  transfers between devices with their start and end apart: 10, of which 5 were waited for; matrix products, arithmetic and copies ran while one was open for 2% of the time, Pallas kernels for 14%

profile of v1, /device:TPU:1, one launch (start us, length us, event | category | flops | bytes accessed | tf_op | source)
XLA Modules:
  0.0 134.1 jit_solution(6069638487850094472)
XLA Ops:
  0.7 2.6 %shard_map.95 = bf16[128,4,512]{2,1,0:T(4,128)(2,1)} custom-call(s32[4,128]{1,0:T(4,128)} %bitcast.16, bf16[512,512]{1,0:T(8,128)(2,1)} %features_ref.7), custom_call_target="tpu_custom_call" | custom-call | tf_op jit(solution)/shard_map/pallas_call | solution.py:83
  3.3 11.5 %all-to-all-start = ((bf16[128,4,512]{2,1,0:T(4,128)(2,1)}), bf16[128,4,512]{2,1,0:T(4,128)(2,1)S(1)}, u32[]{:S(2)}, u32[]{:S(2)}) async-start(bf16[128,4,512]{2,1,0:T(4,128)(2,1)} %shard_map.95), calls=%async_computation | async-start | bytes 1048576 | tf_op jit(solution)/shard_map/all_to_all | solution.py:35
  14.8 0.8 copy.12.nbr_ref
  15.6 8.5 %shard_map.94 = (bf16[2,512,512]{2,1,0:T(8,128)(2,1)}, f32[2,512,512]{2,1,0:T(8,128)}, f32[512,512]{1,0:T(8,128)}) custom-call(bf16[512,512]{1,0:T(8,128)(2,1)} %features_ref.7, bf16[3,512,512]{2,1,0:T(8,128)(2,1)S(1)} %copy-done, s32[512,16]{1,0:T(8,128)} %copy.12.nbr_ref), custom_call_target="tpu_custom_call" | custom-call | tf_op jit(solution)/shard_map/pallas_call | solution.py:83
  24.1 4.3 %all-to-all-done = bf16[128,4,512]{2,1,0:T(4,128)(2,1)S(1)} async-done(((bf16[128,4,512]{2,1,0:T(4,128)(2,1)}), bf16[128,4,512]{2,1,0:T(4,128)(2,1)S(1)}, u32[]{:S(2)}, u32[]{:S(2)}) %all-to-all-start) | async-done | bytes 524320 | tf_op jit(solution)/shard_map/all_to_all | solution.py:35
  28.5 5.0 %shard_map.96 = (bf16[2,512,512]{2,1,0:T(8,128)(2,1)}, bf16[512,512]{1,0:T(8,128)(2,1)S(1)}, bf16[64,8,512]{2,1,0:T(8,128)(2,1)}) custom-call(s32[8]{0:T(128)S(1)} %copy-done.2, bf16[2,512,512]{2,1,0:T(8,128)(2,1)} %get-tuple-element.42.halo_count_ref, bf16[512,512]{1,0:T(8,128)(2,1)S(1)} %reshape.29.halo_ref, f32[2,512,512]{2,1,0:T(8,128)} %get-tuple-element.44.own_sum_ref, ...), custom_call_target="tpu_custom_call" | custom-call | tf_op jit(solution)/shard_map/pallas_call | solution.py:150
  33.5 6.2 %all-to-all-start.1 = ((bf16[64,8,512]{2,1,0:T(8,128)(2,1)}), bf16[64,8,512]{2,1,0:T(8,128)(2,1)S(1)}, u32[]{:S(2)}, u32[]{:S(2)}) async-start(bf16[64,8,512]{2,1,0:T(8,128)(2,1)} %get-tuple-element.47), calls=%async_computation.1 | async-start | bytes 1048576 | tf_op jit(solution)/shard_map/all_to_all | solution.py:35
  40.4 5.1 %shard_map.97 = (f32[512,512]{1,0:T(8,128)}, f32[8,128]{1,0:T(8,128)S(1)}, f32[512,128]{1,0:T(8,128)S(1)}, bf16[512,1024]{1,0:T(8,128)(2,1)S(1)}) custom-call(s32[1]{0:T(128)S(6)} %copy.14.count_ref, bf16[512,512]{1,0:T(8,128)(2,1)S(1)} %get-tuple-element.46.embed_ref, s32[16,2,256]{2,1,0:T(2,128)} %ends_ref.1, bf16[512,512]{1,0:T(8,128)(2,1)} %features_ref.7, ...), custom_call_target="tpu_custom_call" | custom-call | tf_op jit(solution)/shard_map/pallas_call | solution.py:83
  45.5 6.7 %all-to-all-done.1 = bf16[64,8,512]{2,1,0:T(8,128)(2,1)S(1)} async-done(((bf16[64,8,512]{2,1,0:T(8,128)(2,1)}), bf16[64,8,512]{2,1,0:T(8,128)(2,1)S(1)}, u32[]{:S(2)}, u32[]{:S(2)}) %all-to-all-start.1) | async-done | bytes 524320 | tf_op jit(solution)/shard_map/all_to_all | solution.py:35
  52.2 2.0 %collective-permute-start = (bf16[512,512]{1,0:T(8,128)(2,1)S(1)}, bf16[512,512]{1,0:T(8,128)(2,1)S(1)}, u32[]{:S(2)}, u32[]{:S(2)}) collective-permute-start(bf16[512,512]{1,0:T(8,128)(2,1)S(1)} %bitcast.10), channel_id=1, source_target_pairs={{0,1},{1,0},{2,3},{3,2},{4,5},{5,4},{6,7},{7,6},{8,9},{9,8},{10,11... | collective-permute-start | bytes 1572872 | tf_op jit(solution)/shard_map/ppermute | solution.py:39
  54.2 1.8 %shard_map.98 = (bf16[512,512]{1,0:T(8,128)(2,1)S(1)}, f32[512,512]{1,0:T(8,128)S(1)}, f32[8,128]{1,0:T(8,128)S(1)}) custom-call(bf16[512,512]{1,0:T(8,128)(2,1)S(1)} %get-tuple-element.46.embed_ref, bf16[512,512]{1,0:T(8,128)(2,1)S(1)} %bitcast.11, bf16[512,1024]{1,0:T(8,128)(2,1)S(1)} %get-tuple-element.51.spread_ref, ...), custom_call_target="tpu_custom_call" | custom-call | tf_op jit(solution)/shard_map/pallas_call | solution.py:83
  56.0 1.8 %shard_map.99 = (bf16[512,512]{1,0:T(8,128)(2,1)S(1)}, bf16[512,512]{1,0:T(8,128)(2,1)S(1)}, f32[8,128]{1,0:T(8,128)S(1)}) custom-call(bf16[512,512]{1,0:T(8,128)(2,1)S(1)} %get-tuple-element.46.embed_ref, bf16[512,512]{1,0:T(8,128)(2,1)S(1)} %collective-permute-done.rows_ref, bf16[512,1024]{1,0:T(8,128)(2,1)S(1)} %get-tuple-element.51.spread_ref, ...), custom_call_target="tpu_custom_call" | custom-call | tf_op jit(solution)/shard_map/pallas_call | solution.py:83
  57.9 0.4 collective-permute-start.2
  58.3 1.9 %shard_map.100.grad_ref = f32[512,512]{1,0:T(8,128)S(1)} custom-call(bf16[512,512]{1,0:T(8,128)(2,1)S(1)} %get-tuple-element.57.near_weight_ref, bf16[512,512]{1,0:T(8,128)(2,1)S(1)} %bitcast.12, bf16[512,512]{1,0:T(8,128)(2,1)S(1)} %get-tuple-element.58.weight_ref, bf16[512,512]{1,0:T(8,128)(2,1)S(1)} %collective-permute-done.rows_ref, ...), custom_call_target="tpu_custom_call" | custom-call | tf_op jit(solution)/shard_map/pallas_call | solution.py:83
  60.3 1.4 %shard_map.101 = bf16[64,8,640]{2,1,0:T(8,128)(2,1)} custom-call(f32[512,512]{1,0:T(8,128)S(1)} %get-tuple-element.54.part_ref, bf16[512,512]{1,0:T(8,128)(2,1)S(1)} %collective-permute-done.1.arrived_ref, f32[8,128]{1,0:T(8,128)S(1)} %get-tuple-element.61.own_note_ref, f32[8,128]{1,0:T(8,128)S(1)} %collective-permute-done.2.other_note_ref), custom_call_target="tpu_custom_call" | custom-call | tf_op jit(solution)/shard_map/pallas_call | solution.py:83
  61.7 2.9 %shard_map.102 = (f32[1536,256]{1,0:T(8,128)S(1)}, f32[1536,256]{1,0:T(8,128)S(1)}, bf16[16,1536]{1,0:T(8,128)(2,1)S(1)}) custom-call(s32[8]{0:T(128)S(1)} %copy-done.2, s32[1]{0:T(128)} %bitcast.core_ref, f32[512,512]{1,0:T(8,128)S(1)} %shard_map.100.grad_ref, bf16[512,512]{1,0:T(8,128)(2,1)} %features_ref.7, bf16[2,512,512]{2,1,0:T(8,128)(2,1)} %get-tuple-element.48.means_ref), custom_call_target="tpu_custom_call" | custom-call | tf_op jit(solution)/shard_map/pallas_call | solution.py:83
  64.6 1.1 copy-done.1
  65.7 0.3 collective-permute-start.3
  66.0 4.6 %all-to-all-start.2 = ((bf16[64,8,640]{2,1,0:T(8,128)(2,1)}), bf16[64,8,640]{2,1,0:T(8,128)(2,1)S(1)}, u32[]{:S(2)}, u32[]{:S(2)}) async-start(bf16[64,8,640]{2,1,0:T(8,128)(2,1)} %shard_map.101), calls=%async_computation.2 | async-start | bytes 1310720 | tf_op jit(solution)/shard_map/all_to_all | solution.py:35
  70.6 0.3 collective-permute-start.4
  71.0 2.1 %add.3.known_ref = f32[1536,256]{1,0:T(8,128)S(1)} add(f32[1536,256]{1,0:T(8,128)} %copy-done.1, f32[1536,256]{1,0:T(8,128)} %collective-permute-done.3) | non-fusion elementwise | flops 393216 | bytes 4718592 | tf_op jit(solution)/shard_map/add | solution.py:434
  73.0 11.8 %all-to-all-done.2.arrived_ref = bf16[64,8,640]{2,1,0:T(8,128)(2,1)S(1)} async-done(((bf16[64,8,640]{2,1,0:T(8,128)(2,1)}), bf16[64,8,640]{2,1,0:T(8,128)(2,1)S(1)}, u32[]{:S(2)}, u32[]{:S(2)}) %all-to-all-start.2) | async-done | bytes 655392 | tf_op jit(solution)/shard_map/all_to_all | solution.py:35
  84.9 1.5 %shard_map.103 = (bf16[512,512]{1,0:T(8,128)(2,1)}, bf16[16,256]{1,0:T(8,128)(2,1)S(1)}, bf16[16,256]{1,0:T(8,128)(2,1)S(1)}, f32[8,128]{1,0:T(8,128)S(1)}) custom-call(s32[8]{0:T(128)S(1)} %copy-done.2, s32[1]{0:T(128)} %bitcast.core_ref, bf16[64,8,640]{2,1,0:T(8,128)(2,1)S(1)} %all-to-all-done.2.arrived_ref, f32[512,512]{1,0:T(8,128)S(1)} %shard_map.100.grad_ref), custom_call_target="tpu_custom_call" | custom-call | tf_op jit(solution)/shard_map/pallas_call | solution.py:83
  86.4 1.5 %collective-permute-start.5 = (bf16[16,256]{1,0:T(8,128)(2,1)S(1)}, bf16[16,256]{1,0:T(8,128)(2,1)S(1)}, u32[]{:S(2)}, u32[]{:S(2)}) collective-permute-start(bf16[16,256]{1,0:T(8,128)(2,1)S(1)} %get-tuple-element.72), channel_id=1, source_target_pairs={{0,1},{1,0},{2,3},{3,2},{4,5},{5,4},{6,7},{7,6},{8,9},{9,8},{10,11... | collective-permute-start | bytes 24584 | tf_op jit(solution)/shard_map/ppermute | solution.py:39
  87.9 0.8 collective-permute-done.5.other_row_ref
  88.8 0.6 shard_map.104
  89.5 19.4 %all_to_all.25 = f16[64,24,256]{2,1,0:T(8,128)(2,1)S(1)} all-to-all(f16[64,24,256]{2,1,0:T(8,128)(2,1)S(1)} %bitcast.14), channel_id=1, replica_groups=mesh['dom_0'=4,'dom_1'=4,'dom_2'=4,'dom_3'=2] {'dom_0','dom_1','dom_2'}, dimensions={0} | all-to-all | bytes 1572864 | tf_op jit(solution)/shard_map/all_to_all | solution.py:35
  109.1 18.5 %all_to_all.26 = f16[64,24,256]{2,1,0:T(8,128)(2,1)S(1)} all-to-all(f16[64,24,256]{2,1,0:T(8,128)(2,1)S(1)} %broadcast_in_dim.3), channel_id=1, replica_groups=mesh['dom_0'=4,'dom_1'=4,'dom_2'=4,'dom_3'=2] {'dom_0','dom_1','dom_2'}, dimensions={0} | all-to-all | bytes 1572864 | tf_op jit(solution)/shard_map/all_to_all | solution.py:35
  127.6 2.9 %collective-permute-start.6 = (f16[1536,256]{1,0:T(8,128)(2,1)S(1)}, f16[1536,256]{1,0:T(8,128)(2,1)S(1)}, u32[]{:S(2)}, u32[]{:S(2)}) collective-permute-start(f16[1536,256]{1,0:T(8,128)(2,1)S(1)} %bitcast.13), channel_id=1, source_target_pairs={{0,1},{1,0},{2,3},{3,2},{4,5},{5,4},{6,7},{7,6},{8,9},{9,8},{10,11... | collective-permute-start | bytes 2359304 | tf_op jit(solution)/shard_map/ppermute | solution.py:39
  130.7 1.5 %shard_map.105 = (f32[3,512,512]{2,1,0:T(8,128)}, f32[1,1]{1,0:T(1,128)}) custom-call(s32[1]{0:T(128)} %bitcast.core_ref, f32[1536,256]{1,0:T(8,128)S(1)} %bitcast_convert_fusion.half_ref, f32[8,128]{1,0:T(8,128)S(1)} %get-tuple-element.73.note_ref), custom_call_target="tpu_custom_call" | custom-call | tf_op jit(solution)/shard_map/pallas_call | solution.py:456
  132.2 0.2 collective-permute-done.6
  132.6 1.5 %shard_map.106 = f32[3,512,512]{2,1,0:T(8,128)} custom-call(s32[1]{0:T(128)} %bitcast.core_ref, f32[1536,256]{1,0:T(8,128)S(1)} %convert_element_type.19.half_ref, f32[8,128]{1,0:T(8,128)S(1)} %get-tuple-element.73.note_ref, f32[3,512,512]{2,1,0:T(8,128)} %get-tuple-element.76.begun_ref), custom_call_target="tpu_custom_call", output_to_operand_aliasing={{}: (3, {})} | custom-call | tf_op jit(solution)/shard_map/pallas_call | solution.py:458
  (20 shorter events, 0.9 us)
Async XLA Ops:
  0.6 14.1 %copy-start.3 = (s32[512,2,8]{0,2,1:T(8,128)S(1)}, s32[512,2,8]{0,2,1:T(8,128)}, u32[]{:S(2)}) copy-start(s32[512,2,8]{0,2,1:T(8,128)} %param.10) | copy-start | bytes 98308
  0.6 15.0 %copy-start = (bf16[3,512,512]{2,1,0:T(8,128)(2,1)S(1)}, bf16[3,512,512]{2,1,0:T(8,128)(2,1)}, u32[]{:S(2)}) copy-start(bf16[3,512,512]{2,1,0:T(8,128)(2,1)} %w_ref.3) | copy-start | bytes 4718596
  3.3 25.1 %all-to-all-start = ((bf16[128,4,512]{2,1,0:T(4,128)(2,1)}), bf16[128,4,512]{2,1,0:T(4,128)(2,1)S(1)}, u32[]{:S(2)}, u32[]{:S(2)}) async-start(bf16[128,4,512]{2,1,0:T(4,128)(2,1)} %shard_map.95), calls=%async_computation | async-start | bytes 1048576 | tf_op jit(solution)/shard_map/all_to_all | solution.py:35
  15.6 12.9 %copy-start.2 = (s32[8]{0:T(128)S(1)}, s32[8]{0:T(128)}, u32[]{:S(2)}) copy-start(s32[8]{0:T(128)} %neg_ids_ref.5) | copy-start | bytes 100
  33.5 18.7 %all-to-all-start.1 = ((bf16[64,8,512]{2,1,0:T(8,128)(2,1)}), bf16[64,8,512]{2,1,0:T(8,128)(2,1)S(1)}, u32[]{:S(2)}, u32[]{:S(2)}) async-start(bf16[64,8,512]{2,1,0:T(8,128)(2,1)} %get-tuple-element.47), calls=%async_computation.1 | async-start | bytes 1048576 | tf_op jit(solution)/shard_map/all_to_all | solution.py:35
  52.2 3.8 %collective-permute-start = (bf16[512,512]{1,0:T(8,128)(2,1)S(1)}, bf16[512,512]{1,0:T(8,128)(2,1)S(1)}, u32[]{:S(2)}, u32[]{:S(2)}) collective-permute-start(bf16[512,512]{1,0:T(8,128)(2,1)S(1)} %bitcast.10), channel_id=1, source_target_pairs={{0,1},{1,0},{2,3},{3,2},{4,5},{5,4},{6,7},{7,6},{8,9},{9,8},{10,11... | collective-permute-start | bytes 1572872 | tf_op jit(solution)/shard_map/ppermute | solution.py:39
  57.8 2.5 %collective-permute-start.1 = (bf16[512,512]{1,0:T(8,128)(2,1)S(1)}, bf16[512,512]{1,0:T(8,128)(2,1)S(1)}, u32[]{:S(2)}, u32[]{:S(2)}) collective-permute-start(bf16[512,512]{1,0:T(8,128)(2,1)S(1)} %get-tuple-element.56), channel_id=1, source_target_pairs={{0,1},{1,0},{2,3},{3,2},{4,5},{5,4},{6,7},{7,6},{8,9},{9,8},{10,11... | collective-permute-start | bytes 1572872 | tf_op jit(solution)/shard_map/ppermute | solution.py:39
  57.9 2.4 %collective-permute-start.2 = (f32[8,128]{1,0:T(8,128)S(1)}, f32[8,128]{1,0:T(8,128)S(1)}, u32[]{:S(2)}, u32[]{:S(2)}) collective-permute-start(f32[8,128]{1,0:T(8,128)S(1)} %get-tuple-element.61.own_note_ref), channel_id=1, source_target_pairs={{0,1},{1,0},{2,3},{3,2},{4,5},{5,4},{6,7},{7,6},{8,9},{9,8},{10,11... | collective-permute-start | bytes 12296 | tf_op jit(solution)/shard_map/ppermute | solution.py:39
  64.6 1.1 copy-start.1
  65.7 5.2 %collective-permute-start.3 = (f32[1536,256]{1,0:T(8,128)S(1)}, f32[1536,256]{1,0:T(8,128)}, u32[]{:S(2)}, u32[]{:S(2)}) collective-permute-start(f32[1536,256]{1,0:T(8,128)S(1)} %get-tuple-element.66), channel_id=1, source_target_pairs={{0,1},{1,0},{2,3},{3,2},{4,5},{5,4},{6,7},{7,6},{8,9},{9,8},{10,11... | collective-permute-start | bytes 4718600 | tf_op jit(solution)/shard_map/ppermute | solution.py:39
  66.0 18.9 %all-to-all-start.2 = ((bf16[64,8,640]{2,1,0:T(8,128)(2,1)}), bf16[64,8,640]{2,1,0:T(8,128)(2,1)S(1)}, u32[]{:S(2)}, u32[]{:S(2)}) async-start(bf16[64,8,640]{2,1,0:T(8,128)(2,1)} %shard_map.101), calls=%async_computation.2 | async-start | bytes 1310720 | tf_op jit(solution)/shard_map/all_to_all | solution.py:35
  70.6 2.4 %collective-permute-start.4 = (bf16[16,1536]{1,0:T(8,128)(2,1)S(1)}, bf16[16,1536]{1,0:T(8,128)(2,1)S(1)}, u32[]{:S(2)}, u32[]{:S(2)}) collective-permute-start(bf16[16,1536]{1,0:T(8,128)(2,1)S(1)} %get-tuple-element.67.own_chosen_ref), channel_id=1, source_target_pairs={{0,1},{1,0},{2,3},{3,2},{4,5},{5,4},{6,7},{7,6},{8,9},{9,8},{10,11... | collective-permute-start | bytes 147464 | tf_op jit(solution)/shard_map/ppermute | solution.py:39
  86.4 2.4 %collective-permute-start.5 = (bf16[16,256]{1,0:T(8,128)(2,1)S(1)}, bf16[16,256]{1,0:T(8,128)(2,1)S(1)}, u32[]{:S(2)}, u32[]{:S(2)}) collective-permute-start(bf16[16,256]{1,0:T(8,128)(2,1)S(1)} %get-tuple-element.72), channel_id=1, source_target_pairs={{0,1},{1,0},{2,3},{3,2},{4,5},{5,4},{6,7},{7,6},{8,9},{9,8},{10,11... | collective-permute-start | bytes 24584 | tf_op jit(solution)/shard_map/ppermute | solution.py:39
  127.6 4.8 %collective-permute-start.6 = (f16[1536,256]{1,0:T(8,128)(2,1)S(1)}, f16[1536,256]{1,0:T(8,128)(2,1)S(1)}, u32[]{:S(2)}, u32[]{:S(2)}) collective-permute-start(f16[1536,256]{1,0:T(8,128)(2,1)S(1)} %bitcast.13), channel_id=1, source_target_pairs={{0,1},{1,0},{2,3},{3,2},{4,5},{5,4},{6,7},{7,6},{8,9},{9,8},{10,11... | collective-permute-start | bytes 2359304 | tf_op jit(solution)/shard_map/ppermute | solution.py:39

commit v2 on v1

--- a/solution.py
+++ b/solution.py
@@ -125,44 +125,18 @@
     pre_ref[...] = dot(own, w_ref[0])
 
 
-def layer_body(neg_ids_ref, halo_count_ref, halo_ref, own_sum_ref, pre_ref, w_ref, mean_ref, embed_ref, picked_ref, total_ref):
-    r = pl.program_id(0)
-    total = own_sum_ref[0] + dot(halo_count_ref[0], halo_ref[...])
-    mean = (total * (1.0 / FAN)).astype(BF16)
-    mean_ref[0] = mean
-    part = dot(mean, w_ref[0])
-
-    @pl.when(r == 0)
-    def _():
-        total_ref[...] = pre_ref[...] + part
-
-    @pl.when(r == RELS - 1)
-    def _():
-        embed = (total_ref[...] + part).astype(BF16)
-        embed_ref[...] = embed
-        picked = dot(chosen_rows(neg_ids_ref), embed)[:NEG_DEV]
-        picked_ref[...] = jnp.broadcast_to(picked[None], (CHIPS, NEG_DEV, H)).astype(BF16)
-
-
-def layer(neg_ids, halo_count, halo, own_sum, pre, weights):
-    per_relation = pl.BlockSpec((1, NODE_DEV, H), lambda r: (r, 0, 0))
-    from_hbm = lambda x: pltpu.with_memory_space_constraint(x, pltpu.HBM)
-    return pl.pallas_call(
-        layer_body,
-        out_shape=[hbm((RELS, NODE_DEV, H), BF16), pltpu.VMEM((NODE_DEV, H), BF16), hbm((CHIPS, NEG_DEV, H), BF16)],
-        grid=(RELS,),
-        in_specs=[
-            smem(),
-            per_relation,
-            vmem(),
-            per_relation,
-            pl.BlockSpec((NODE_DEV, H), lambda r: (0, 0)),
-            pl.BlockSpec((1, H, H), lambda r: (r + 1, 0, 0)),
-        ],
-        out_specs=[per_relation, vmem(), pl.BlockSpec((CHIPS, NEG_DEV, H), lambda r: (0, 0, 0))],
-        scratch_shapes=[pltpu.VMEM((NODE_DEV, H), F32)],
-        compiler_params=pltpu.CompilerParams(vmem_limit_bytes=28 << 20),
-    )(neg_ids, from_hbm(halo_count), near_memory(halo), from_hbm(own_sum), from_hbm(pre), from_hbm(weights))
+def layer_body(neg_ids_ref, halo_count_ref, halo_ref, own_sum_ref, pre_ref, first_ref, second_ref, means_ref, embed_ref, picked_ref):
+    halo = halo_ref[...]
+    preact = pre_ref[...]
+    for r, w_ref in enumerate((first_ref, second_ref)):
+        total = own_sum_ref[r] + dot(halo_count_ref[r], halo)
+        mean = (total * (1.0 / FAN)).astype(BF16)
+        means_ref[r] = mean
+        preact = preact + dot(mean, w_ref[0])
+    embed = preact.astype(BF16)
+    embed_ref[...] = embed
+    picked = dot(chosen_rows(neg_ids_ref), embed)[:NEG_DEV]
+    picked_ref[...] = jnp.broadcast_to(picked[None], (CHIPS, NEG_DEV, H)).astype(BF16)
 
 
 def soft_parts(x):
@@ -221,7 +195,9 @@
     high, low = split_two(-((pairs + pairs.T) * sigmoid_ref[...]))
     base = dot(high, embed) + dot(low, embed)
     grad_ref[...] = base
-    note_ref[...] = notes_of((loss, tiles.astype(F32), widest, NODE_DEV * largest(base)))
+    count = tiles.astype(F32)
+    known = widest * NODE_DEV * largest(base)
+    note_ref[...] = notes_of((loss, count, 0.0, known, widest * TILE * count, NEG_DEV * widest, 0.0))
 
 
 def scored(embed, rows, sources, spread):
@@ -241,10 +217,10 @@
     part_ref[...] = part.astype(part_ref.dtype)
     note = note_in_ref[...]
     lane = lax.broadcasted_iota(jnp.int32, note.shape, 1)
-    note = note + jnp.where(lane == 0, loss, 0.0)
-    tallest = jnp.maximum(note, jnp.where(lane == 4, largest(rows.astype(F32)), 0.0))
-    note = jnp.where(lane == 4, tallest, note)
-    note_ref[...] = jnp.where(lane == 5, jnp.maximum(note, largest(part)), note)
+    tallest = largest(rows.astype(F32))
+    note = jnp.where(lane == 0, note + loss, note)
+    note = jnp.where(lane == 2, jnp.maximum(note, note[:, 3:4] + note[:, 4:5] * tallest), note)
+    note_ref[...] = jnp.where(lane == 6, jnp.maximum(note, largest(part)), note)
 
 
 def rest_body(near_weight_ref, near_rows_ref, weight_ref, rows_ref, sources_ref, base_ref, grad_ref):
@@ -252,20 +228,16 @@
     grad_ref[...] = base_ref[...] + sources_ref[:, 0:1] * total
 
 
-def shared_note(note_ref):
-    loss, tiles, widest, base, tallest, part = (note_ref[0:1, i : i + 1] for i in range(6))
-    return loss, tiles, widest * (base + TILE * tiles * tallest), NEG_DEV * widest, part
-
-
 def merge_body(part_ref, arrived_ref, own_note_ref, other_note_ref, send_ref):
+    note = own_note_ref[...] + other_note_ref[...]
+    first = note.astype(BF16).astype(F32)
+    second = (note - first).astype(BF16).astype(F32)
+    third = (note - first) - second
+    lane = lax.broadcasted_iota(jnp.int32, note.shape, 1)
+    note = jnp.where(lane == 3, pltpu.roll(second, 3, 1), jnp.where(lane == 4, pltpu.roll(third, 4, 1), first))
+    send_ref[:, :, H:] = jnp.broadcast_to(note[None], (CHIPS, NEG_DEV, 128)).astype(BF16)
     total = part_ref[...] + arrived_ref[...].astype(F32)
     send_ref[:, :, 0:H] = total.reshape(CHIPS, NEG_DEV, H).astype(BF16)
-    both = zip(shared_note(own_note_ref), shared_note(other_note_ref))
-    loss, tiles, known, wide, part = (own + other for own, other in both)
-    first = loss.astype(BF16).astype(F32)
-    second = (loss - first).astype(BF16).astype(F32)
-    note = notes_of((first, second, (loss - first) - second, tiles, known, wide, part))
-    send_ref[:, :, H:] = jnp.broadcast_to(note[None], (CHIPS, NEG_DEV, 128)).astype(BF16)
 
 
 def chosen_rows(neg_ids_ref):
@@ -298,65 +270,64 @@
         chosen_ref[:, at] = dot(picks, rows).astype(BF16)
 
 
-def outer_body(neg_ids_ref, core_ref, arrived_ref, grad_ref, pre_ref, own_ref, other_ref, note_ref, sum_ref, row_ref):
+def outer_body(neg_ids_ref, core_ref, arrived_ref, grad_ref, total_ref, own_ref, other_ref, note_ref, row_ref):
     total = jnp.sum(arrived_ref[...].astype(F32), axis=0)
     note_ref[...] = total[:, H:]
+    total_ref[...] = total[:, :H]
+    row_ref[...] = jnp.zeros((16, H), F32)
+    firsts = []
+    for i in range(NEG_DEV):
+        first = i
+        for j in reversed(range(i)):
+            first = jnp.where(neg_ids_ref[j] == neg_ids_ref[i], j, first)
+        firsts.append(first)
+        row = grad_ref[pl.ds(neg_ids_ref[i], 1), :]
+        row_ref[i : i + 1, :] = row if i == 0 else jnp.where(first == i, row, 0.0)
+    for i, first in enumerate(firsts):
+        row_ref[pl.ds(first, 1), :] += total_ref[i : i + 1, :]
+    own_ref[...] = row_ref[:, half_at(core_ref[0])].astype(BF16)
+    other_ref[...] = row_ref[:, half_at(1 - core_ref[0])].astype(BF16)
+
+
+def pre_body(neg_ids_ref, total_ref, grad_ref, pre_ref, sum_ref):
     sum_ref[...] = grad_ref[...]
     for i in range(NEG_DEV):
-        at = pl.ds(neg_ids_ref[i], 1)
-        sum_ref[at, :] += total[i : i + 1, 0:H]
-    row_ref[...] = jnp.zeros((16, H), F32)
-    for i in range(NEG_DEV):
-        fresh = jnp.bool_(True)
-        for j in range(i):
-            fresh = fresh & (neg_ids_ref[j] != neg_ids_ref[i])
-        row = sum_ref[pl.ds(neg_ids_ref[i], 1), :]
-        row_ref[i : i + 1, :] = jnp.where(fresh, row, 0.0)
+        sum_ref[pl.ds(neg_ids_ref[i], 1), :] += total_ref[i : i + 1, :]
     pre_ref[...] = sum_ref[...].astype(BF16)
-    own_ref[...] = row_ref[:, half_at(core_ref[0])].astype(BF16)
-    other_ref[...] = row_ref[:, half_at(1 - core_ref[0])].astype(BF16)
-
-
-def update_body(known_ref, own_chosen_ref, other_chosen_ref, own_row_ref, other_row_ref, note_ref, out_ref):
+
+
+def update_body(known_ref, own_chosen_ref, other_chosen_ref, own_row_ref, other_row_ref, note_ref, out_ref, factor_ref):
     chosen = jnp.concatenate([own_chosen_ref[...], other_chosen_ref[...]], axis=0)
     rows = jnp.concatenate([own_row_ref[...], other_row_ref[...]], axis=0)
     extra = lax.dot_general(chosen, rows, TN, preferred_element_type=F32)
-    out_ref[...] = (known_ref[...] + extra) * scale_of(note_ref)
-
-
-def scale_of(note_ref):
-    known, wide, part = (note_ref[0:1, i : i + 1] for i in (4, 5, 6))
-    return SPAN / (known + wide * part + TINY)
-
-
-def factor_of(note_ref):
-    return 1.0 / scale_of(note_ref) / (note_ref[0:1, 3:4] * TILE)
-
-
-def first_half_body(core_ref, half_ref, note_ref, weight_ref, loss_ref):
+    known, wide, part = (note_ref[0:1, i : i + 1] for i in (2, 5, 6))
+    bound = known + wide * part + TINY
+    out_ref[...] = (known_ref[...] + extra) * (SPAN / bound)
+    factor_ref[...] = jnp.broadcast_to(bound / SPAN / (note_ref[0:1, 1:2] * TILE), (8, HALF))
+
+
+def first_half_body(core_ref, half_ref, factor_ref, note_ref, weight_ref, loss_ref):
     note = note_ref[0:1, :]
-    loss = note[:, 0:1] + note[:, 1:2] + note[:, 2:3]
-    loss_ref[...] = loss / (note[:, 3:4] * TILE)
-    weight_ref[...] = (half_ref[...] * factor_of(note_ref)).reshape(RELS + 1, H, HALF)
-
-
-def second_half_body(core_ref, half_ref, note_ref, begun_ref, weight_ref):
-    weight_ref[...] = (half_ref[...] * factor_of(note_ref)).reshape(RELS + 1, H, HALF)
+    loss_ref[...] = (note[:, 0:1] + note[:, 3:4] + note[:, 4:5]) / (note[:, 1:2] * TILE)
+    weight_ref[0] = half_ref[...] * factor_ref[0:1, :]
+
+
+def second_half_body(core_ref, half_ref, factor_ref, note_ref, begun_ref, weight_ref):
+    weight_ref[0] = half_ref[...] * factor_ref[0:1, :]
 
 
 def halves(body, which, extra, alias):
-    whole = jax.ShapeDtypeStruct((RELS + 1, H, H), F32)
-    block = pl.BlockSpec((RELS + 1, H, HALF), lambda i, core: (0, 0, which(core[0])))
-    scalar = pl.BlockSpec((1, 1), lambda i, core: (0, 0))
-    full = vmem()
-    note = vmem()
+    whole_weight = jax.ShapeDtypeStruct((RELS + 1, H, H), F32)
+    block = pl.BlockSpec((1, H, HALF), lambda r, core: (r, 0, which(core[0])))
+    scalar = pl.BlockSpec((1, 1), lambda r, core: (0, 0))
+    full = pl.BlockSpec((H, HALF), lambda r, core: (r, 0))
     return pl.pallas_call(
         body,
-        out_shape=[whole, jax.ShapeDtypeStruct((1, 1), F32)][: 1 + extra],
+        out_shape=[whole_weight, jax.ShapeDtypeStruct((1, 1), F32)][: 1 + extra],
         grid_spec=pltpu.PrefetchScalarGridSpec(
             num_scalar_prefetch=1,
-            grid=(1,),
-            in_specs=[full, note] + [pl.BlockSpec(memory_space=pl.ANY)] * len(alias),
+            grid=(RELS + 1,),
+            in_specs=[full, vmem(), vmem()] + [pl.BlockSpec(memory_space=pl.ANY)] * len(alias),
             out_specs=[block, scalar][: 1 + extra],
         ),
         input_output_aliases=alias,
@@ -372,14 +343,21 @@
     (outgoing,) = call(halo_body, [hbm((N_DOM, HALO_PEER, H), BF16)], [FROM_HBM, FROM_HBM], (), (halo_send[0].T, features))
     incoming = swap(outgoing, DOM)
     neighbours = nbr_index.reshape(NODE_DEV, RELS * FAN)
+    weights = pltpu.with_memory_space_constraint(weights, pltpu.HBM)
     halo_count, own_sum, pre = call(
         counts_body,
-        [hbm((RELS, NODE_DEV, 512), BF16), hbm((RELS, *square), F32), hbm(square, F32)],
-        [FROM_HBM, weight_at(0), FROM_HBM],
+        [hbm((RELS, NODE_DEV, 512), BF16), ((RELS, *square), F32), hbm(square, F32)],
+        [FROM_HBM, weight_at(0), vmem()],
         [pltpu.VMEM((RELS, NODE_DEV, NODE_DEV), BF16)],
         (features, weights, neighbours),
     )
-    means, embed, picked = layer(neg_ids, halo_count, incoming.reshape(512, H), own_sum, pre, weights)
+    means, embed, picked = call(
+        layer_body,
+        [hbm((RELS, *square), BF16), (square, BF16), hbm((CHIPS, NEG_DEV, H), BF16)],
+        [smem(), FROM_HBM, vmem(), vmem(), FROM_HBM, weight_at(1), weight_at(2)],
+        (),
+        (neg_ids, halo_count, incoming.reshape(512, H), own_sum, pre, weights, weights),
+    )
     near_rows = swap(picked, FAR).reshape(square)
     base, note, sources, spread = call(
         positive_body,
@@ -433,29 +411,37 @@
     other_chosen = core_swap(chosen)
     known = known_own + core_swap(known_other)
     arrived, known, other_chosen = lax.optimization_barrier((arrived, known, other_chosen))
-    pre_grad, own_row, send_row, note = call(
+    total, own_row, send_row, note = call(
         outer_body,
-        [hbm(square, BF16), ((16, HALF), BF16), ((16, HALF), BF16), ((NEG_DEV, 128), F32)],
+        [((NEG_DEV, H), F32), ((16, HALF), BF16), ((16, HALF), BF16), ((NEG_DEV, 128), F32)],
         [smem(), smem(), vmem(), vmem()],
-        [pltpu.VMEM(square, F32), pltpu.VMEM((16, H), F32)],
+        [pltpu.VMEM((16, H), F32)],
         (neg_ids, core, arrived, grad),
     )
-    (partial,) = call(
+    other_row = core_swap(send_row)
+    (pre_grad,) = call(
+        pre_body,
+        [hbm(square, BF16)],
+        [smem(), vmem(), vmem()],
+        [pltpu.VMEM(square, F32)],
+        (neg_ids, total, grad),
+    )
+    partial, factor = call(
         update_body,
-        [(tall, F32)],
+        [(tall, F32), ((8, HALF), F32)],
         [vmem()] * 6,
         (),
-        (known, chosen, other_chosen, own_row, core_swap(send_row), note),
+        (known, chosen, other_chosen, own_row, other_row, note),
     )
     chunks = (CHIPS, 24, HALF)
     mine = jnp.sum(swap(partial.astype(F16).reshape(chunks), FAR).astype(F32), axis=0).astype(F16)
     half = swap(jnp.broadcast_to(mine, chunks), FAR).reshape(tall)
     other_half = core_swap(half).astype(F32)
     half = half.astype(F32)
-    note = near_memory(note)
-    begun, mean_loss = halves(first_half_body, lambda c: c, 1, {})(core, near_memory(half), note)
+    close = near_memory(factor), near_memory(note)
+    begun, mean_loss = halves(first_half_body, lambda c: c, 1, {})(core, near_memory(half), *close)
     (begun, other_half) = lax.optimization_barrier((begun, other_half))
-    (weight_grad,) = halves(second_half_body, lambda c: 1 - c, 0, {3: 0})(core, near_memory(other_half), note, begun)
+    (weight_grad,) = halves(second_half_body, lambda c: 1 - c, 0, {4: 0})(core, near_memory(other_half), *close, begun)
     return weight_grad, mean_loss.reshape(()), pre_grad
 
 

time: 135 us -> 135 us (level)
    pallas_call x3 -> x2, Pallas kernels: 8.01 us -> 3.38 us  [the longest x1 1.69 us: on_device(): halves(first_half_body, lambda c: c, 1, {})(core, near_memory(half), *close)]
    pallas_call x10 -> x12, Pallas kernels: 28.1 us -> 32.3 us  [call(): pl.pallas_call(body, out_shape=[pltpu.VMEM(*o) if isinstance(o, tuple) el...]
  transfers between devices with their start and end apart: 10 -> 10, of which waited for: 5 -> 4; matrix products, arithmetic and copies ran while one was open for 2% -> 2% of each run, Pallas kernels for 14% -> 15%
where the time goes in v2:
time: 135 us; the launch traced here: 134 us
  blocking collectives  37.9 us (28%)
  Pallas kernels  35.7 us (26%)
  starting transfers between devices  29.9 us (22%)
  waiting for transfers between devices  24.2 us (18%)
  other arithmetic  2.64 us (2%)
  local copies, waits for them, and re-layouts  2.5 us (2%)
  between operations  1.43 us (1%)
    all_to_all x2, blocking collectives, swap(): return lax.all_to_all(x, axes, split_axis=0, concat_axis=0, tiled=True)  37.9 us
    pallas_call x12, Pallas kernels, call(): pl.pallas_call(body, out_shape=[pltpu.VMEM(*o) if isinstance(o, tuple) el...  32.3 us
    all_to_all x3, waiting for transfers between devices, swap(): return lax.all_to_all(x, axes, split_axis=0, concat_axis=0, tiled=True)  23.3 us
    all_to_all x3, starting transfers between devices, swap(): return lax.all_to_all(x, axes, split_axis=0, concat_axis=0, tiled=True)  22.3 us
    ppermute x7, starting transfers between devices, core_swap(): return lax.ppermute(x, 'dom_3', [(0, 1), (1, 0)])  7.6 us
  transfers between devices with their start and end apart: 10, of which 4 were waited for; matrix products, arithmetic and copies ran while one was open for 2% of the time, Pallas kernels for 15%

profile of v2, /device:TPU:1, one launch (start us, length us, event | category | flops | bytes accessed | tf_op | source)
XLA Modules:
  0.0 134.2 jit_solution(3132171119838718624)
XLA Ops:
  0.6 2.5 %shard_map.95 = bf16[128,4,512]{2,1,0:T(4,128)(2,1)} custom-call(s32[4,128]{1,0:T(4,128)} %bitcast.16, bf16[512,512]{1,0:T(8,128)(2,1)} %features_ref.7), custom_call_target="tpu_custom_call" | custom-call | tf_op jit(solution)/shard_map/pallas_call | solution.py:83
  3.1 11.9 %all-to-all-start = ((bf16[128,4,512]{2,1,0:T(4,128)(2,1)}), bf16[128,4,512]{2,1,0:T(4,128)(2,1)}, u32[]{:S(2)}, u32[]{:S(2)}) async-start(bf16[128,4,512]{2,1,0:T(4,128)(2,1)} %shard_map.95), calls=%async_computation | async-start | bytes 1048576 | tf_op jit(solution)/shard_map/all_to_all | solution.py:35
  15.2 8.3 %shard_map.94 = (bf16[2,512,512]{2,1,0:T(8,128)(2,1)}, f32[2,512,512]{2,1,0:T(8,128)S(1)}, f32[512,512]{1,0:T(8,128)}) custom-call(bf16[512,512]{1,0:T(8,128)(2,1)} %features_ref.7, bf16[3,512,512]{2,1,0:T(8,128)(2,1)} %second_ref.1, s32[512,16]{1,0:T(8,128)S(1)} %copy.12.nbr_ref), custom_call_target="tpu_custom_call" | custom-call | tf_op jit(solution)/shard_map/pallas_call | solution.py:83
  23.5 4.8 %all-to-all-done = bf16[128,4,512]{2,1,0:T(4,128)(2,1)} async-done(((bf16[128,4,512]{2,1,0:T(4,128)(2,1)}), bf16[128,4,512]{2,1,0:T(4,128)(2,1)}, u32[]{:S(2)}, u32[]{:S(2)}) %all-to-all-start) | async-done | bytes 524320 | tf_op jit(solution)/shard_map/all_to_all | solution.py:35
  28.3 1.2 reshape.29.halo_ref
  29.5 4.1 %shard_map.96 = (bf16[2,512,512]{2,1,0:T(8,128)(2,1)}, bf16[512,512]{1,0:T(8,128)(2,1)S(1)}, bf16[64,8,512]{2,1,0:T(8,128)(2,1)}) custom-call(s32[8]{0:T(128)S(1)} %copy-done.1, bf16[2,512,512]{2,1,0:T(8,128)(2,1)} %get-tuple-element.44.halo_count_ref, bf16[512,512]{1,0:T(8,128)(2,1)S(1)} %reshape.29.halo_ref, ...), custom_call_target="tpu_custom_call" | custom-call | tf_op jit(solution)/shard_map/pallas_call | solution.py:83
  33.6 5.7 %all-to-all-start.1 = ((bf16[64,8,512]{2,1,0:T(8,128)(2,1)}), bf16[64,8,512]{2,1,0:T(8,128)(2,1)S(1)}, u32[]{:S(2)}, u32[]{:S(2)}) async-start(bf16[64,8,512]{2,1,0:T(8,128)(2,1)} %get-tuple-element.49), calls=%async_computation.1 | async-start | bytes 1048576 | tf_op jit(solution)/shard_map/all_to_all | solution.py:35
  39.9 5.1 %shard_map.97 = (f32[512,512]{1,0:T(8,128)}, f32[8,128]{1,0:T(8,128)S(1)}, f32[512,128]{1,0:T(8,128)S(1)}, bf16[512,1024]{1,0:T(8,128)(2,1)S(1)}) custom-call(s32[1]{0:T(128)S(6)} %copy.14.count_ref, bf16[512,512]{1,0:T(8,128)(2,1)S(1)} %get-tuple-element.48.embed_ref, s32[16,2,256]{2,1,0:T(2,128)} %ends_ref.1, bf16[512,512]{1,0:T(8,128)(2,1)} %features_ref.7, ...), custom_call_target="tpu_custom_call" | custom-call | tf_op jit(solution)/shard_map/pallas_call | solution.py:83
  45.1 6.7 %all-to-all-done.1 = bf16[64,8,512]{2,1,0:T(8,128)(2,1)S(1)} async-done(((bf16[64,8,512]{2,1,0:T(8,128)(2,1)}), bf16[64,8,512]{2,1,0:T(8,128)(2,1)S(1)}, u32[]{:S(2)}, u32[]{:S(2)}) %all-to-all-start.1) | async-done | bytes 524320 | tf_op jit(solution)/shard_map/all_to_all | solution.py:35
  51.7 2.0 %collective-permute-start = (bf16[512,512]{1,0:T(8,128)(2,1)S(1)}, bf16[512,512]{1,0:T(8,128)(2,1)S(1)}, u32[]{:S(2)}, u32[]{:S(2)}) collective-permute-start(bf16[512,512]{1,0:T(8,128)(2,1)S(1)} %bitcast.10), channel_id=1, source_target_pairs={{0,1},{1,0},{2,3},{3,2},{4,5},{5,4},{6,7},{7,6},{8,9},{9,8},{10,11... | collective-permute-start | bytes 1572872 | tf_op jit(solution)/shard_map/ppermute | solution.py:39
  53.7 1.8 %shard_map.98 = (bf16[512,512]{1,0:T(8,128)(2,1)S(1)}, f32[512,512]{1,0:T(8,128)S(1)}, f32[8,128]{1,0:T(8,128)S(1)}) custom-call(bf16[512,512]{1,0:T(8,128)(2,1)S(1)} %get-tuple-element.48.embed_ref, bf16[512,512]{1,0:T(8,128)(2,1)S(1)} %bitcast.11, bf16[512,1024]{1,0:T(8,128)(2,1)S(1)} %get-tuple-element.53.spread_ref, ...), custom_call_target="tpu_custom_call" | custom-call | tf_op jit(solution)/shard_map/pallas_call | solution.py:83
  55.5 1.8 %shard_map.99 = (bf16[512,512]{1,0:T(8,128)(2,1)S(1)}, bf16[512,512]{1,0:T(8,128)(2,1)S(1)}, f32[8,128]{1,0:T(8,128)S(1)}) custom-call(bf16[512,512]{1,0:T(8,128)(2,1)S(1)} %get-tuple-element.48.embed_ref, bf16[512,512]{1,0:T(8,128)(2,1)S(1)} %collective-permute-done.rows_ref, bf16[512,1024]{1,0:T(8,128)(2,1)S(1)} %get-tuple-element.53.spread_ref, ...), custom_call_target="tpu_custom_call" | custom-call | tf_op jit(solution)/shard_map/pallas_call | solution.py:83
  57.4 0.4 collective-permute-start.2
  57.9 1.9 %shard_map.100.grad_ref = f32[512,512]{1,0:T(8,128)S(1)} custom-call(bf16[512,512]{1,0:T(8,128)(2,1)S(1)} %get-tuple-element.59.near_weight_ref, bf16[512,512]{1,0:T(8,128)(2,1)S(1)} %bitcast.12, bf16[512,512]{1,0:T(8,128)(2,1)S(1)} %get-tuple-element.60.weight_ref, bf16[512,512]{1,0:T(8,128)(2,1)S(1)} %collective-permute-done.rows_ref, ...), custom_call_target="tpu_custom_call" | custom-call | tf_op jit(solution)/shard_map/pallas_call | solution.py:83
  59.8 1.2 shard_map.101
  61.0 2.9 %shard_map.102 = (f32[1536,256]{1,0:T(8,128)S(1)}, f32[1536,256]{1,0:T(8,128)S(1)}, bf16[16,1536]{1,0:T(8,128)(2,1)S(1)}) custom-call(s32[8]{0:T(128)S(1)} %copy-done.1, s32[1]{0:T(128)} %bitcast.core_ref, f32[512,512]{1,0:T(8,128)S(1)} %shard_map.100.grad_ref, bf16[512,512]{1,0:T(8,128)(2,1)} %features_ref.7, bf16[2,512,512]{2,1,0:T(8,128)(2,1)} %get-tuple-element.50.means_ref), custom_call_target="tpu_custom_call" | custom-call | tf_op jit(solution)/shard_map/pallas_call | solution.py:83
  63.9 1.1 copy-done
  65.0 0.3 collective-permute-start.3
  65.3 4.6 %all-to-all-start.2 = ((bf16[64,8,640]{2,1,0:T(8,128)(2,1)}), bf16[64,8,640]{2,1,0:T(8,128)(2,1)S(1)}, u32[]{:S(2)}, u32[]{:S(2)}) async-start(bf16[64,8,640]{2,1,0:T(8,128)(2,1)} %shard_map.101), calls=%async_computation.2 | async-start | bytes 1310720 | tf_op jit(solution)/shard_map/all_to_all | solution.py:35
  69.9 0.3 collective-permute-start.4
  70.3 2.1 %add.3.known_ref = f32[1536,256]{1,0:T(8,128)S(1)} add(f32[1536,256]{1,0:T(8,128)} %copy-done, f32[1536,256]{1,0:T(8,128)} %collective-permute-done.3) | non-fusion elementwise | flops 393216 | bytes 4718592 | tf_op jit(solution)/shard_map/add | solution.py:412
  72.3 11.8 %all-to-all-done.2.arrived_ref = bf16[64,8,640]{2,1,0:T(8,128)(2,1)S(1)} async-done(((bf16[64,8,640]{2,1,0:T(8,128)(2,1)}), bf16[64,8,640]{2,1,0:T(8,128)(2,1)S(1)}, u32[]{:S(2)}, u32[]{:S(2)}) %all-to-all-start.2) | async-done | bytes 655392 | tf_op jit(solution)/shard_map/all_to_all | solution.py:35
  84.2 0.7 shard_map.103
  84.9 1.6 %collective-permute-start.5 = (bf16[16,256]{1,0:T(8,128)(2,1)S(1)}, bf16[16,256]{1,0:T(8,128)(2,1)S(1)}, u32[]{:S(2)}, u32[]{:S(2)}) collective-permute-start(bf16[16,256]{1,0:T(8,128)(2,1)S(1)} %get-tuple-element.74), channel_id=1, source_target_pairs={{0,1},{1,0},{2,3},{3,2},{4,5},{5,4},{6,7},{7,6},{8,9},{9,8},{10,11... | collective-permute-start | bytes 24584 | tf_op jit(solution)/shard_map/ppermute | solution.py:39
  86.5 0.8 collective-permute-done.5.other_row_ref
  87.3 0.6 shard_map.104
  88.0 19.4 %all_to_all.25 = f16[64,24,256]{2,1,0:T(8,128)(2,1)S(1)} all-to-all(f16[64,24,256]{2,1,0:T(8,128)(2,1)S(1)} %bitcast.14), channel_id=1, replica_groups=mesh['dom_0'=4,'dom_1'=4,'dom_2'=4,'dom_3'=2] {'dom_0','dom_1','dom_2'}, dimensions={0} | all-to-all | bytes 1572864 | tf_op jit(solution)/shard_map/all_to_all | solution.py:35
  107.6 18.5 %all_to_all.26 = f16[64,24,256]{2,1,0:T(8,128)(2,1)S(1)} all-to-all(f16[64,24,256]{2,1,0:T(8,128)(2,1)S(1)} %broadcast_in_dim.3), channel_id=1, replica_groups=mesh['dom_0'=4,'dom_1'=4,'dom_2'=4,'dom_3'=2] {'dom_0','dom_1','dom_2'}, dimensions={0} | all-to-all | bytes 1572864 | tf_op jit(solution)/shard_map/all_to_all | solution.py:35
  126.1 2.9 %collective-permute-start.6 = (f16[1536,256]{1,0:T(8,128)(2,1)S(1)}, f16[1536,256]{1,0:T(8,128)(2,1)S(1)}, u32[]{:S(2)}, u32[]{:S(2)}) collective-permute-start(f16[1536,256]{1,0:T(8,128)(2,1)S(1)} %bitcast.13), channel_id=1, source_target_pairs={{0,1},{1,0},{2,3},{3,2},{4,5},{5,4},{6,7},{7,6},{8,9},{9,8},{10,11... | collective-permute-start | bytes 2359304 | tf_op jit(solution)/shard_map/ppermute | solution.py:39
  129.0 1.5 %shard_map.107 = bf16[512,512]{1,0:T(8,128)(2,1)} custom-call(s32[8]{0:T(128)S(1)} %copy-done.1, f32[8,512]{1,0:T(8,128)S(1)} %get-tuple-element.82.total_ref, f32[512,512]{1,0:T(8,128)S(1)} %shard_map.100.grad_ref), custom_call_target="tpu_custom_call" | custom-call | tf_op jit(solution)/shard_map/pallas_call | solution.py:83
  130.7 1.7 %shard_map.105 = (f32[3,512,512]{2,1,0:T(8,128)}, f32[1,1]{1,0:T(1,128)}) custom-call(s32[1]{0:T(128)} %bitcast.core_ref, f32[1536,256]{1,0:T(8,128)S(1)} %bitcast_convert_fusion.half_ref, f32[8,256]{1,0:T(8,128)S(1)} %get-tuple-element.77.factor_ref, f32[8,128]{1,0:T(8,128)S(1)} %get-tuple-element.75.note_ref), custom_call_target="tpu_custom_call" | custom-call | tf_op jit(solution)/shard_map/pallas_call | solution.py:442
  132.5 1.7 %shard_map.106 = f32[3,512,512]{2,1,0:T(8,128)} custom-call(s32[1]{0:T(128)} %bitcast.core_ref, f32[1536,256]{1,0:T(8,128)S(1)} %convert_element_type.19.half_ref, f32[8,256]{1,0:T(8,128)S(1)} %get-tuple-element.77.factor_ref, f32[8,128]{1,0:T(8,128)S(1)} %get-tuple-element.75.note_ref, ...), custom_call_target="tpu_custom_call", output_to_operand_aliasing={{}: (4, {})} | custom-call | tf_op jit(solution)/shard_map/pallas_call | solution.py:444
  (19 shorter events, 0.9 us)
Async XLA Ops:
  0.6 14.5 %copy-start.2 = (s32[512,2,8]{0,2,1:T(8,128)S(1)}, s32[512,2,8]{0,2,1:T(8,128)}, u32[]{:S(2)}) copy-start(s32[512,2,8]{0,2,1:T(8,128)} %param.10) | copy-start | bytes 98308
  3.1 25.2 %all-to-all-start = ((bf16[128,4,512]{2,1,0:T(4,128)(2,1)}), bf16[128,4,512]{2,1,0:T(4,128)(2,1)}, u32[]{:S(2)}, u32[]{:S(2)}) async-start(bf16[128,4,512]{2,1,0:T(4,128)(2,1)} %shard_map.95), calls=%async_computation | async-start | bytes 1048576 | tf_op jit(solution)/shard_map/all_to_all | solution.py:35
  15.2 14.3 %copy-start.1 = (s32[8]{0:T(128)S(1)}, s32[8]{0:T(128)}, u32[]{:S(2)}) copy-start(s32[8]{0:T(128)} %neg_ids_ref.7) | copy-start | bytes 100
  33.6 18.1 %all-to-all-start.1 = ((bf16[64,8,512]{2,1,0:T(8,128)(2,1)}), bf16[64,8,512]{2,1,0:T(8,128)(2,1)S(1)}, u32[]{:S(2)}, u32[]{:S(2)}) async-start(bf16[64,8,512]{2,1,0:T(8,128)(2,1)} %get-tuple-element.49), calls=%async_computation.1 | async-start | bytes 1048576 | tf_op jit(solution)/shard_map/all_to_all | solution.py:35
  51.7 3.8 %collective-permute-start = (bf16[512,512]{1,0:T(8,128)(2,1)S(1)}, bf16[512,512]{1,0:T(8,128)(2,1)S(1)}, u32[]{:S(2)}, u32[]{:S(2)}) collective-permute-start(bf16[512,512]{1,0:T(8,128)(2,1)S(1)} %bitcast.10), channel_id=1, source_target_pairs={{0,1},{1,0},{2,3},{3,2},{4,5},{5,4},{6,7},{7,6},{8,9},{9,8},{10,11... | collective-permute-start | bytes 1572872 | tf_op jit(solution)/shard_map/ppermute | solution.py:39
  57.3 2.5 %collective-permute-start.1 = (bf16[512,512]{1,0:T(8,128)(2,1)S(1)}, bf16[512,512]{1,0:T(8,128)(2,1)S(1)}, u32[]{:S(2)}, u32[]{:S(2)}) collective-permute-start(bf16[512,512]{1,0:T(8,128)(2,1)S(1)} %get-tuple-element.58), channel_id=1, source_target_pairs={{0,1},{1,0},{2,3},{3,2},{4,5},{5,4},{6,7},{7,6},{8,9},{9,8},{10,11... | collective-permute-start | bytes 1572872 | tf_op jit(solution)/shard_map/ppermute | solution.py:39
  57.4 2.4 %collective-permute-start.2 = (f32[8,128]{1,0:T(8,128)S(1)}, f32[8,128]{1,0:T(8,128)S(1)}, u32[]{:S(2)}, u32[]{:S(2)}) collective-permute-start(f32[8,128]{1,0:T(8,128)S(1)} %get-tuple-element.63.own_note_ref), channel_id=1, source_target_pairs={{0,1},{1,0},{2,3},{3,2},{4,5},{5,4},{6,7},{7,6},{8,9},{9,8},{10,11... | collective-permute-start | bytes 12296 | tf_op jit(solution)/shard_map/ppermute | solution.py:39
  63.9 1.1 copy-start
  65.0 5.2 %collective-permute-start.3 = (f32[1536,256]{1,0:T(8,128)S(1)}, f32[1536,256]{1,0:T(8,128)}, u32[]{:S(2)}, u32[]{:S(2)}) collective-permute-start(f32[1536,256]{1,0:T(8,128)S(1)} %get-tuple-element.68), channel_id=1, source_target_pairs={{0,1},{1,0},{2,3},{3,2},{4,5},{5,4},{6,7},{7,6},{8,9},{9,8},{10,11... | collective-permute-start | bytes 4718600 | tf_op jit(solution)/shard_map/ppermute | solution.py:39
  65.3 18.9 %all-to-all-start.2 = ((bf16[64,8,640]{2,1,0:T(8,128)(2,1)}), bf16[64,8,640]{2,1,0:T(8,128)(2,1)S(1)}, u32[]{:S(2)}, u32[]{:S(2)}) async-start(bf16[64,8,640]{2,1,0:T(8,128)(2,1)} %shard_map.101), calls=%async_computation.2 | async-start | bytes 1310720 | tf_op jit(solution)/shard_map/all_to_all | solution.py:35
  69.9 2.4 %collective-permute-start.4 = (bf16[16,1536]{1,0:T(8,128)(2,1)S(1)}, bf16[16,1536]{1,0:T(8,128)(2,1)S(1)}, u32[]{:S(2)}, u32[]{:S(2)}) collective-permute-start(bf16[16,1536]{1,0:T(8,128)(2,1)S(1)} %get-tuple-element.69.own_chosen_ref), channel_id=1, source_target_pairs={{0,1},{1,0},{2,3},{3,2},{4,5},{5,4},{6,7},{7,6},{8,9},{9,8},{10,11... | collective-permute-start | bytes 147464 | tf_op jit(solution)/shard_map/ppermute | solution.py:39
  84.9 2.4 %collective-permute-start.5 = (bf16[16,256]{1,0:T(8,128)(2,1)S(1)}, bf16[16,256]{1,0:T(8,128)(2,1)S(1)}, u32[]{:S(2)}, u32[]{:S(2)}) collective-permute-start(bf16[16,256]{1,0:T(8,128)(2,1)S(1)} %get-tuple-element.74), channel_id=1, source_target_pairs={{0,1},{1,0},{2,3},{3,2},{4,5},{5,4},{6,7},{7,6},{8,9},{9,8},{10,11... | collective-permute-start | bytes 24584 | tf_op jit(solution)/shard_map/ppermute | solution.py:39
  126.1 6.3 %collective-permute-start.6 = (f16[1536,256]{1,0:T(8,128)(2,1)S(1)}, f16[1536,256]{1,0:T(8,128)(2,1)S(1)}, u32[]{:S(2)}, u32[]{:S(2)}) collective-permute-start(f16[1536,256]{1,0:T(8,128)(2,1)S(1)} %bitcast.13), channel_id=1, source_target_pairs={{0,1},{1,0},{2,3},{3,2},{4,5},{5,4},{6,7},{7,6},{8,9},{9,8},{10,11... | collective-permute-start | bytes 2359304 | tf_op jit(solution)/shard_map/ppermute | solution.py:39

commit v3 on v2

--- a/solution.py
+++ b/solution.py
@@ -29,6 +29,7 @@
 NT = (((1,), (1,)), ((), ()))
 TN = (((0,), (0,)), ((), ()))
 FROM_HBM = "hbm"
+BY_HAND = "by_hand"
 
 
 def swap(x, axes):
@@ -56,10 +57,6 @@
     return pl.BlockSpec(shape, lambda i: (0,) * len(shape))
 
 
-def weight_at(k):
-    return pl.BlockSpec((1, H, H), lambda i: (k, 0, 0))
-
-
 def smem():
     return pl.BlockSpec(memory_space=pltpu.SMEM)
 
@@ -73,19 +70,31 @@
 
 
 def call(body, outs, specs, scratch=(), args=()):
-    given = []
+    given, ins, made, back = [], [], [], []
     for spec, x in zip(specs, args):
-        if spec is FROM_HBM:
+        if spec is FROM_HBM or spec is BY_HAND:
             x = pltpu.with_memory_space_constraint(x, pltpu.HBM)
+            spec = whole(x.shape) if spec is FROM_HBM else pl.BlockSpec(memory_space=pl.ANY)
         elif spec.memory_space == pltpu.VMEM and x.dtype != jnp.int32:
             x = near_memory(x)
         given.append(x)
+        ins.append(spec)
+    for o in outs:
+        if isinstance(o, tuple) and len(o) == 3:
+            made.append(hbm(*o[:2]))
+            back.append(pl.BlockSpec(memory_space=pl.ANY))
+        elif isinstance(o, tuple):
+            made.append(pltpu.VMEM(*o))
+            back.append(vmem())
+        else:
+            made.append(o)
+            back.append(whole(o.shape))
     return pl.pallas_call(
         body,
-        out_shape=[pltpu.VMEM(*o) if isinstance(o, tuple) else o for o in outs],
+        out_shape=made,
         grid=(1,),
-        in_specs=[whole(x.shape) if spec is FROM_HBM else spec for spec, x in zip(specs, args)],
-        out_specs=[vmem() if isinstance(o, tuple) else whole(o.shape) for o in outs],
+        in_specs=ins,
+        out_specs=back,
         scratch_shapes=list(scratch),
         compiler_params=pltpu.CompilerParams(vmem_limit_bytes=28 << 20),
     )(*given)
@@ -99,7 +108,12 @@
         out_ref[:, k, :] = lax.dot_general(hit, own, TN, preferred_element_type=F32).astype(BF16)
 
 
-def counts_body(features_ref, w_ref, nbr_ref, halo_count_ref, own_sum_ref, pre_ref, own_count_ref):
+def counts_body(features_ref, w_ref, nbr_ref, halo_count_ref, own_sum_ref, pre_ref, own_buf, w_buf, halo_buf, count_buf, sum_buf, pre_buf, sems):
+    copy = pltpu.make_async_copy
+    fetch_own = copy(features_ref, own_buf, sems.at[0])
+    fetch_w = copy(w_ref.at[0], w_buf, sems.at[1])
+    fetch_own.start()
+    fetch_w.start()
     rows = 32
     lanes = lax.broadcasted_iota(jnp.int32, (rows, NODE_DEV), 1)
 
@@ -113,30 +127,54 @@
                     hit = lanes == (index[:, k : k + 1] - half * NODE_DEV)
                     total = total + jnp.where(hit, 1.0, 0.0)
                 if half == 0:
-                    own_count_ref[r, at, :] = total.astype(BF16)
+                    count_buf[r, at, :] = total.astype(BF16)
                 else:
-                    halo_count_ref[r, at, :] = total.astype(BF16)
+                    halo_buf[r, at, :] = total.astype(BF16)
         return 0
 
     lax.fori_loop(0, NODE_DEV // rows, chunk, 0)
-    own = features_ref[...]
+    leave = [copy(halo_buf, halo_count_ref, sems.at[2])]
+    leave[0].start()
+    fetch_own.wait()
+    own = own_buf[...]
     for r in range(RELS):
-        own_sum_ref[r] = dot(own_count_ref[r], own)
-    pre_ref[...] = dot(own, w_ref[0])
-
-
-def layer_body(neg_ids_ref, halo_count_ref, halo_ref, own_sum_ref, pre_ref, first_ref, second_ref, means_ref, embed_ref, picked_ref):
+        sum_buf[r] = dot(count_buf[r], own)
+        leave.append(copy(sum_buf.at[r], own_sum_ref.at[r], sems.at[3 + r]))
+        leave[-1].start()
+    fetch_w.wait()
+    pre_buf[...] = dot(own, w_buf[...])
+    leave.append(copy(pre_buf, pre_ref, sems.at[5]))
+    leave[-1].start()
+    for one in leave:
+        one.wait()
+
+
+def layer_body(neg_ids_ref, halo_count_ref, halo_ref, own_sum_ref, pre_ref, w_ref, means_ref, embed_ref, picked_ref, count_buf, sum_buf, w_buf, pre_buf, mean_buf, sems):
+    copy = pltpu.make_async_copy
+    counts = [copy(halo_count_ref.at[r], count_buf.at[r], sems.at[r]) for r in range(RELS)]
+    sums = [copy(own_sum_ref.at[r], sum_buf.at[r], sems.at[2 + r]) for r in range(RELS)]
+    maps = [copy(w_ref.at[r + 1], w_buf.at[r], sems.at[4 + r]) for r in range(RELS)]
+    first = copy(pre_ref, pre_buf, sems.at[6])
+    for one in (counts[0], sums[0], maps[0], counts[1], sums[1], first, maps[1]):
+        one.start()
     halo = halo_ref[...]
-    preact = pre_ref[...]
-    for r, w_ref in enumerate((first_ref, second_ref)):
-        total = own_sum_ref[r] + dot(halo_count_ref[r], halo)
-        mean = (total * (1.0 / FAN)).astype(BF16)
-        means_ref[r] = mean
-        preact = preact + dot(mean, w_ref[0])
-    embed = preact.astype(BF16)
+    parts, leave = [], []
+    for r in range(RELS):
+        counts[r].wait()
+        total = dot(count_buf[r], halo)
+        sums[r].wait()
+        mean_buf[r] = ((sum_buf[r] + total) * (1.0 / FAN)).astype(BF16)
+        leave.append(copy(mean_buf.at[r], means_ref.at[r], sems.at[7 + r]))
+        leave[r].start()
+        maps[r].wait()
+        parts.append(dot(mean_buf[r], w_buf[r]))
+    first.wait()
+    embed = (pre_buf[...] + parts[0] + parts[1]).astype(BF16)
     embed_ref[...] = embed
     picked = dot(chosen_rows(neg_ids_ref), embed)[:NEG_DEV]
     picked_ref[...] = jnp.broadcast_to(picked[None], (CHIPS, NEG_DEV, H)).astype(BF16)
+    for one in leave:
+        one.wait()
 
 
 def soft_parts(x):
@@ -309,25 +347,24 @@
 def first_half_body(core_ref, half_ref, factor_ref, note_ref, weight_ref, loss_ref):
     note = note_ref[0:1, :]
     loss_ref[...] = (note[:, 0:1] + note[:, 3:4] + note[:, 4:5]) / (note[:, 1:2] * TILE)
-    weight_ref[0] = half_ref[...] * factor_ref[0:1, :]
+    weight_ref[...] = (half_ref[...] * factor_ref[0:1, :]).reshape(RELS + 1, H, HALF)
 
 
 def second_half_body(core_ref, half_ref, factor_ref, note_ref, begun_ref, weight_ref):
-    weight_ref[0] = half_ref[...] * factor_ref[0:1, :]
+    weight_ref[...] = (half_ref[...] * factor_ref[0:1, :]).reshape(RELS + 1, H, HALF)
 
 
 def halves(body, which, extra, alias):
     whole_weight = jax.ShapeDtypeStruct((RELS + 1, H, H), F32)
-    block = pl.BlockSpec((1, H, HALF), lambda r, core: (r, 0, which(core[0])))
+    block = pl.BlockSpec((RELS + 1, H, HALF), lambda r, core: (0, 0, which(core[0])))
     scalar = pl.BlockSpec((1, 1), lambda r, core: (0, 0))
-    full = pl.BlockSpec((H, HALF), lambda r, core: (r, 0))
     return pl.pallas_call(
         body,
         out_shape=[whole_weight, jax.ShapeDtypeStruct((1, 1), F32)][: 1 + extra],
         grid_spec=pltpu.PrefetchScalarGridSpec(
             num_scalar_prefetch=1,
-            grid=(RELS + 1,),
-            in_specs=[full, vmem(), vmem()] + [pl.BlockSpec(memory_space=pl.ANY)] * len(alias),
+            grid=(1,),
+            in_specs=[vmem(), vmem(), vmem()] + [pl.BlockSpec(memory_space=pl.ANY)] * len(alias),
             out_specs=[block, scalar][: 1 + extra],
         ),
         input_output_aliases=alias,
@@ -343,20 +380,20 @@
     (outgoing,) = call(halo_body, [hbm((N_DOM, HALO_PEER, H), BF16)], [FROM_HBM, FROM_HBM], (), (halo_send[0].T, features))
     incoming = swap(outgoing, DOM)
     neighbours = nbr_index.reshape(NODE_DEV, RELS * FAN)
-    weights = pltpu.with_memory_space_constraint(weights, pltpu.HBM)
+    two = (RELS, *square)
     halo_count, own_sum, pre = call(
         counts_body,
-        [hbm((RELS, NODE_DEV, 512), BF16), ((RELS, *square), F32), hbm(square, F32)],
-        [FROM_HBM, weight_at(0), vmem()],
-        [pltpu.VMEM((RELS, NODE_DEV, NODE_DEV), BF16)],
+        [(two, BF16, BY_HAND), (two, F32, BY_HAND), (square, F32, BY_HAND)],
+        [BY_HAND, BY_HAND, vmem()],
+        [pltpu.VMEM(square, BF16)] * 2 + [pltpu.VMEM(two, BF16)] * 2 + [pltpu.VMEM(two, F32), pltpu.VMEM(square, F32), pltpu.SemaphoreType.DMA((6,))],
         (features, weights, neighbours),
     )
     means, embed, picked = call(
         layer_body,
-        [hbm((RELS, *square), BF16), (square, BF16), hbm((CHIPS, NEG_DEV, H), BF16)],
-        [smem(), FROM_HBM, vmem(), vmem(), FROM_HBM, weight_at(1), weight_at(2)],
-        (),
-        (neg_ids, halo_count, incoming.reshape(512, H), own_sum, pre, weights, weights),
+        [(two, BF16, BY_HAND), (square, BF16), hbm((CHIPS, NEG_DEV, H), BF16)],
+        [smem(), BY_HAND, vmem(), BY_HAND, BY_HAND, BY_HAND],
+        [pltpu.VMEM(two, BF16), pltpu.VMEM(two, F32), pltpu.VMEM(two, BF16), pltpu.VMEM(square, F32), pltpu.VMEM(two, BF16), pltpu.SemaphoreType.DMA((9,))],
+        (neg_ids, halo_count, incoming.reshape(512, H), own_sum, pre, weights),
     )
     near_rows = swap(picked, FAR).reshape(square)
     base, note, sources, spread = call(
@@ -434,7 +471,8 @@
         (known, chosen, other_chosen, own_row, other_row, note),
     )
     chunks = (CHIPS, 24, HALF)
-    mine = jnp.sum(swap(partial.astype(F16).reshape(chunks), FAR).astype(F32), axis=0).astype(F16)
+    sums = swap(partial.astype(F16).reshape(chunks), FAR)
+    mine = jnp.sum(sums.astype(F32), axis=0).astype(F16)
     half = swap(jnp.broadcast_to(mine, chunks), FAR).reshape(tall)
     other_half = core_swap(half).astype(F32)
     half = half.astype(F32)

time: 135 us -> 132 us (0.978)
  Pallas kernels: 35.7 us -> 34.3 us
    all_to_all x3, starting transfers between devices: 22.3 us -> 20.8 us  [swap(): return lax.all_to_all(x, axes, split_axis=0, concat_axis=0, tiled=True)]
  transfers between devices with their start and end apart: 10 -> 10, of which waited for: 4 -> 4; matrix products, arithmetic and copies ran while one was open for 2% -> 2% of each run, Pallas kernels for 15% -> 14%
where the time goes in v3:
time: 132 us
  blocking collectives  37.9 us (29%)
  Pallas kernels  34.3 us (26%)
  starting transfers between devices  28.9 us (22%)
  waiting for transfers between devices  25 us (19%)
  other arithmetic  2.64 us (2%)
  local copies, waits for them, and re-layouts  1.46 us (1%)
  between operations  1.45 us (1%)
    all_to_all x2, blocking collectives, swap(): return lax.all_to_all(x, axes, split_axis=0, concat_axis=0, tiled=True)  37.9 us
    pallas_call x12, Pallas kernels, call(): pl.pallas_call(body, out_shape=made, grid=(1,), in_specs=ins, out_specs=b...  31.7 us
    all_to_all x3, waiting for transfers between devices, swap(): return lax.all_to_all(x, axes, split_axis=0, concat_axis=0, tiled=True)  24.2 us
    all_to_all x3, starting transfers between devices, swap(): return lax.all_to_all(x, axes, split_axis=0, concat_axis=0, tiled=True)  20.8 us
    ppermute x7, starting transfers between devices, core_swap(): return lax.ppermute(x, 'dom_3', [(0, 1), (1, 0)])  8.17 us
  transfers between devices with their start and end apart: 10, of which 4 were waited for; matrix products, arithmetic and copies ran while one was open for 2% of the time, Pallas kernels for 14%

profile of v3, /device:TPU:1, one launch (start us, length us, event | category | flops | bytes accessed | tf_op | source)
XLA Modules:
  0.0 131.7 jit_solution(11602478486721256892)
XLA Ops:
  0.6 2.5 %shard_map.95 = bf16[128,4,512]{2,1,0:T(4,128)(2,1)} custom-call(s32[4,128]{1,0:T(4,128)} %bitcast.16, bf16[512,512]{1,0:T(8,128)(2,1)} %features_ref.7), custom_call_target="tpu_custom_call" | custom-call | tf_op jit(solution)/shard_map/pallas_call | solution.py:92
  3.1 11.5 %all-to-all-start = ((bf16[128,4,512]{2,1,0:T(4,128)(2,1)}), bf16[128,4,512]{2,1,0:T(4,128)(2,1)S(1)}, u32[]{:S(2)}, u32[]{:S(2)}) async-start(bf16[128,4,512]{2,1,0:T(4,128)(2,1)} %shard_map.95), calls=%async_computation | async-start | bytes 1048576 | tf_op jit(solution)/shard_map/all_to_all | solution.py:36
  14.8 7.2 %shard_map.94 = (bf16[2,512,512]{2,1,0:T(8,128)(2,1)}, f32[2,512,512]{2,1,0:T(8,128)}, f32[512,512]{1,0:T(8,128)}) custom-call(bf16[512,512]{1,0:T(8,128)(2,1)} %features_ref.7, bf16[3,512,512]{2,1,0:T(8,128)(2,1)} %w_ref.3, s32[512,16]{1,0:T(8,128)S(1)} %copy.12.nbr_ref), custom_call_target="tpu_custom_call" | custom-call | tf_op jit(solution)/shard_map/pallas_call | solution.py:92
  22.0 6.3 %all-to-all-done = bf16[128,4,512]{2,1,0:T(4,128)(2,1)S(1)} async-done(((bf16[128,4,512]{2,1,0:T(4,128)(2,1)}), bf16[128,4,512]{2,1,0:T(4,128)(2,1)S(1)}, u32[]{:S(2)}, u32[]{:S(2)}) %all-to-all-start) | async-done | bytes 524320 | tf_op jit(solution)/shard_map/all_to_all | solution.py:36
  28.4 4.6 %shard_map.96 = (bf16[2,512,512]{2,1,0:T(8,128)(2,1)}, bf16[512,512]{1,0:T(8,128)(2,1)S(1)}, bf16[64,8,512]{2,1,0:T(8,128)(2,1)}) custom-call(s32[8]{0:T(128)S(1)} %copy-done.1, bf16[2,512,512]{2,1,0:T(8,128)(2,1)} %get-tuple-element.44.halo_count_ref, bf16[512,512]{1,0:T(8,128)(2,1)S(1)} %reshape.29.halo_ref, f32[2,512,512]{2,1,0:T(8,128)} %get-tuple-element.46.own_sum_ref, ...), custom_call_target="tpu_custom_call" | custom-call | tf_op jit(solution)/shard_map/pallas_call | solution.py:92
  33.0 4.6 %all-to-all-start.1 = ((bf16[64,8,512]{2,1,0:T(8,128)(2,1)}), bf16[64,8,512]{2,1,0:T(8,128)(2,1)S(1)}, u32[]{:S(2)}, u32[]{:S(2)}) async-start(bf16[64,8,512]{2,1,0:T(8,128)(2,1)} %get-tuple-element.49), calls=%async_computation.1 | async-start | bytes 1048576 | tf_op jit(solution)/shard_map/all_to_all | solution.py:36
  38.3 5.1 %shard_map.97 = (f32[512,512]{1,0:T(8,128)}, f32[8,128]{1,0:T(8,128)S(1)}, f32[512,128]{1,0:T(8,128)S(1)}, bf16[512,1024]{1,0:T(8,128)(2,1)S(1)}) custom-call(s32[1]{0:T(128)S(6)} %copy.14.count_ref, bf16[512,512]{1,0:T(8,128)(2,1)S(1)} %get-tuple-element.48.embed_ref, s32[16,2,256]{2,1,0:T(2,128)} %ends_ref.1, bf16[512,512]{1,0:T(8,128)(2,1)} %features_ref.7, ...), custom_call_target="tpu_custom_call" | custom-call | tf_op jit(solution)/shard_map/pallas_call | solution.py:92
  43.4 6.1 %all-to-all-done.1 = bf16[64,8,512]{2,1,0:T(8,128)(2,1)S(1)} async-done(((bf16[64,8,512]{2,1,0:T(8,128)(2,1)}), bf16[64,8,512]{2,1,0:T(8,128)(2,1)S(1)}, u32[]{:S(2)}, u32[]{:S(2)}) %all-to-all-start.1) | async-done | bytes 524320 | tf_op jit(solution)/shard_map/all_to_all | solution.py:36
  49.5 2.6 %collective-permute-start = (bf16[512,512]{1,0:T(8,128)(2,1)S(1)}, bf16[512,512]{1,0:T(8,128)(2,1)S(1)}, u32[]{:S(2)}, u32[]{:S(2)}) collective-permute-start(bf16[512,512]{1,0:T(8,128)(2,1)S(1)} %bitcast.10), channel_id=1, source_target_pairs={{0,1},{1,0},{2,3},{3,2},{4,5},{5,4},{6,7},{7,6},{8,9},{9,8},{10,11... | collective-permute-start | bytes 1572872 | tf_op jit(solution)/shard_map/ppermute | solution.py:40
  52.1 1.8 %shard_map.98 = (bf16[512,512]{1,0:T(8,128)(2,1)S(1)}, f32[512,512]{1,0:T(8,128)S(1)}, f32[8,128]{1,0:T(8,128)S(1)}) custom-call(bf16[512,512]{1,0:T(8,128)(2,1)S(1)} %get-tuple-element.48.embed_ref, bf16[512,512]{1,0:T(8,128)(2,1)S(1)} %bitcast.11, bf16[512,1024]{1,0:T(8,128)(2,1)S(1)} %get-tuple-element.53.spread_ref, ...), custom_call_target="tpu_custom_call" | custom-call | tf_op jit(solution)/shard_map/pallas_call | solution.py:92
  53.9 1.8 %shard_map.99 = (bf16[512,512]{1,0:T(8,128)(2,1)S(1)}, bf16[512,512]{1,0:T(8,128)(2,1)S(1)}, f32[8,128]{1,0:T(8,128)S(1)}) custom-call(bf16[512,512]{1,0:T(8,128)(2,1)S(1)} %get-tuple-element.48.embed_ref, bf16[512,512]{1,0:T(8,128)(2,1)S(1)} %collective-permute-done.rows_ref, bf16[512,1024]{1,0:T(8,128)(2,1)S(1)} %get-tuple-element.53.spread_ref, ...), custom_call_target="tpu_custom_call" | custom-call | tf_op jit(solution)/shard_map/pallas_call | solution.py:92
  55.8 0.5 collective-permute-start.2
  56.3 1.9 %shard_map.100.grad_ref = f32[512,512]{1,0:T(8,128)S(1)} custom-call(bf16[512,512]{1,0:T(8,128)(2,1)S(1)} %get-tuple-element.59.near_weight_ref, bf16[512,512]{1,0:T(8,128)(2,1)S(1)} %bitcast.12, bf16[512,512]{1,0:T(8,128)(2,1)S(1)} %get-tuple-element.60.weight_ref, bf16[512,512]{1,0:T(8,128)(2,1)S(1)} %collective-permute-done.rows_ref, ...), custom_call_target="tpu_custom_call" | custom-call | tf_op jit(solution)/shard_map/pallas_call | solution.py:92
  58.2 1.1 shard_map.101
  59.3 2.9 %shard_map.102 = (f32[1536,256]{1,0:T(8,128)S(1)}, f32[1536,256]{1,0:T(8,128)S(1)}, bf16[16,1536]{1,0:T(8,128)(2,1)S(1)}) custom-call(s32[8]{0:T(128)S(1)} %copy-done.1, s32[1]{0:T(128)} %bitcast.core_ref, f32[512,512]{1,0:T(8,128)S(1)} %shard_map.100.grad_ref, bf16[512,512]{1,0:T(8,128)(2,1)} %features_ref.7, bf16[2,512,512]{2,1,0:T(8,128)(2,1)} %get-tuple-element.50.means_ref), custom_call_target="tpu_custom_call" | custom-call | tf_op jit(solution)/shard_map/pallas_call | solution.py:92
  62.2 1.1 copy-done
  63.4 0.3 collective-permute-start.3
  63.6 4.6 %all-to-all-start.2 = ((bf16[64,8,640]{2,1,0:T(8,128)(2,1)}), bf16[64,8,640]{2,1,0:T(8,128)(2,1)S(1)}, u32[]{:S(2)}, u32[]{:S(2)}) async-start(bf16[64,8,640]{2,1,0:T(8,128)(2,1)} %shard_map.101), calls=%async_computation.2 | async-start | bytes 1310720 | tf_op jit(solution)/shard_map/all_to_all | solution.py:36
  68.3 0.3 collective-permute-start.4
  68.6 2.1 %add.3.known_ref = f32[1536,256]{1,0:T(8,128)S(1)} add(f32[1536,256]{1,0:T(8,128)} %copy-done, f32[1536,256]{1,0:T(8,128)} %collective-permute-done.3) | non-fusion elementwise | flops 393216 | bytes 4718592 | tf_op jit(solution)/shard_map/add | solution.py:449
  70.7 11.8 %all-to-all-done.2.arrived_ref = bf16[64,8,640]{2,1,0:T(8,128)(2,1)S(1)} async-done(((bf16[64,8,640]{2,1,0:T(8,128)(2,1)}), bf16[64,8,640]{2,1,0:T(8,128)(2,1)S(1)}, u32[]{:S(2)}, u32[]{:S(2)}) %all-to-all-start.2) | async-done | bytes 655392 | tf_op jit(solution)/shard_map/all_to_all | solution.py:36
  82.5 0.7 shard_map.103
  83.2 1.6 %collective-permute-start.5 = (bf16[16,256]{1,0:T(8,128)(2,1)S(1)}, bf16[16,256]{1,0:T(8,128)(2,1)S(1)}, u32[]{:S(2)}, u32[]{:S(2)}) collective-permute-start(bf16[16,256]{1,0:T(8,128)(2,1)S(1)} %get-tuple-element.74), channel_id=1, source_target_pairs={{0,1},{1,0},{2,3},{3,2},{4,5},{5,4},{6,7},{7,6},{8,9},{9,8},{10,11... | collective-permute-start | bytes 24584 | tf_op jit(solution)/shard_map/ppermute | solution.py:40
  84.8 0.8 collective-permute-done.5.other_row_ref
  85.6 0.6 shard_map.104
  86.4 19.4 %all_to_all.25 = f16[64,24,256]{2,1,0:T(8,128)(2,1)S(1)} all-to-all(f16[64,24,256]{2,1,0:T(8,128)(2,1)S(1)} %bitcast.14), channel_id=1, replica_groups=mesh['dom_0'=4,'dom_1'=4,'dom_2'=4,'dom_3'=2] {'dom_0','dom_1','dom_2'}, dimensions={0} | all-to-all | bytes 1572864 | tf_op jit(solution)/shard_map/all_to_all | solution.py:36
  106.0 18.5 %all_to_all.26 = f16[64,24,256]{2,1,0:T(8,128)(2,1)S(1)} all-to-all(f16[64,24,256]{2,1,0:T(8,128)(2,1)S(1)} %broadcast_in_dim.3), channel_id=1, replica_groups=mesh['dom_0'=4,'dom_1'=4,'dom_2'=4,'dom_3'=2] {'dom_0','dom_1','dom_2'}, dimensions={0} | all-to-all | bytes 1572864 | tf_op jit(solution)/shard_map/all_to_all | solution.py:36
  124.5 2.9 %collective-permute-start.6 = (f16[1536,256]{1,0:T(8,128)(2,1)S(1)}, f16[1536,256]{1,0:T(8,128)(2,1)S(1)}, u32[]{:S(2)}, u32[]{:S(2)}) collective-permute-start(f16[1536,256]{1,0:T(8,128)(2,1)S(1)} %bitcast.13), channel_id=1, source_target_pairs={{0,1},{1,0},{2,3},{3,2},{4,5},{5,4},{6,7},{7,6},{8,9},{9,8},{10,11... | collective-permute-start | bytes 2359304 | tf_op jit(solution)/shard_map/ppermute | solution.py:40
  127.4 1.5 %shard_map.107 = bf16[512,512]{1,0:T(8,128)(2,1)} custom-call(s32[8]{0:T(128)S(1)} %copy-done.1, f32[8,512]{1,0:T(8,128)S(1)} %get-tuple-element.82.total_ref, f32[512,512]{1,0:T(8,128)S(1)} %shard_map.100.grad_ref), custom_call_target="tpu_custom_call" | custom-call | tf_op jit(solution)/shard_map/pallas_call | solution.py:92
  128.9 0.2 bitcast_convert_fusion.half_ref
  129.0 1.3 shard_map.105
  130.5 1.3 shard_map.106
  (19 shorter events, 0.8 us)
Async XLA Ops:
  0.6 14.0 %copy-start.2 = (s32[512,2,8]{0,2,1:T(8,128)S(1)}, s32[512,2,8]{0,2,1:T(8,128)}, u32[]{:S(2)}) copy-start(s32[512,2,8]{0,2,1:T(8,128)} %param.10) | copy-start | bytes 98308
  3.1 25.1 %all-to-all-start = ((bf16[128,4,512]{2,1,0:T(4,128)(2,1)}), bf16[128,4,512]{2,1,0:T(4,128)(2,1)S(1)}, u32[]{:S(2)}, u32[]{:S(2)}) async-start(bf16[128,4,512]{2,1,0:T(4,128)(2,1)} %shard_map.95), calls=%async_computation | async-start | bytes 1048576 | tf_op jit(solution)/shard_map/all_to_all | solution.py:36
  14.8 13.6 %copy-start.1 = (s32[8]{0:T(128)S(1)}, s32[8]{0:T(128)}, u32[]{:S(2)}) copy-start(s32[8]{0:T(128)} %neg_ids_ref.7) | copy-start | bytes 100
  33.0 16.5 %all-to-all-start.1 = ((bf16[64,8,512]{2,1,0:T(8,128)(2,1)}), bf16[64,8,512]{2,1,0:T(8,128)(2,1)S(1)}, u32[]{:S(2)}, u32[]{:S(2)}) async-start(bf16[64,8,512]{2,1,0:T(8,128)(2,1)} %get-tuple-element.49), calls=%async_computation.1 | async-start | bytes 1048576 | tf_op jit(solution)/shard_map/all_to_all | solution.py:36
  49.5 4.4 %collective-permute-start = (bf16[512,512]{1,0:T(8,128)(2,1)S(1)}, bf16[512,512]{1,0:T(8,128)(2,1)S(1)}, u32[]{:S(2)}, u32[]{:S(2)}) collective-permute-start(bf16[512,512]{1,0:T(8,128)(2,1)S(1)} %bitcast.10), channel_id=1, source_target_pairs={{0,1},{1,0},{2,3},{3,2},{4,5},{5,4},{6,7},{7,6},{8,9},{9,8},{10,11... | collective-permute-start | bytes 1572872 | tf_op jit(solution)/shard_map/ppermute | solution.py:40
  55.7 2.5 %collective-permute-start.1 = (bf16[512,512]{1,0:T(8,128)(2,1)S(1)}, bf16[512,512]{1,0:T(8,128)(2,1)S(1)}, u32[]{:S(2)}, u32[]{:S(2)}) collective-permute-start(bf16[512,512]{1,0:T(8,128)(2,1)S(1)} %get-tuple-element.58), channel_id=1, source_target_pairs={{0,1},{1,0},{2,3},{3,2},{4,5},{5,4},{6,7},{7,6},{8,9},{9,8},{10,11... | collective-permute-start | bytes 1572872 | tf_op jit(solution)/shard_map/ppermute | solution.py:40
  55.8 2.4 %collective-permute-start.2 = (f32[8,128]{1,0:T(8,128)S(1)}, f32[8,128]{1,0:T(8,128)S(1)}, u32[]{:S(2)}, u32[]{:S(2)}) collective-permute-start(f32[8,128]{1,0:T(8,128)S(1)} %get-tuple-element.63.own_note_ref), channel_id=1, source_target_pairs={{0,1},{1,0},{2,3},{3,2},{4,5},{5,4},{6,7},{7,6},{8,9},{9,8},{10,11... | collective-permute-start | bytes 12296 | tf_op jit(solution)/shard_map/ppermute | solution.py:40
  62.2 1.1 copy-start
  63.4 5.2 %collective-permute-start.3 = (f32[1536,256]{1,0:T(8,128)S(1)}, f32[1536,256]{1,0:T(8,128)}, u32[]{:S(2)}, u32[]{:S(2)}) collective-permute-start(f32[1536,256]{1,0:T(8,128)S(1)} %get-tuple-element.68), channel_id=1, source_target_pairs={{0,1},{1,0},{2,3},{3,2},{4,5},{5,4},{6,7},{7,6},{8,9},{9,8},{10,11... | collective-permute-start | bytes 4718600 | tf_op jit(solution)/shard_map/ppermute | solution.py:40
  63.6 18.9 %all-to-all-start.2 = ((bf16[64,8,640]{2,1,0:T(8,128)(2,1)}), bf16[64,8,640]{2,1,0:T(8,128)(2,1)S(1)}, u32[]{:S(2)}, u32[]{:S(2)}) async-start(bf16[64,8,640]{2,1,0:T(8,128)(2,1)} %shard_map.101), calls=%async_computation.2 | async-start | bytes 1310720 | tf_op jit(solution)/shard_map/all_to_all | solution.py:36
  68.3 2.4 %collective-permute-start.4 = (bf16[16,1536]{1,0:T(8,128)(2,1)S(1)}, bf16[16,1536]{1,0:T(8,128)(2,1)S(1)}, u32[]{:S(2)}, u32[]{:S(2)}) collective-permute-start(bf16[16,1536]{1,0:T(8,128)(2,1)S(1)} %get-tuple-element.69.own_chosen_ref), channel_id=1, source_target_pairs={{0,1},{1,0},{2,3},{3,2},{4,5},{5,4},{6,7},{7,6},{8,9},{9,8},{10,11... | collective-permute-start | bytes 147464 | tf_op jit(solution)/shard_map/ppermute | solution.py:40
  83.2 2.4 %collective-permute-start.5 = (bf16[16,256]{1,0:T(8,128)(2,1)S(1)}, bf16[16,256]{1,0:T(8,128)(2,1)S(1)}, u32[]{:S(2)}, u32[]{:S(2)}) collective-permute-start(bf16[16,256]{1,0:T(8,128)(2,1)S(1)} %get-tuple-element.74), channel_id=1, source_target_pairs={{0,1},{1,0},{2,3},{3,2},{4,5},{5,4},{6,7},{7,6},{8,9},{9,8},{10,11... | collective-permute-start | bytes 24584 | tf_op jit(solution)/shard_map/ppermute | solution.py:40
  124.5 5.9 %collective-permute-start.6 = (f16[1536,256]{1,0:T(8,128)(2,1)S(1)}, f16[1536,256]{1,0:T(8,128)(2,1)S(1)}, u32[]{:S(2)}, u32[]{:S(2)}) collective-permute-start(f16[1536,256]{1,0:T(8,128)(2,1)S(1)} %bitcast.13), channel_id=1, source_target_pairs={{0,1},{1,0},{2,3},{3,2},{4,5},{5,4},{6,7},{7,6},{8,9},{9,8},{10,11... | collective-permute-start | bytes 2359304 | tf_op jit(solution)/shard_map/ppermute | solution.py:40

commit v4 on v3

--- a/solution.py
+++ b/solution.py
@@ -149,13 +149,12 @@
         one.wait()
 
 
-def layer_body(neg_ids_ref, halo_count_ref, halo_ref, own_sum_ref, pre_ref, w_ref, means_ref, embed_ref, picked_ref, count_buf, sum_buf, w_buf, pre_buf, mean_buf, sems):
+def layer_body(neg_ids_ref, count_ref, halo_ref, own_sum_ref, pre_ref, w_ref, means_ref, embed_ref, picked_ref, count_buf, sum_buf, pre_buf, mean_buf, row_buf, sems):
     copy = pltpu.make_async_copy
-    counts = [copy(halo_count_ref.at[r], count_buf.at[r], sems.at[r]) for r in range(RELS)]
-    sums = [copy(own_sum_ref.at[r], sum_buf.at[r], sems.at[2 + r]) for r in range(RELS)]
-    maps = [copy(w_ref.at[r + 1], w_buf.at[r], sems.at[4 + r]) for r in range(RELS)]
-    first = copy(pre_ref, pre_buf, sems.at[6])
-    for one in (counts[0], sums[0], maps[0], counts[1], sums[1], first, maps[1]):
+    counts = [copy(count_ref.at[r], count_buf.at[r], sems.at[5 + r]) for r in range(RELS)]
+    sums = [copy(own_sum_ref.at[r], sum_buf.at[r], sems.at[r]) for r in range(RELS)]
+    first = copy(pre_ref, pre_buf, sems.at[2])
+    for one in (counts[0], sums[0], counts[1], sums[1], first):
         one.start()
     halo = halo_ref[...]
     parts, leave = [], []
@@ -164,15 +163,16 @@
         total = dot(count_buf[r], halo)
         sums[r].wait()
         mean_buf[r] = ((sum_buf[r] + total) * (1.0 / FAN)).astype(BF16)
-        leave.append(copy(mean_buf.at[r], means_ref.at[r], sems.at[7 + r]))
+        leave.append(copy(mean_buf.at[r], means_ref.at[r], sems.at[3 + r]))
         leave[r].start()
-        maps[r].wait()
-        parts.append(dot(mean_buf[r], w_buf[r]))
+        parts.append(dot(mean_buf[r], w_ref[r + 1]))
     first.wait()
-    embed = (pre_buf[...] + parts[0] + parts[1]).astype(BF16)
-    embed_ref[...] = embed
-    picked = dot(chosen_rows(neg_ids_ref), embed)[:NEG_DEV]
-    picked_ref[...] = jnp.broadcast_to(picked[None], (CHIPS, NEG_DEV, H)).astype(BF16)
+    preact = pre_buf[...] + parts[0] + parts[1]
+    pre_buf[...] = preact
+    for i in range(NEG_DEV):
+        row_buf[i : i + 1, :] = pre_buf[pl.ds(neg_ids_ref[i], 1), :]
+    picked_ref[...] = jnp.broadcast_to(row_buf[...][None], (CHIPS, NEG_DEV, H)).astype(BF16)
+    embed_ref[...] = preact.astype(BF16)
     for one in leave:
         one.wait()
 
@@ -197,7 +197,11 @@
     return note
 
 
-def positive_body(count_ref, embed_ref, ends_ref, features_ref, means_ref, grad_ref, note_ref, sources_ref, spread_ref, pairs_ref, sigmoid_ref, softplus_ref):
+def positive_body(count_ref, embed_ref, ends_ref, features_ref, means_ref, grad_ref, note_ref, sources_ref, spread_ref, pairs_ref, sigmoid_ref, softplus_ref, own_buf, mean_buf, sems):
+    fetch_own = pltpu.make_async_copy(features_ref, own_buf, sems.at[0])
+    fetch_means = pltpu.make_async_copy(means_ref, mean_buf, sems.at[1])
+    fetch_own.start()
+    fetch_means.start()
     embed = embed_ref[...]
     scores = lax.dot_general(embed, embed, NT, preferred_element_type=F32)
     sigmoid, softplus = soft_parts(-scores)
@@ -205,9 +209,6 @@
     softplus_ref[...] = softplus
     pairs_ref[...] = jnp.zeros((NODE_DEV, NODE_DEV), F32)
     node = lax.broadcasted_iota(jnp.int32, (NODE_DEV, TILE), 0)
-    widest = largest(features_ref[...].astype(F32))
-    for r in range(RELS):
-        widest = jnp.maximum(widest, largest(means_ref[r].astype(F32)))
     tiles = count_ref[0]
 
     def group(step, _):
@@ -233,6 +234,11 @@
     high, low = split_two(-((pairs + pairs.T) * sigmoid_ref[...]))
     base = dot(high, embed) + dot(low, embed)
     grad_ref[...] = base
+    fetch_own.wait()
+    fetch_means.wait()
+    widest = largest(own_buf[...].astype(F32))
+    for r in range(RELS):
+        widest = jnp.maximum(widest, largest(mean_buf[r].astype(F32)))
     count = tiles.astype(F32)
     known = widest * NODE_DEV * largest(base)
     note_ref[...] = notes_of((loss, count, 0.0, known, widest * TILE * count, NEG_DEV * widest, 0.0))
@@ -391,16 +397,16 @@
     means, embed, picked = call(
         layer_body,
         [(two, BF16, BY_HAND), (square, BF16), hbm((CHIPS, NEG_DEV, H), BF16)],
-        [smem(), BY_HAND, vmem(), BY_HAND, BY_HAND, BY_HAND],
-        [pltpu.VMEM(two, BF16), pltpu.VMEM(two, F32), pltpu.VMEM(two, BF16), pltpu.VMEM(square, F32), pltpu.VMEM(two, BF16), pltpu.SemaphoreType.DMA((9,))],
+        [smem(), BY_HAND, vmem(), BY_HAND, BY_HAND, vmem()],
+        [pltpu.VMEM(two, BF16), pltpu.VMEM(two, F32), pltpu.VMEM(square, F32), pltpu.VMEM(two, BF16), pltpu.VMEM((NEG_DEV, H), F32), pltpu.SemaphoreType.DMA((7,))],
         (neg_ids, halo_count, incoming.reshape(512, H), own_sum, pre, weights),
     )
     near_rows = swap(picked, FAR).reshape(square)
     base, note, sources, spread = call(
         positive_body,
         [hbm(square, F32), ((8, 128), F32), ((NODE_DEV, 128), F32), ((NODE_DEV, 2 * H), BF16)],
-        [smem(), vmem(), FROM_HBM, FROM_HBM, FROM_HBM],
-        [pltpu.VMEM(square, F32)] * 3,
+        [smem(), vmem(), FROM_HBM, BY_HAND, BY_HAND],
+        [pltpu.VMEM(square, F32)] * 3 + [pltpu.VMEM(square, BF16), pltpu.VMEM(two, BF16), pltpu.SemaphoreType.DMA((2,))],
         (tile_count, embed, edge_ends, features, means),
     )
     near_rows, note = lax.optimization_barrier((near_rows, note))

time: 132 us -> 132 us (level)
  no operation moved by 1% of the time
where the time goes in v4:
time: 132 us
  blocking collectives  37.9 us (29%)
  Pallas kernels  33.7 us (26%)
  starting transfers between devices  29 us (22%)
  waiting for transfers between devices  25.7 us (19%)
  other arithmetic  2.64 us (2%)
  local copies, waits for them, and re-layouts  1.47 us (1%)
  between operations  1.47 us (1%)
    all_to_all x2, blocking collectives, swap(): return lax.all_to_all(x, axes, split_axis=0, concat_axis=0, tiled=True)  37.9 us
    pallas_call x12, Pallas kernels, call(): pl.pallas_call(body, out_shape=made, grid=(1,), in_specs=ins, out_specs=b...  31.2 us
    all_to_all x3, waiting for transfers between devices, swap(): return lax.all_to_all(x, axes, split_axis=0, concat_axis=0, tiled=True)  24.9 us
    all_to_all x3, starting transfers between devices, swap(): return lax.all_to_all(x, axes, split_axis=0, concat_axis=0, tiled=True)  20.8 us
    ppermute x7, starting transfers between devices, core_swap(): return lax.ppermute(x, 'dom_3', [(0, 1), (1, 0)])  8.19 us
  transfers between devices with their start and end apart: 10, of which 4 were waited for; matrix products, arithmetic and copies ran while one was open for 2% of the time, Pallas kernels for 14%

profile of v4, /device:TPU:1, one launch (start us, length us, event | category | flops | bytes accessed | tf_op | source)
XLA Modules:
  0.0 131.9 jit_solution(3144541356831446958)
XLA Ops:
  0.6 2.5 %shard_map.95 = bf16[128,4,512]{2,1,0:T(4,128)(2,1)} custom-call(s32[4,128]{1,0:T(4,128)} %bitcast.16, bf16[512,512]{1,0:T(8,128)(2,1)} %features_ref.7), custom_call_target="tpu_custom_call" | custom-call | tf_op jit(solution)/shard_map/pallas_call | solution.py:92
  3.1 11.5 %all-to-all-start = ((bf16[128,4,512]{2,1,0:T(4,128)(2,1)}), bf16[128,4,512]{2,1,0:T(4,128)(2,1)S(1)}, u32[]{:S(2)}, u32[]{:S(2)}) async-start(bf16[128,4,512]{2,1,0:T(4,128)(2,1)} %shard_map.95), calls=%async_computation | async-start | bytes 1048576 | tf_op jit(solution)/shard_map/all_to_all | solution.py:36
  14.8 7.2 %shard_map.94 = (bf16[2,512,512]{2,1,0:T(8,128)(2,1)}, f32[2,512,512]{2,1,0:T(8,128)}, f32[512,512]{1,0:T(8,128)}) custom-call(bf16[512,512]{1,0:T(8,128)(2,1)} %features_ref.7, bf16[3,512,512]{2,1,0:T(8,128)(2,1)} %w_ref.3, s32[512,16]{1,0:T(8,128)S(1)} %copy.12.nbr_ref), custom_call_target="tpu_custom_call" | custom-call | tf_op jit(solution)/shard_map/pallas_call | solution.py:92
  22.0 6.3 %all-to-all-done = bf16[128,4,512]{2,1,0:T(4,128)(2,1)S(1)} async-done(((bf16[128,4,512]{2,1,0:T(4,128)(2,1)}), bf16[128,4,512]{2,1,0:T(4,128)(2,1)S(1)}, u32[]{:S(2)}, u32[]{:S(2)}) %all-to-all-start) | async-done | bytes 524320 | tf_op jit(solution)/shard_map/all_to_all | solution.py:36
  28.4 4.8 %shard_map.96 = (bf16[2,512,512]{2,1,0:T(8,128)(2,1)}, bf16[512,512]{1,0:T(8,128)(2,1)S(1)}, bf16[64,8,512]{2,1,0:T(8,128)(2,1)}) custom-call(s32[8]{0:T(128)S(1)} %copy-done.2, bf16[2,512,512]{2,1,0:T(8,128)(2,1)} %get-tuple-element.44.count_ref, bf16[512,512]{1,0:T(8,128)(2,1)S(1)} %reshape.29.halo_ref, f32[2,512,512]{2,1,0:T(8,128)} %get-tuple-element.46.own_sum_ref, ...), custom_call_target="tpu_custom_call" | custom-call | tf_op jit(solution)/shard_map/pallas_call | solution.py:92
  33.2 4.6 %all-to-all-start.1 = ((bf16[64,8,512]{2,1,0:T(8,128)(2,1)}), bf16[64,8,512]{2,1,0:T(8,128)(2,1)S(1)}, u32[]{:S(2)}, u32[]{:S(2)}) async-start(bf16[64,8,512]{2,1,0:T(8,128)(2,1)} %get-tuple-element.49), calls=%async_computation.1 | async-start | bytes 1048576 | tf_op jit(solution)/shard_map/all_to_all | solution.py:36
  38.5 4.4 %shard_map.97 = (f32[512,512]{1,0:T(8,128)}, f32[8,128]{1,0:T(8,128)S(1)}, f32[512,128]{1,0:T(8,128)S(1)}, bf16[512,1024]{1,0:T(8,128)(2,1)S(1)}) custom-call(s32[1]{0:T(128)S(6)} %copy.14.count_ref, bf16[512,512]{1,0:T(8,128)(2,1)S(1)} %get-tuple-element.48.embed_ref, s32[16,2,256]{2,1,0:T(2,128)} %ends_ref.1, bf16[512,512]{1,0:T(8,128)(2,1)} %features_ref.7, ...), custom_call_target="tpu_custom_call" | custom-call | tf_op jit(solution)/shard_map/pallas_call | solution.py:92
  42.9 6.8 %all-to-all-done.1 = bf16[64,8,512]{2,1,0:T(8,128)(2,1)S(1)} async-done(((bf16[64,8,512]{2,1,0:T(8,128)(2,1)}), bf16[64,8,512]{2,1,0:T(8,128)(2,1)S(1)}, u32[]{:S(2)}, u32[]{:S(2)}) %all-to-all-start.1) | async-done | bytes 524320 | tf_op jit(solution)/shard_map/all_to_all | solution.py:36
  49.7 2.6 %collective-permute-start = (bf16[512,512]{1,0:T(8,128)(2,1)S(1)}, bf16[512,512]{1,0:T(8,128)(2,1)S(1)}, u32[]{:S(2)}, u32[]{:S(2)}) collective-permute-start(bf16[512,512]{1,0:T(8,128)(2,1)S(1)} %bitcast.10), channel_id=1, source_target_pairs={{0,1},{1,0},{2,3},{3,2},{4,5},{5,4},{6,7},{7,6},{8,9},{9,8},{10,11... | collective-permute-start | bytes 1572872 | tf_op jit(solution)/shard_map/ppermute | solution.py:40
  52.2 1.8 %shard_map.98 = (bf16[512,512]{1,0:T(8,128)(2,1)S(1)}, f32[512,512]{1,0:T(8,128)S(1)}, f32[8,128]{1,0:T(8,128)S(1)}) custom-call(bf16[512,512]{1,0:T(8,128)(2,1)S(1)} %get-tuple-element.48.embed_ref, bf16[512,512]{1,0:T(8,128)(2,1)S(1)} %bitcast.11, bf16[512,1024]{1,0:T(8,128)(2,1)S(1)} %get-tuple-element.53.spread_ref, ...), custom_call_target="tpu_custom_call" | custom-call | tf_op jit(solution)/shard_map/pallas_call | solution.py:92
  54.0 1.8 %shard_map.99 = (bf16[512,512]{1,0:T(8,128)(2,1)S(1)}, bf16[512,512]{1,0:T(8,128)(2,1)S(1)}, f32[8,128]{1,0:T(8,128)S(1)}) custom-call(bf16[512,512]{1,0:T(8,128)(2,1)S(1)} %get-tuple-element.48.embed_ref, bf16[512,512]{1,0:T(8,128)(2,1)S(1)} %collective-permute-done.rows_ref, bf16[512,1024]{1,0:T(8,128)(2,1)S(1)} %get-tuple-element.53.spread_ref, ...), custom_call_target="tpu_custom_call" | custom-call | tf_op jit(solution)/shard_map/pallas_call | solution.py:92
  56.0 0.4 collective-permute-start.2
  56.4 1.9 %shard_map.100.grad_ref = f32[512,512]{1,0:T(8,128)S(1)} custom-call(bf16[512,512]{1,0:T(8,128)(2,1)S(1)} %get-tuple-element.59.near_weight_ref, bf16[512,512]{1,0:T(8,128)(2,1)S(1)} %bitcast.12, bf16[512,512]{1,0:T(8,128)(2,1)S(1)} %get-tuple-element.60.weight_ref, bf16[512,512]{1,0:T(8,128)(2,1)S(1)} %collective-permute-done.rows_ref, ...), custom_call_target="tpu_custom_call" | custom-call | tf_op jit(solution)/shard_map/pallas_call | solution.py:92
  58.3 1.1 shard_map.101
  59.5 2.9 %shard_map.102 = (f32[1536,256]{1,0:T(8,128)S(1)}, f32[1536,256]{1,0:T(8,128)S(1)}, bf16[16,1536]{1,0:T(8,128)(2,1)S(1)}) custom-call(s32[8]{0:T(128)S(1)} %copy-done.2, s32[1]{0:T(128)} %bitcast.core_ref, f32[512,512]{1,0:T(8,128)S(1)} %shard_map.100.grad_ref, bf16[512,512]{1,0:T(8,128)(2,1)} %features_ref.7, bf16[2,512,512]{2,1,0:T(8,128)(2,1)} %get-tuple-element.50.means_ref), custom_call_target="tpu_custom_call" | custom-call | tf_op jit(solution)/shard_map/pallas_call | solution.py:92
  62.4 1.1 copy-done.1
  63.5 0.3 collective-permute-start.3
  63.8 4.6 %all-to-all-start.2 = ((bf16[64,8,640]{2,1,0:T(8,128)(2,1)}), bf16[64,8,640]{2,1,0:T(8,128)(2,1)S(1)}, u32[]{:S(2)}, u32[]{:S(2)}) async-start(bf16[64,8,640]{2,1,0:T(8,128)(2,1)} %shard_map.101), calls=%async_computation.2 | async-start | bytes 1310720 | tf_op jit(solution)/shard_map/all_to_all | solution.py:36
  68.4 0.3 collective-permute-start.4
  68.7 2.1 %add.3.known_ref = f32[1536,256]{1,0:T(8,128)S(1)} add(f32[1536,256]{1,0:T(8,128)} %copy-done.1, f32[1536,256]{1,0:T(8,128)} %collective-permute-done.3) | non-fusion elementwise | flops 393216 | bytes 4718592 | tf_op jit(solution)/shard_map/add | solution.py:455
  70.8 11.8 %all-to-all-done.2.arrived_ref = bf16[64,8,640]{2,1,0:T(8,128)(2,1)S(1)} async-done(((bf16[64,8,640]{2,1,0:T(8,128)(2,1)}), bf16[64,8,640]{2,1,0:T(8,128)(2,1)S(1)}, u32[]{:S(2)}, u32[]{:S(2)}) %all-to-all-start.2) | async-done | bytes 655392 | tf_op jit(solution)/shard_map/all_to_all | solution.py:36
  82.7 0.7 shard_map.103
  83.4 1.6 %collective-permute-start.5 = (bf16[16,256]{1,0:T(8,128)(2,1)S(1)}, bf16[16,256]{1,0:T(8,128)(2,1)S(1)}, u32[]{:S(2)}, u32[]{:S(2)}) collective-permute-start(bf16[16,256]{1,0:T(8,128)(2,1)S(1)} %get-tuple-element.74), channel_id=1, source_target_pairs={{0,1},{1,0},{2,3},{3,2},{4,5},{5,4},{6,7},{7,6},{8,9},{9,8},{10,11... | collective-permute-start | bytes 24584 | tf_op jit(solution)/shard_map/ppermute | solution.py:40
  85.0 0.8 collective-permute-done.5.other_row_ref
  85.8 0.6 shard_map.104
  86.5 19.4 %all_to_all.25 = f16[64,24,256]{2,1,0:T(8,128)(2,1)S(1)} all-to-all(f16[64,24,256]{2,1,0:T(8,128)(2,1)S(1)} %bitcast.14), channel_id=1, replica_groups=mesh['dom_0'=4,'dom_1'=4,'dom_2'=4,'dom_3'=2] {'dom_0','dom_1','dom_2'}, dimensions={0} | all-to-all | bytes 1572864 | tf_op jit(solution)/shard_map/all_to_all | solution.py:36
  106.1 18.5 %all_to_all.26 = f16[64,24,256]{2,1,0:T(8,128)(2,1)S(1)} all-to-all(f16[64,24,256]{2,1,0:T(8,128)(2,1)S(1)} %broadcast_in_dim.3), channel_id=1, replica_groups=mesh['dom_0'=4,'dom_1'=4,'dom_2'=4,'dom_3'=2] {'dom_0','dom_1','dom_2'}, dimensions={0} | all-to-all | bytes 1572864 | tf_op jit(solution)/shard_map/all_to_all | solution.py:36
  124.6 2.9 %collective-permute-start.6 = (f16[1536,256]{1,0:T(8,128)(2,1)S(1)}, f16[1536,256]{1,0:T(8,128)(2,1)S(1)}, u32[]{:S(2)}, u32[]{:S(2)}) collective-permute-start(f16[1536,256]{1,0:T(8,128)(2,1)S(1)} %bitcast.13), channel_id=1, source_target_pairs={{0,1},{1,0},{2,3},{3,2},{4,5},{5,4},{6,7},{7,6},{8,9},{9,8},{10,11... | collective-permute-start | bytes 2359304 | tf_op jit(solution)/shard_map/ppermute | solution.py:40
  127.5 1.5 %shard_map.107 = bf16[512,512]{1,0:T(8,128)(2,1)} custom-call(s32[8]{0:T(128)S(1)} %copy-done.2, f32[8,512]{1,0:T(8,128)S(1)} %get-tuple-element.82.total_ref, f32[512,512]{1,0:T(8,128)S(1)} %shard_map.100.grad_ref), custom_call_target="tpu_custom_call" | custom-call | tf_op jit(solution)/shard_map/pallas_call | solution.py:92
  129.0 0.2 bitcast_convert_fusion.half_ref
  129.2 1.3 shard_map.105
  130.6 1.3 shard_map.106
  (21 shorter events, 0.8 us)
Async XLA Ops:
  0.6 14.0 %copy-start.3 = (s32[512,2,8]{0,2,1:T(8,128)S(1)}, s32[512,2,8]{0,2,1:T(8,128)}, u32[]{:S(2)}) copy-start(s32[512,2,8]{0,2,1:T(8,128)} %param.10) | copy-start | bytes 98308
  3.1 25.1 %all-to-all-start = ((bf16[128,4,512]{2,1,0:T(4,128)(2,1)}), bf16[128,4,512]{2,1,0:T(4,128)(2,1)S(1)}, u32[]{:S(2)}, u32[]{:S(2)}) async-start(bf16[128,4,512]{2,1,0:T(4,128)(2,1)} %shard_map.95), calls=%async_computation | async-start | bytes 1048576 | tf_op jit(solution)/shard_map/all_to_all | solution.py:36
  14.8 13.6 %copy-start = (bf16[3,512,512]{2,1,0:T(8,128)(2,1)S(1)}, bf16[3,512,512]{2,1,0:T(8,128)(2,1)}, u32[]{:S(2)}) copy-start(bf16[3,512,512]{2,1,0:T(8,128)(2,1)} %w_ref.3) | copy-start | bytes 4718596
  14.8 13.6 %copy-start.2 = (s32[8]{0:T(128)S(1)}, s32[8]{0:T(128)}, u32[]{:S(2)}) copy-start(s32[8]{0:T(128)} %neg_ids_ref.7) | copy-start | bytes 100
  33.2 16.5 %all-to-all-start.1 = ((bf16[64,8,512]{2,1,0:T(8,128)(2,1)}), bf16[64,8,512]{2,1,0:T(8,128)(2,1)S(1)}, u32[]{:S(2)}, u32[]{:S(2)}) async-start(bf16[64,8,512]{2,1,0:T(8,128)(2,1)} %get-tuple-element.49), calls=%async_computation.1 | async-start | bytes 1048576 | tf_op jit(solution)/shard_map/all_to_all | solution.py:36
  49.7 4.4 %collective-permute-start = (bf16[512,512]{1,0:T(8,128)(2,1)S(1)}, bf16[512,512]{1,0:T(8,128)(2,1)S(1)}, u32[]{:S(2)}, u32[]{:S(2)}) collective-permute-start(bf16[512,512]{1,0:T(8,128)(2,1)S(1)} %bitcast.10), channel_id=1, source_target_pairs={{0,1},{1,0},{2,3},{3,2},{4,5},{5,4},{6,7},{7,6},{8,9},{9,8},{10,11... | collective-permute-start | bytes 1572872 | tf_op jit(solution)/shard_map/ppermute | solution.py:40
  55.9 2.5 %collective-permute-start.1 = (bf16[512,512]{1,0:T(8,128)(2,1)S(1)}, bf16[512,512]{1,0:T(8,128)(2,1)S(1)}, u32[]{:S(2)}, u32[]{:S(2)}) collective-permute-start(bf16[512,512]{1,0:T(8,128)(2,1)S(1)} %get-tuple-element.58), channel_id=1, source_target_pairs={{0,1},{1,0},{2,3},{3,2},{4,5},{5,4},{6,7},{7,6},{8,9},{9,8},{10,11... | collective-permute-start | bytes 1572872 | tf_op jit(solution)/shard_map/ppermute | solution.py:40
  56.0 2.4 %collective-permute-start.2 = (f32[8,128]{1,0:T(8,128)S(1)}, f32[8,128]{1,0:T(8,128)S(1)}, u32[]{:S(2)}, u32[]{:S(2)}) collective-permute-start(f32[8,128]{1,0:T(8,128)S(1)} %get-tuple-element.63.own_note_ref), channel_id=1, source_target_pairs={{0,1},{1,0},{2,3},{3,2},{4,5},{5,4},{6,7},{7,6},{8,9},{9,8},{10,11... | collective-permute-start | bytes 12296 | tf_op jit(solution)/shard_map/ppermute | solution.py:40
  62.3 1.1 copy-start.1
  63.5 5.2 %collective-permute-start.3 = (f32[1536,256]{1,0:T(8,128)S(1)}, f32[1536,256]{1,0:T(8,128)}, u32[]{:S(2)}, u32[]{:S(2)}) collective-permute-start(f32[1536,256]{1,0:T(8,128)S(1)} %get-tuple-element.68), channel_id=1, source_target_pairs={{0,1},{1,0},{2,3},{3,2},{4,5},{5,4},{6,7},{7,6},{8,9},{9,8},{10,11... | collective-permute-start | bytes 4718600 | tf_op jit(solution)/shard_map/ppermute | solution.py:40
  63.8 18.9 %all-to-all-start.2 = ((bf16[64,8,640]{2,1,0:T(8,128)(2,1)}), bf16[64,8,640]{2,1,0:T(8,128)(2,1)S(1)}, u32[]{:S(2)}, u32[]{:S(2)}) async-start(bf16[64,8,640]{2,1,0:T(8,128)(2,1)} %shard_map.101), calls=%async_computation.2 | async-start | bytes 1310720 | tf_op jit(solution)/shard_map/all_to_all | solution.py:36
  68.4 2.4 %collective-permute-start.4 = (bf16[16,1536]{1,0:T(8,128)(2,1)S(1)}, bf16[16,1536]{1,0:T(8,128)(2,1)S(1)}, u32[]{:S(2)}, u32[]{:S(2)}) collective-permute-start(bf16[16,1536]{1,0:T(8,128)(2,1)S(1)} %get-tuple-element.69.own_chosen_ref), channel_id=1, source_target_pairs={{0,1},{1,0},{2,3},{3,2},{4,5},{5,4},{6,7},{7,6},{8,9},{9,8},{10,11... | collective-permute-start | bytes 147464 | tf_op jit(solution)/shard_map/ppermute | solution.py:40
  83.4 2.4 %collective-permute-start.5 = (bf16[16,256]{1,0:T(8,128)(2,1)S(1)}, bf16[16,256]{1,0:T(8,128)(2,1)S(1)}, u32[]{:S(2)}, u32[]{:S(2)}) collective-permute-start(bf16[16,256]{1,0:T(8,128)(2,1)S(1)} %get-tuple-element.74), channel_id=1, source_target_pairs={{0,1},{1,0},{2,3},{3,2},{4,5},{5,4},{6,7},{7,6},{8,9},{9,8},{10,11... | collective-permute-start | bytes 24584 | tf_op jit(solution)/shard_map/ppermute | solution.py:40
  124.6 5.9 %collective-permute-start.6 = (f16[1536,256]{1,0:T(8,128)(2,1)S(1)}, f16[1536,256]{1,0:T(8,128)(2,1)S(1)}, u32[]{:S(2)}, u32[]{:S(2)}) collective-permute-start(f16[1536,256]{1,0:T(8,128)(2,1)S(1)} %bitcast.13), channel_id=1, source_target_pairs={{0,1},{1,0},{2,3},{3,2},{4,5},{5,4},{6,7},{7,6},{8,9},{9,8},{10,11... | collective-permute-start | bytes 2359304 | tf_op jit(solution)/shard_map/ppermute | solution.py:40

commit v5 on v4

--- a/solution.py
+++ b/solution.py
@@ -149,25 +149,17 @@
         one.wait()
 
 
-def layer_body(neg_ids_ref, count_ref, halo_ref, own_sum_ref, pre_ref, w_ref, means_ref, embed_ref, picked_ref, count_buf, sum_buf, pre_buf, mean_buf, row_buf, sems):
-    copy = pltpu.make_async_copy
-    counts = [copy(count_ref.at[r], count_buf.at[r], sems.at[5 + r]) for r in range(RELS)]
-    sums = [copy(own_sum_ref.at[r], sum_buf.at[r], sems.at[r]) for r in range(RELS)]
-    first = copy(pre_ref, pre_buf, sems.at[2])
-    for one in (counts[0], sums[0], counts[1], sums[1], first):
+def layer_body(neg_ids_ref, count_ref, halo_ref, own_sum_ref, pre_ref, w_ref, means_ref, embed_ref, picked_ref, pre_buf, mean_buf, row_buf, sems):
+    halo = halo_ref[...]
+    preact = pre_ref[...]
+    for r in range(RELS):
+        total = own_sum_ref[r] + dot(count_ref[r], halo)
+        mean = (total * (1.0 / FAN)).astype(BF16)
+        mean_buf[r] = mean
+        preact = preact + dot(mean, w_ref[r + 1])
+    leave = [pltpu.make_async_copy(mean_buf.at[r], means_ref.at[r], sems.at[r]) for r in range(RELS)]
+    for one in leave:
         one.start()
-    halo = halo_ref[...]
-    parts, leave = [], []
-    for r in range(RELS):
-        counts[r].wait()
-        total = dot(count_buf[r], halo)
-        sums[r].wait()
-        mean_buf[r] = ((sum_buf[r] + total) * (1.0 / FAN)).astype(BF16)
-        leave.append(copy(mean_buf.at[r], means_ref.at[r], sems.at[3 + r]))
-        leave[r].start()
-        parts.append(dot(mean_buf[r], w_ref[r + 1]))
-    first.wait()
-    preact = pre_buf[...] + parts[0] + parts[1]
     pre_buf[...] = preact
     for i in range(NEG_DEV):
         row_buf[i : i + 1, :] = pre_buf[pl.ds(neg_ids_ref[i], 1), :]
@@ -397,8 +389,8 @@
     means, embed, picked = call(
         layer_body,
         [(two, BF16, BY_HAND), (square, BF16), hbm((CHIPS, NEG_DEV, H), BF16)],
-        [smem(), BY_HAND, vmem(), BY_HAND, BY_HAND, vmem()],
-        [pltpu.VMEM(two, BF16), pltpu.VMEM(two, F32), pltpu.VMEM(square, F32), pltpu.VMEM(two, BF16), pltpu.VMEM((NEG_DEV, H), F32), pltpu.SemaphoreType.DMA((7,))],
+        [smem(), FROM_HBM, vmem(), FROM_HBM, FROM_HBM, vmem()],
+        [pltpu.VMEM(square, F32), pltpu.VMEM(two, BF16), pltpu.VMEM((NEG_DEV, H), F32), pltpu.SemaphoreType.DMA((RELS,))],
         (neg_ids, halo_count, incoming.reshape(512, H), own_sum, pre, weights),
     )
     near_rows = swap(picked, FAR).reshape(square)

time: 132 us -> 133 us (level)
  no operation moved by 1% of the time
where the time goes in v5:
time: 133 us; the launch traced here: 132 us
  blocking collectives  37.9 us (28%)
  Pallas kernels  33.9 us (25%)
  starting transfers between devices  29 us (22%)
  waiting for transfers between devices  25.7 us (19%)
  other arithmetic  2.64 us (2%)
  local copies, waits for them, and re-layouts  1.47 us (1%)
  between operations  1.47 us (1%)
    all_to_all x2, blocking collectives, swap(): return lax.all_to_all(x, axes, split_axis=0, concat_axis=0, tiled=True)  37.9 us
    pallas_call x12, Pallas kernels, call(): pl.pallas_call(body, out_shape=made, grid=(1,), in_specs=ins, out_specs=b...  31.4 us
    all_to_all x3, waiting for transfers between devices, swap(): return lax.all_to_all(x, axes, split_axis=0, concat_axis=0, tiled=True)  24.9 us
    all_to_all x3, starting transfers between devices, swap(): return lax.all_to_all(x, axes, split_axis=0, concat_axis=0, tiled=True)  20.8 us
    ppermute x7, starting transfers between devices, core_swap(): return lax.ppermute(x, 'dom_3', [(0, 1), (1, 0)])  8.19 us
  transfers between devices with their start and end apart: 10, of which 4 were waited for; matrix products, arithmetic and copies ran while one was open for 2% of the time, Pallas kernels for 14%

profile of v5, /device:TPU:1, one launch (start us, length us, event | category | flops | bytes accessed | tf_op | source)
XLA Modules:
  0.0 132.1 jit_solution(14074698858208739818)
XLA Ops:
  0.6 2.5 %shard_map.95 = bf16[128,4,512]{2,1,0:T(4,128)(2,1)} custom-call(s32[4,128]{1,0:T(4,128)} %bitcast.16, bf16[512,512]{1,0:T(8,128)(2,1)} %features_ref.7), custom_call_target="tpu_custom_call" | custom-call | tf_op jit(solution)/shard_map/pallas_call | solution.py:92
  3.1 11.5 %all-to-all-start = ((bf16[128,4,512]{2,1,0:T(4,128)(2,1)}), bf16[128,4,512]{2,1,0:T(4,128)(2,1)S(1)}, u32[]{:S(2)}, u32[]{:S(2)}) async-start(bf16[128,4,512]{2,1,0:T(4,128)(2,1)} %shard_map.95), calls=%async_computation | async-start | bytes 1048576 | tf_op jit(solution)/shard_map/all_to_all | solution.py:36
  14.8 7.2 %shard_map.94 = (bf16[2,512,512]{2,1,0:T(8,128)(2,1)}, f32[2,512,512]{2,1,0:T(8,128)}, f32[512,512]{1,0:T(8,128)}) custom-call(bf16[512,512]{1,0:T(8,128)(2,1)} %features_ref.7, bf16[3,512,512]{2,1,0:T(8,128)(2,1)} %w_ref.3, s32[512,16]{1,0:T(8,128)S(1)} %copy.12.nbr_ref), custom_call_target="tpu_custom_call" | custom-call | tf_op jit(solution)/shard_map/pallas_call | solution.py:92
  22.0 6.3 %all-to-all-done = bf16[128,4,512]{2,1,0:T(4,128)(2,1)S(1)} async-done(((bf16[128,4,512]{2,1,0:T(4,128)(2,1)}), bf16[128,4,512]{2,1,0:T(4,128)(2,1)S(1)}, u32[]{:S(2)}, u32[]{:S(2)}) %all-to-all-start) | async-done | bytes 524320 | tf_op jit(solution)/shard_map/all_to_all | solution.py:36
  28.4 5.0 %shard_map.96 = (bf16[2,512,512]{2,1,0:T(8,128)(2,1)}, bf16[512,512]{1,0:T(8,128)(2,1)S(1)}, bf16[64,8,512]{2,1,0:T(8,128)(2,1)}) custom-call(s32[8]{0:T(128)S(1)} %copy-done.2, bf16[2,512,512]{2,1,0:T(8,128)(2,1)} %get-tuple-element.44.count_ref, bf16[512,512]{1,0:T(8,128)(2,1)S(1)} %reshape.29.halo_ref, f32[2,512,512]{2,1,0:T(8,128)} %get-tuple-element.46.own_sum_ref, ...), custom_call_target="tpu_custom_call" | custom-call | tf_op jit(solution)/shard_map/pallas_call | solution.py:92
  33.4 4.6 %all-to-all-start.1 = ((bf16[64,8,512]{2,1,0:T(8,128)(2,1)}), bf16[64,8,512]{2,1,0:T(8,128)(2,1)S(1)}, u32[]{:S(2)}, u32[]{:S(2)}) async-start(bf16[64,8,512]{2,1,0:T(8,128)(2,1)} %get-tuple-element.49), calls=%async_computation.1 | async-start | bytes 1048576 | tf_op jit(solution)/shard_map/all_to_all | solution.py:36
  38.7 4.4 %shard_map.97 = (f32[512,512]{1,0:T(8,128)}, f32[8,128]{1,0:T(8,128)S(1)}, f32[512,128]{1,0:T(8,128)S(1)}, bf16[512,1024]{1,0:T(8,128)(2,1)S(1)}) custom-call(s32[1]{0:T(128)S(6)} %copy.14.count_ref, bf16[512,512]{1,0:T(8,128)(2,1)S(1)} %get-tuple-element.48.embed_ref, s32[16,2,256]{2,1,0:T(2,128)} %ends_ref.1, bf16[512,512]{1,0:T(8,128)(2,1)} %features_ref.7, ...), custom_call_target="tpu_custom_call" | custom-call | tf_op jit(solution)/shard_map/pallas_call | solution.py:92
  43.1 6.8 %all-to-all-done.1 = bf16[64,8,512]{2,1,0:T(8,128)(2,1)S(1)} async-done(((bf16[64,8,512]{2,1,0:T(8,128)(2,1)}), bf16[64,8,512]{2,1,0:T(8,128)(2,1)S(1)}, u32[]{:S(2)}, u32[]{:S(2)}) %all-to-all-start.1) | async-done | bytes 524320 | tf_op jit(solution)/shard_map/all_to_all | solution.py:36
  49.9 2.6 %collective-permute-start = (bf16[512,512]{1,0:T(8,128)(2,1)S(1)}, bf16[512,512]{1,0:T(8,128)(2,1)S(1)}, u32[]{:S(2)}, u32[]{:S(2)}) collective-permute-start(bf16[512,512]{1,0:T(8,128)(2,1)S(1)} %bitcast.10), channel_id=1, source_target_pairs={{0,1},{1,0},{2,3},{3,2},{4,5},{5,4},{6,7},{7,6},{8,9},{9,8},{10,11... | collective-permute-start | bytes 1572872 | tf_op jit(solution)/shard_map/ppermute | solution.py:40
  52.4 1.8 %shard_map.98 = (bf16[512,512]{1,0:T(8,128)(2,1)S(1)}, f32[512,512]{1,0:T(8,128)S(1)}, f32[8,128]{1,0:T(8,128)S(1)}) custom-call(bf16[512,512]{1,0:T(8,128)(2,1)S(1)} %get-tuple-element.48.embed_ref, bf16[512,512]{1,0:T(8,128)(2,1)S(1)} %bitcast.11, bf16[512,1024]{1,0:T(8,128)(2,1)S(1)} %get-tuple-element.53.spread_ref, ...), custom_call_target="tpu_custom_call" | custom-call | tf_op jit(solution)/shard_map/pallas_call | solution.py:92
  54.3 1.8 %shard_map.99 = (bf16[512,512]{1,0:T(8,128)(2,1)S(1)}, bf16[512,512]{1,0:T(8,128)(2,1)S(1)}, f32[8,128]{1,0:T(8,128)S(1)}) custom-call(bf16[512,512]{1,0:T(8,128)(2,1)S(1)} %get-tuple-element.48.embed_ref, bf16[512,512]{1,0:T(8,128)(2,1)S(1)} %collective-permute-done.rows_ref, bf16[512,1024]{1,0:T(8,128)(2,1)S(1)} %get-tuple-element.53.spread_ref, ...), custom_call_target="tpu_custom_call" | custom-call | tf_op jit(solution)/shard_map/pallas_call | solution.py:92
  56.2 0.4 collective-permute-start.2
  56.6 1.9 %shard_map.100.grad_ref = f32[512,512]{1,0:T(8,128)S(1)} custom-call(bf16[512,512]{1,0:T(8,128)(2,1)S(1)} %get-tuple-element.59.near_weight_ref, bf16[512,512]{1,0:T(8,128)(2,1)S(1)} %bitcast.12, bf16[512,512]{1,0:T(8,128)(2,1)S(1)} %get-tuple-element.60.weight_ref, bf16[512,512]{1,0:T(8,128)(2,1)S(1)} %collective-permute-done.rows_ref, ...), custom_call_target="tpu_custom_call" | custom-call | tf_op jit(solution)/shard_map/pallas_call | solution.py:92
  58.6 1.1 shard_map.101
  59.7 2.9 %shard_map.102 = (f32[1536,256]{1,0:T(8,128)S(1)}, f32[1536,256]{1,0:T(8,128)S(1)}, bf16[16,1536]{1,0:T(8,128)(2,1)S(1)}) custom-call(s32[8]{0:T(128)S(1)} %copy-done.2, s32[1]{0:T(128)} %bitcast.core_ref, f32[512,512]{1,0:T(8,128)S(1)} %shard_map.100.grad_ref, bf16[512,512]{1,0:T(8,128)(2,1)} %features_ref.7, bf16[2,512,512]{2,1,0:T(8,128)(2,1)} %get-tuple-element.50.means_ref), custom_call_target="tpu_custom_call" | custom-call | tf_op jit(solution)/shard_map/pallas_call | solution.py:92
  62.6 1.1 copy-done.1
  63.7 0.3 collective-permute-start.3
  64.0 4.6 %all-to-all-start.2 = ((bf16[64,8,640]{2,1,0:T(8,128)(2,1)}), bf16[64,8,640]{2,1,0:T(8,128)(2,1)S(1)}, u32[]{:S(2)}, u32[]{:S(2)}) async-start(bf16[64,8,640]{2,1,0:T(8,128)(2,1)} %shard_map.101), calls=%async_computation.2 | async-start | bytes 1310720 | tf_op jit(solution)/shard_map/all_to_all | solution.py:36
  68.6 0.3 collective-permute-start.4
  69.0 2.1 %add.3.known_ref = f32[1536,256]{1,0:T(8,128)S(1)} add(f32[1536,256]{1,0:T(8,128)} %copy-done.1, f32[1536,256]{1,0:T(8,128)} %collective-permute-done.3) | non-fusion elementwise | flops 393216 | bytes 4718592 | tf_op jit(solution)/shard_map/add | solution.py:447
  71.1 11.8 %all-to-all-done.2.arrived_ref = bf16[64,8,640]{2,1,0:T(8,128)(2,1)S(1)} async-done(((bf16[64,8,640]{2,1,0:T(8,128)(2,1)}), bf16[64,8,640]{2,1,0:T(8,128)(2,1)S(1)}, u32[]{:S(2)}, u32[]{:S(2)}) %all-to-all-start.2) | async-done | bytes 655392 | tf_op jit(solution)/shard_map/all_to_all | solution.py:36
  82.9 0.7 shard_map.103
  83.6 1.6 %collective-permute-start.5 = (bf16[16,256]{1,0:T(8,128)(2,1)S(1)}, bf16[16,256]{1,0:T(8,128)(2,1)S(1)}, u32[]{:S(2)}, u32[]{:S(2)}) collective-permute-start(bf16[16,256]{1,0:T(8,128)(2,1)S(1)} %get-tuple-element.74), channel_id=1, source_target_pairs={{0,1},{1,0},{2,3},{3,2},{4,5},{5,4},{6,7},{7,6},{8,9},{9,8},{10,11... | collective-permute-start | bytes 24584 | tf_op jit(solution)/shard_map/ppermute | solution.py:40
  85.2 0.8 collective-permute-done.5.other_row_ref
  86.0 0.6 shard_map.104
  86.7 19.4 %all_to_all.25 = f16[64,24,256]{2,1,0:T(8,128)(2,1)S(1)} all-to-all(f16[64,24,256]{2,1,0:T(8,128)(2,1)S(1)} %bitcast.14), channel_id=1, replica_groups=mesh['dom_0'=4,'dom_1'=4,'dom_2'=4,'dom_3'=2] {'dom_0','dom_1','dom_2'}, dimensions={0} | all-to-all | bytes 1572864 | tf_op jit(solution)/shard_map/all_to_all | solution.py:36
  106.3 18.5 %all_to_all.26 = f16[64,24,256]{2,1,0:T(8,128)(2,1)S(1)} all-to-all(f16[64,24,256]{2,1,0:T(8,128)(2,1)S(1)} %broadcast_in_dim.3), channel_id=1, replica_groups=mesh['dom_0'=4,'dom_1'=4,'dom_2'=4,'dom_3'=2] {'dom_0','dom_1','dom_2'}, dimensions={0} | all-to-all | bytes 1572864 | tf_op jit(solution)/shard_map/all_to_all | solution.py:36
  124.8 2.9 %collective-permute-start.6 = (f16[1536,256]{1,0:T(8,128)(2,1)S(1)}, f16[1536,256]{1,0:T(8,128)(2,1)S(1)}, u32[]{:S(2)}, u32[]{:S(2)}) collective-permute-start(f16[1536,256]{1,0:T(8,128)(2,1)S(1)} %bitcast.13), channel_id=1, source_target_pairs={{0,1},{1,0},{2,3},{3,2},{4,5},{5,4},{6,7},{7,6},{8,9},{9,8},{10,11... | collective-permute-start | bytes 2359304 | tf_op jit(solution)/shard_map/ppermute | solution.py:40
  127.8 1.5 %shard_map.107 = bf16[512,512]{1,0:T(8,128)(2,1)} custom-call(s32[8]{0:T(128)S(1)} %copy-done.2, f32[8,512]{1,0:T(8,128)S(1)} %get-tuple-element.82.total_ref, f32[512,512]{1,0:T(8,128)S(1)} %shard_map.100.grad_ref), custom_call_target="tpu_custom_call" | custom-call | tf_op jit(solution)/shard_map/pallas_call | solution.py:92
  129.2 0.2 bitcast_convert_fusion.half_ref
  129.4 1.3 shard_map.105
  130.8 1.3 shard_map.106
  (21 shorter events, 0.8 us)
Async XLA Ops:
  0.6 14.0 %copy-start.3 = (s32[512,2,8]{0,2,1:T(8,128)S(1)}, s32[512,2,8]{0,2,1:T(8,128)}, u32[]{:S(2)}) copy-start(s32[512,2,8]{0,2,1:T(8,128)} %param.10) | copy-start | bytes 98308
  3.1 25.1 %all-to-all-start = ((bf16[128,4,512]{2,1,0:T(4,128)(2,1)}), bf16[128,4,512]{2,1,0:T(4,128)(2,1)S(1)}, u32[]{:S(2)}, u32[]{:S(2)}) async-start(bf16[128,4,512]{2,1,0:T(4,128)(2,1)} %shard_map.95), calls=%async_computation | async-start | bytes 1048576 | tf_op jit(solution)/shard_map/all_to_all | solution.py:36
  14.8 13.6 %copy-start = (bf16[3,512,512]{2,1,0:T(8,128)(2,1)S(1)}, bf16[3,512,512]{2,1,0:T(8,128)(2,1)}, u32[]{:S(2)}) copy-start(bf16[3,512,512]{2,1,0:T(8,128)(2,1)} %w_ref.3) | copy-start | bytes 4718596
  14.8 13.6 %copy-start.2 = (s32[8]{0:T(128)S(1)}, s32[8]{0:T(128)}, u32[]{:S(2)}) copy-start(s32[8]{0:T(128)} %neg_ids_ref.7) | copy-start | bytes 100
  33.4 16.5 %all-to-all-start.1 = ((bf16[64,8,512]{2,1,0:T(8,128)(2,1)}), bf16[64,8,512]{2,1,0:T(8,128)(2,1)S(1)}, u32[]{:S(2)}, u32[]{:S(2)}) async-start(bf16[64,8,512]{2,1,0:T(8,128)(2,1)} %get-tuple-element.49), calls=%async_computation.1 | async-start | bytes 1048576 | tf_op jit(solution)/shard_map/all_to_all | solution.py:36
  49.9 4.4 %collective-permute-start = (bf16[512,512]{1,0:T(8,128)(2,1)S(1)}, bf16[512,512]{1,0:T(8,128)(2,1)S(1)}, u32[]{:S(2)}, u32[]{:S(2)}) collective-permute-start(bf16[512,512]{1,0:T(8,128)(2,1)S(1)} %bitcast.10), channel_id=1, source_target_pairs={{0,1},{1,0},{2,3},{3,2},{4,5},{5,4},{6,7},{7,6},{8,9},{9,8},{10,11... | collective-permute-start | bytes 1572872 | tf_op jit(solution)/shard_map/ppermute | solution.py:40
  56.1 2.5 %collective-permute-start.1 = (bf16[512,512]{1,0:T(8,128)(2,1)S(1)}, bf16[512,512]{1,0:T(8,128)(2,1)S(1)}, u32[]{:S(2)}, u32[]{:S(2)}) collective-permute-start(bf16[512,512]{1,0:T(8,128)(2,1)S(1)} %get-tuple-element.58), channel_id=1, source_target_pairs={{0,1},{1,0},{2,3},{3,2},{4,5},{5,4},{6,7},{7,6},{8,9},{9,8},{10,11... | collective-permute-start | bytes 1572872 | tf_op jit(solution)/shard_map/ppermute | solution.py:40
  56.2 2.4 %collective-permute-start.2 = (f32[8,128]{1,0:T(8,128)S(1)}, f32[8,128]{1,0:T(8,128)S(1)}, u32[]{:S(2)}, u32[]{:S(2)}) collective-permute-start(f32[8,128]{1,0:T(8,128)S(1)} %get-tuple-element.63.own_note_ref), channel_id=1, source_target_pairs={{0,1},{1,0},{2,3},{3,2},{4,5},{5,4},{6,7},{7,6},{8,9},{9,8},{10,11... | collective-permute-start | bytes 12296 | tf_op jit(solution)/shard_map/ppermute | solution.py:40
  62.6 1.1 copy-start.1
  63.7 5.2 %collective-permute-start.3 = (f32[1536,256]{1,0:T(8,128)S(1)}, f32[1536,256]{1,0:T(8,128)}, u32[]{:S(2)}, u32[]{:S(2)}) collective-permute-start(f32[1536,256]{1,0:T(8,128)S(1)} %get-tuple-element.68), channel_id=1, source_target_pairs={{0,1},{1,0},{2,3},{3,2},{4,5},{5,4},{6,7},{7,6},{8,9},{9,8},{10,11... | collective-permute-start | bytes 4718600 | tf_op jit(solution)/shard_map/ppermute | solution.py:40
  64.0 18.9 %all-to-all-start.2 = ((bf16[64,8,640]{2,1,0:T(8,128)(2,1)}), bf16[64,8,640]{2,1,0:T(8,128)(2,1)S(1)}, u32[]{:S(2)}, u32[]{:S(2)}) async-start(bf16[64,8,640]{2,1,0:T(8,128)(2,1)} %shard_map.101), calls=%async_computation.2 | async-start | bytes 1310720 | tf_op jit(solution)/shard_map/all_to_all | solution.py:36
  68.6 2.4 %collective-permute-start.4 = (bf16[16,1536]{1,0:T(8,128)(2,1)S(1)}, bf16[16,1536]{1,0:T(8,128)(2,1)S(1)}, u32[]{:S(2)}, u32[]{:S(2)}) collective-permute-start(bf16[16,1536]{1,0:T(8,128)(2,1)S(1)} %get-tuple-element.69.own_chosen_ref), channel_id=1, source_target_pairs={{0,1},{1,0},{2,3},{3,2},{4,5},{5,4},{6,7},{7,6},{8,9},{9,8},{10,11... | collective-permute-start | bytes 147464 | tf_op jit(solution)/shard_map/ppermute | solution.py:40
  83.6 2.4 %collective-permute-start.5 = (bf16[16,256]{1,0:T(8,128)(2,1)S(1)}, bf16[16,256]{1,0:T(8,128)(2,1)S(1)}, u32[]{:S(2)}, u32[]{:S(2)}) collective-permute-start(bf16[16,256]{1,0:T(8,128)(2,1)S(1)} %get-tuple-element.74), channel_id=1, source_target_pairs={{0,1},{1,0},{2,3},{3,2},{4,5},{5,4},{6,7},{7,6},{8,9},{9,8},{10,11... | collective-permute-start | bytes 24584 | tf_op jit(solution)/shard_map/ppermute | solution.py:40
  124.8 5.9 %collective-permute-start.6 = (f16[1536,256]{1,0:T(8,128)(2,1)S(1)}, f16[1536,256]{1,0:T(8,128)(2,1)S(1)}, u32[]{:S(2)}, u32[]{:S(2)}) collective-permute-start(f16[1536,256]{1,0:T(8,128)(2,1)S(1)} %bitcast.13), channel_id=1, source_target_pairs={{0,1},{1,0},{2,3},{3,2},{4,5},{5,4},{6,7},{7,6},{8,9},{9,8},{10,11... | collective-permute-start | bytes 2359304 | tf_op jit(solution)/shard_map/ppermute | solution.py:40

commit v6 on v5

--- a/solution.py
+++ b/solution.py
@@ -149,24 +149,18 @@
         one.wait()
 
 
-def layer_body(neg_ids_ref, count_ref, halo_ref, own_sum_ref, pre_ref, w_ref, means_ref, embed_ref, picked_ref, pre_buf, mean_buf, row_buf, sems):
+def layer_body(neg_ids_ref, count_ref, halo_ref, own_sum_ref, pre_ref, w_ref, means_ref, embed_ref, picked_ref):
     halo = halo_ref[...]
     preact = pre_ref[...]
     for r in range(RELS):
         total = own_sum_ref[r] + dot(count_ref[r], halo)
         mean = (total * (1.0 / FAN)).astype(BF16)
-        mean_buf[r] = mean
+        means_ref[r] = mean
         preact = preact + dot(mean, w_ref[r + 1])
-    leave = [pltpu.make_async_copy(mean_buf.at[r], means_ref.at[r], sems.at[r]) for r in range(RELS)]
-    for one in leave:
-        one.start()
-    pre_buf[...] = preact
-    for i in range(NEG_DEV):
-        row_buf[i : i + 1, :] = pre_buf[pl.ds(neg_ids_ref[i], 1), :]
-    picked_ref[...] = jnp.broadcast_to(row_buf[...][None], (CHIPS, NEG_DEV, H)).astype(BF16)
-    embed_ref[...] = preact.astype(BF16)
-    for one in leave:
-        one.wait()
+    embed = preact.astype(BF16)
+    embed_ref[...] = embed
+    picked = dot(chosen_rows(neg_ids_ref), embed)[:NEG_DEV]
+    picked_ref[...] = jnp.broadcast_to(picked[None], (CHIPS, NEG_DEV, H)).astype(BF16)
 
 
 def soft_parts(x):
@@ -388,9 +382,9 @@
     )
     means, embed, picked = call(
         layer_body,
-        [(two, BF16, BY_HAND), (square, BF16), hbm((CHIPS, NEG_DEV, H), BF16)],
+        [hbm(two, BF16), (square, BF16), hbm((CHIPS, NEG_DEV, H), BF16)],
         [smem(), FROM_HBM, vmem(), FROM_HBM, FROM_HBM, vmem()],
-        [pltpu.VMEM(square, F32), pltpu.VMEM(two, BF16), pltpu.VMEM((NEG_DEV, H), F32), pltpu.SemaphoreType.DMA((RELS,))],
+        (),
         (neg_ids, halo_count, incoming.reshape(512, H), own_sum, pre, weights),
     )
     near_rows = swap(picked, FAR).reshape(square)

time: 133 us -> 132 us (level)
  no operation moved by 1% of the time
where the time goes in v6:
time: 132 us
  blocking collectives  37.9 us (29%)
  Pallas kernels  33.4 us (25%)
  starting transfers between devices  28.9 us (22%)
  waiting for transfers between devices  25.7 us (19%)
  other arithmetic  2.64 us (2%)
  local copies, waits for them, and re-layouts  1.47 us (1%)
  between operations  1.46 us (1%)
    all_to_all x2, blocking collectives, swap(): return lax.all_to_all(x, axes, split_axis=0, concat_axis=0, tiled=True)  37.9 us
    pallas_call x12, Pallas kernels, call(): pl.pallas_call(body, out_shape=made, grid=(1,), in_specs=ins, out_specs=b...  30.8 us
    all_to_all x3, waiting for transfers between devices, swap(): return lax.all_to_all(x, axes, split_axis=0, concat_axis=0, tiled=True)  24.9 us
    all_to_all x3, starting transfers between devices, swap(): return lax.all_to_all(x, axes, split_axis=0, concat_axis=0, tiled=True)  20.8 us
    ppermute x7, starting transfers between devices, core_swap(): return lax.ppermute(x, 'dom_3', [(0, 1), (1, 0)])  8.19 us
  transfers between devices with their start and end apart: 10, of which 4 were waited for; matrix products, arithmetic and copies ran while one was open for 2% of the time, Pallas kernels for 14%

profile of v6, /device:TPU:1, one launch (start us, length us, event | category | flops | bytes accessed | tf_op | source)
XLA Modules:
  0.0 131.5 jit_solution(1456942624807271143)
XLA Ops:
  0.6 2.5 %shard_map.95 = bf16[128,4,512]{2,1,0:T(4,128)(2,1)} custom-call(s32[4,128]{1,0:T(4,128)} %bitcast.16, bf16[512,512]{1,0:T(8,128)(2,1)} %features_ref.7), custom_call_target="tpu_custom_call" | custom-call | tf_op jit(solution)/shard_map/pallas_call | solution.py:92
  3.1 11.5 %all-to-all-start = ((bf16[128,4,512]{2,1,0:T(4,128)(2,1)}), bf16[128,4,512]{2,1,0:T(4,128)(2,1)S(1)}, u32[]{:S(2)}, u32[]{:S(2)}) async-start(bf16[128,4,512]{2,1,0:T(4,128)(2,1)} %shard_map.95), calls=%async_computation | async-start | bytes 1048576 | tf_op jit(solution)/shard_map/all_to_all | solution.py:36
  14.8 7.2 %shard_map.94 = (bf16[2,512,512]{2,1,0:T(8,128)(2,1)}, f32[2,512,512]{2,1,0:T(8,128)}, f32[512,512]{1,0:T(8,128)}) custom-call(bf16[512,512]{1,0:T(8,128)(2,1)} %features_ref.7, bf16[3,512,512]{2,1,0:T(8,128)(2,1)} %w_ref.3, s32[512,16]{1,0:T(8,128)S(1)} %copy.12.nbr_ref), custom_call_target="tpu_custom_call" | custom-call | tf_op jit(solution)/shard_map/pallas_call | solution.py:92
  22.0 6.3 %all-to-all-done = bf16[128,4,512]{2,1,0:T(4,128)(2,1)S(1)} async-done(((bf16[128,4,512]{2,1,0:T(4,128)(2,1)}), bf16[128,4,512]{2,1,0:T(4,128)(2,1)S(1)}, u32[]{:S(2)}, u32[]{:S(2)}) %all-to-all-start) | async-done | bytes 524320 | tf_op jit(solution)/shard_map/all_to_all | solution.py:36
  28.4 4.4 %shard_map.96 = (bf16[2,512,512]{2,1,0:T(8,128)(2,1)}, bf16[512,512]{1,0:T(8,128)(2,1)S(1)}, bf16[64,8,512]{2,1,0:T(8,128)(2,1)}) custom-call(s32[8]{0:T(128)S(1)} %copy-done.2, bf16[2,512,512]{2,1,0:T(8,128)(2,1)} %get-tuple-element.44.count_ref, bf16[512,512]{1,0:T(8,128)(2,1)S(1)} %reshape.29.halo_ref, f32[2,512,512]{2,1,0:T(8,128)} %get-tuple-element.46.own_sum_ref, ...), custom_call_target="tpu_custom_call" | custom-call | tf_op jit(solution)/shard_map/pallas_call | solution.py:92
  32.8 4.6 %all-to-all-start.1 = ((bf16[64,8,512]{2,1,0:T(8,128)(2,1)}), bf16[64,8,512]{2,1,0:T(8,128)(2,1)S(1)}, u32[]{:S(2)}, u32[]{:S(2)}) async-start(bf16[64,8,512]{2,1,0:T(8,128)(2,1)} %get-tuple-element.49), calls=%async_computation.1 | async-start | bytes 1048576 | tf_op jit(solution)/shard_map/all_to_all | solution.py:36
  38.1 4.4 %shard_map.97 = (f32[512,512]{1,0:T(8,128)}, f32[8,128]{1,0:T(8,128)S(1)}, f32[512,128]{1,0:T(8,128)S(1)}, bf16[512,1024]{1,0:T(8,128)(2,1)S(1)}) custom-call(s32[1]{0:T(128)S(6)} %copy.14.count_ref, bf16[512,512]{1,0:T(8,128)(2,1)S(1)} %get-tuple-element.48.embed_ref, s32[16,2,256]{2,1,0:T(2,128)} %ends_ref.1, bf16[512,512]{1,0:T(8,128)(2,1)} %features_ref.7, ...), custom_call_target="tpu_custom_call" | custom-call | tf_op jit(solution)/shard_map/pallas_call | solution.py:92
  42.5 6.8 %all-to-all-done.1 = bf16[64,8,512]{2,1,0:T(8,128)(2,1)S(1)} async-done(((bf16[64,8,512]{2,1,0:T(8,128)(2,1)}), bf16[64,8,512]{2,1,0:T(8,128)(2,1)S(1)}, u32[]{:S(2)}, u32[]{:S(2)}) %all-to-all-start.1) | async-done | bytes 524320 | tf_op jit(solution)/shard_map/all_to_all | solution.py:36
  49.3 2.6 %collective-permute-start = (bf16[512,512]{1,0:T(8,128)(2,1)S(1)}, bf16[512,512]{1,0:T(8,128)(2,1)S(1)}, u32[]{:S(2)}, u32[]{:S(2)}) collective-permute-start(bf16[512,512]{1,0:T(8,128)(2,1)S(1)} %bitcast.10), channel_id=1, source_target_pairs={{0,1},{1,0},{2,3},{3,2},{4,5},{5,4},{6,7},{7,6},{8,9},{9,8},{10,11... | collective-permute-start | bytes 1572872 | tf_op jit(solution)/shard_map/ppermute | solution.py:40
  51.9 1.8 %shard_map.98 = (bf16[512,512]{1,0:T(8,128)(2,1)S(1)}, f32[512,512]{1,0:T(8,128)S(1)}, f32[8,128]{1,0:T(8,128)S(1)}) custom-call(bf16[512,512]{1,0:T(8,128)(2,1)S(1)} %get-tuple-element.48.embed_ref, bf16[512,512]{1,0:T(8,128)(2,1)S(1)} %bitcast.11, bf16[512,1024]{1,0:T(8,128)(2,1)S(1)} %get-tuple-element.53.spread_ref, ...), custom_call_target="tpu_custom_call" | custom-call | tf_op jit(solution)/shard_map/pallas_call | solution.py:92
  53.7 1.8 %shard_map.99 = (bf16[512,512]{1,0:T(8,128)(2,1)S(1)}, bf16[512,512]{1,0:T(8,128)(2,1)S(1)}, f32[8,128]{1,0:T(8,128)S(1)}) custom-call(bf16[512,512]{1,0:T(8,128)(2,1)S(1)} %get-tuple-element.48.embed_ref, bf16[512,512]{1,0:T(8,128)(2,1)S(1)} %collective-permute-done.rows_ref, bf16[512,1024]{1,0:T(8,128)(2,1)S(1)} %get-tuple-element.53.spread_ref, ...), custom_call_target="tpu_custom_call" | custom-call | tf_op jit(solution)/shard_map/pallas_call | solution.py:92
  55.6 0.4 collective-permute-start.2
  56.0 1.9 %shard_map.100.grad_ref = f32[512,512]{1,0:T(8,128)S(1)} custom-call(bf16[512,512]{1,0:T(8,128)(2,1)S(1)} %get-tuple-element.59.near_weight_ref, bf16[512,512]{1,0:T(8,128)(2,1)S(1)} %bitcast.12, bf16[512,512]{1,0:T(8,128)(2,1)S(1)} %get-tuple-element.60.weight_ref, bf16[512,512]{1,0:T(8,128)(2,1)S(1)} %collective-permute-done.rows_ref, ...), custom_call_target="tpu_custom_call" | custom-call | tf_op jit(solution)/shard_map/pallas_call | solution.py:92
  58.0 1.1 shard_map.101
  59.1 2.9 %shard_map.102 = (f32[1536,256]{1,0:T(8,128)S(1)}, f32[1536,256]{1,0:T(8,128)S(1)}, bf16[16,1536]{1,0:T(8,128)(2,1)S(1)}) custom-call(s32[8]{0:T(128)S(1)} %copy-done.2, s32[1]{0:T(128)} %bitcast.core_ref, f32[512,512]{1,0:T(8,128)S(1)} %shard_map.100.grad_ref, bf16[512,512]{1,0:T(8,128)(2,1)} %features_ref.7, bf16[2,512,512]{2,1,0:T(8,128)(2,1)} %get-tuple-element.50.means_ref), custom_call_target="tpu_custom_call" | custom-call | tf_op jit(solution)/shard_map/pallas_call | solution.py:92
  62.0 1.1 copy-done.1
  63.2 0.3 collective-permute-start.3
  63.4 4.6 %all-to-all-start.2 = ((bf16[64,8,640]{2,1,0:T(8,128)(2,1)}), bf16[64,8,640]{2,1,0:T(8,128)(2,1)S(1)}, u32[]{:S(2)}, u32[]{:S(2)}) async-start(bf16[64,8,640]{2,1,0:T(8,128)(2,1)} %shard_map.101), calls=%async_computation.2 | async-start | bytes 1310720 | tf_op jit(solution)/shard_map/all_to_all | solution.py:36
  68.1 0.3 collective-permute-start.4
  68.4 2.1 %add.3.known_ref = f32[1536,256]{1,0:T(8,128)S(1)} add(f32[1536,256]{1,0:T(8,128)} %copy-done.1, f32[1536,256]{1,0:T(8,128)} %collective-permute-done.3) | non-fusion elementwise | flops 393216 | bytes 4718592 | tf_op jit(solution)/shard_map/add | solution.py:441
  70.5 11.8 %all-to-all-done.2.arrived_ref = bf16[64,8,640]{2,1,0:T(8,128)(2,1)S(1)} async-done(((bf16[64,8,640]{2,1,0:T(8,128)(2,1)}), bf16[64,8,640]{2,1,0:T(8,128)(2,1)S(1)}, u32[]{:S(2)}, u32[]{:S(2)}) %all-to-all-start.2) | async-done | bytes 655392 | tf_op jit(solution)/shard_map/all_to_all | solution.py:36
  82.3 0.7 shard_map.103
  83.0 1.6 %collective-permute-start.5 = (bf16[16,256]{1,0:T(8,128)(2,1)S(1)}, bf16[16,256]{1,0:T(8,128)(2,1)S(1)}, u32[]{:S(2)}, u32[]{:S(2)}) collective-permute-start(bf16[16,256]{1,0:T(8,128)(2,1)S(1)} %get-tuple-element.74), channel_id=1, source_target_pairs={{0,1},{1,0},{2,3},{3,2},{4,5},{5,4},{6,7},{7,6},{8,9},{9,8},{10,11... | collective-permute-start | bytes 24584 | tf_op jit(solution)/shard_map/ppermute | solution.py:40
  84.6 0.8 collective-permute-done.5.other_row_ref
  85.4 0.6 shard_map.104
  86.2 19.4 %all_to_all.25 = f16[64,24,256]{2,1,0:T(8,128)(2,1)S(1)} all-to-all(f16[64,24,256]{2,1,0:T(8,128)(2,1)S(1)} %bitcast.14), channel_id=1, replica_groups=mesh['dom_0'=4,'dom_1'=4,'dom_2'=4,'dom_3'=2] {'dom_0','dom_1','dom_2'}, dimensions={0} | all-to-all | bytes 1572864 | tf_op jit(solution)/shard_map/all_to_all | solution.py:36
  105.8 18.5 %all_to_all.26 = f16[64,24,256]{2,1,0:T(8,128)(2,1)S(1)} all-to-all(f16[64,24,256]{2,1,0:T(8,128)(2,1)S(1)} %broadcast_in_dim.3), channel_id=1, replica_groups=mesh['dom_0'=4,'dom_1'=4,'dom_2'=4,'dom_3'=2] {'dom_0','dom_1','dom_2'}, dimensions={0} | all-to-all | bytes 1572864 | tf_op jit(solution)/shard_map/all_to_all | solution.py:36
  124.3 2.9 %collective-permute-start.6 = (f16[1536,256]{1,0:T(8,128)(2,1)S(1)}, f16[1536,256]{1,0:T(8,128)(2,1)S(1)}, u32[]{:S(2)}, u32[]{:S(2)}) collective-permute-start(f16[1536,256]{1,0:T(8,128)(2,1)S(1)} %bitcast.13), channel_id=1, source_target_pairs={{0,1},{1,0},{2,3},{3,2},{4,5},{5,4},{6,7},{7,6},{8,9},{9,8},{10,11... | collective-permute-start | bytes 2359304 | tf_op jit(solution)/shard_map/ppermute | solution.py:40
  127.2 1.5 %shard_map.107 = bf16[512,512]{1,0:T(8,128)(2,1)} custom-call(s32[8]{0:T(128)S(1)} %copy-done.2, f32[8,512]{1,0:T(8,128)S(1)} %get-tuple-element.82.total_ref, f32[512,512]{1,0:T(8,128)S(1)} %shard_map.100.grad_ref), custom_call_target="tpu_custom_call" | custom-call | tf_op jit(solution)/shard_map/pallas_call | solution.py:92
  128.7 0.2 bitcast_convert_fusion.half_ref
  128.8 1.3 shard_map.105
  130.3 1.3 shard_map.106
  (21 shorter events, 0.8 us)
Async XLA Ops:
  0.6 14.0 %copy-start.3 = (s32[512,2,8]{0,2,1:T(8,128)S(1)}, s32[512,2,8]{0,2,1:T(8,128)}, u32[]{:S(2)}) copy-start(s32[512,2,8]{0,2,1:T(8,128)} %param.10) | copy-start | bytes 98308
  3.1 25.1 %all-to-all-start = ((bf16[128,4,512]{2,1,0:T(4,128)(2,1)}), bf16[128,4,512]{2,1,0:T(4,128)(2,1)S(1)}, u32[]{:S(2)}, u32[]{:S(2)}) async-start(bf16[128,4,512]{2,1,0:T(4,128)(2,1)} %shard_map.95), calls=%async_computation | async-start | bytes 1048576 | tf_op jit(solution)/shard_map/all_to_all | solution.py:36
  14.8 13.6 %copy-start = (bf16[3,512,512]{2,1,0:T(8,128)(2,1)S(1)}, bf16[3,512,512]{2,1,0:T(8,128)(2,1)}, u32[]{:S(2)}) copy-start(bf16[3,512,512]{2,1,0:T(8,128)(2,1)} %w_ref.3) | copy-start | bytes 4718596
  14.8 13.6 %copy-start.2 = (s32[8]{0:T(128)S(1)}, s32[8]{0:T(128)}, u32[]{:S(2)}) copy-start(s32[8]{0:T(128)} %neg_ids_ref.7) | copy-start | bytes 100
  32.8 16.5 %all-to-all-start.1 = ((bf16[64,8,512]{2,1,0:T(8,128)(2,1)}), bf16[64,8,512]{2,1,0:T(8,128)(2,1)S(1)}, u32[]{:S(2)}, u32[]{:S(2)}) async-start(bf16[64,8,512]{2,1,0:T(8,128)(2,1)} %get-tuple-element.49), calls=%async_computation.1 | async-start | bytes 1048576 | tf_op jit(solution)/shard_map/all_to_all | solution.py:36
  49.3 4.4 %collective-permute-start = (bf16[512,512]{1,0:T(8,128)(2,1)S(1)}, bf16[512,512]{1,0:T(8,128)(2,1)S(1)}, u32[]{:S(2)}, u32[]{:S(2)}) collective-permute-start(bf16[512,512]{1,0:T(8,128)(2,1)S(1)} %bitcast.10), channel_id=1, source_target_pairs={{0,1},{1,0},{2,3},{3,2},{4,5},{5,4},{6,7},{7,6},{8,9},{9,8},{10,11... | collective-permute-start | bytes 1572872 | tf_op jit(solution)/shard_map/ppermute | solution.py:40
  55.5 2.5 %collective-permute-start.1 = (bf16[512,512]{1,0:T(8,128)(2,1)S(1)}, bf16[512,512]{1,0:T(8,128)(2,1)S(1)}, u32[]{:S(2)}, u32[]{:S(2)}) collective-permute-start(bf16[512,512]{1,0:T(8,128)(2,1)S(1)} %get-tuple-element.58), channel_id=1, source_target_pairs={{0,1},{1,0},{2,3},{3,2},{4,5},{5,4},{6,7},{7,6},{8,9},{9,8},{10,11... | collective-permute-start | bytes 1572872 | tf_op jit(solution)/shard_map/ppermute | solution.py:40
  55.6 2.4 %collective-permute-start.2 = (f32[8,128]{1,0:T(8,128)S(1)}, f32[8,128]{1,0:T(8,128)S(1)}, u32[]{:S(2)}, u32[]{:S(2)}) collective-permute-start(f32[8,128]{1,0:T(8,128)S(1)} %get-tuple-element.63.own_note_ref), channel_id=1, source_target_pairs={{0,1},{1,0},{2,3},{3,2},{4,5},{5,4},{6,7},{7,6},{8,9},{9,8},{10,11... | collective-permute-start | bytes 12296 | tf_op jit(solution)/shard_map/ppermute | solution.py:40
  62.0 1.1 copy-start.1
  63.2 5.2 %collective-permute-start.3 = (f32[1536,256]{1,0:T(8,128)S(1)}, f32[1536,256]{1,0:T(8,128)}, u32[]{:S(2)}, u32[]{:S(2)}) collective-permute-start(f32[1536,256]{1,0:T(8,128)S(1)} %get-tuple-element.68), channel_id=1, source_target_pairs={{0,1},{1,0},{2,3},{3,2},{4,5},{5,4},{6,7},{7,6},{8,9},{9,8},{10,11... | collective-permute-start | bytes 4718600 | tf_op jit(solution)/shard_map/ppermute | solution.py:40
  63.4 18.9 %all-to-all-start.2 = ((bf16[64,8,640]{2,1,0:T(8,128)(2,1)}), bf16[64,8,640]{2,1,0:T(8,128)(2,1)S(1)}, u32[]{:S(2)}, u32[]{:S(2)}) async-start(bf16[64,8,640]{2,1,0:T(8,128)(2,1)} %shard_map.101), calls=%async_computation.2 | async-start | bytes 1310720 | tf_op jit(solution)/shard_map/all_to_all | solution.py:36
  68.1 2.4 %collective-permute-start.4 = (bf16[16,1536]{1,0:T(8,128)(2,1)S(1)}, bf16[16,1536]{1,0:T(8,128)(2,1)S(1)}, u32[]{:S(2)}, u32[]{:S(2)}) collective-permute-start(bf16[16,1536]{1,0:T(8,128)(2,1)S(1)} %get-tuple-element.69.own_chosen_ref), channel_id=1, source_target_pairs={{0,1},{1,0},{2,3},{3,2},{4,5},{5,4},{6,7},{7,6},{8,9},{9,8},{10,11... | collective-permute-start | bytes 147464 | tf_op jit(solution)/shard_map/ppermute | solution.py:40
  83.0 2.4 %collective-permute-start.5 = (bf16[16,256]{1,0:T(8,128)(2,1)S(1)}, bf16[16,256]{1,0:T(8,128)(2,1)S(1)}, u32[]{:S(2)}, u32[]{:S(2)}) collective-permute-start(bf16[16,256]{1,0:T(8,128)(2,1)S(1)} %get-tuple-element.74), channel_id=1, source_target_pairs={{0,1},{1,0},{2,3},{3,2},{4,5},{5,4},{6,7},{7,6},{8,9},{9,8},{10,11... | collective-permute-start | bytes 24584 | tf_op jit(solution)/shard_map/ppermute | solution.py:40
  124.3 5.9 %collective-permute-start.6 = (f16[1536,256]{1,0:T(8,128)(2,1)S(1)}, f16[1536,256]{1,0:T(8,128)(2,1)S(1)}, u32[]{:S(2)}, u32[]{:S(2)}) collective-permute-start(f16[1536,256]{1,0:T(8,128)(2,1)S(1)} %bitcast.13), channel_id=1, source_target_pairs={{0,1},{1,0},{2,3},{3,2},{4,5},{5,4},{6,7},{7,6},{8,9},{9,8},{10,11... | collective-permute-start | bytes 2359304 | tf_op jit(solution)/shard_map/ppermute | solution.py:40

commit v7 on v6

--- a/solution.py
+++ b/solution.py
@@ -26,6 +26,7 @@
 F16 = jnp.float16
 SPAN = 60000.0
 TINY = 1e-30
+CODE = 32.0
 NT = (((1,), (1,)), ((), ()))
 TN = (((0,), (0,)), ((), ()))
 FROM_HBM = "hbm"
@@ -121,15 +122,15 @@
         at = pl.ds(pl.multiple_of(step * rows, rows), rows)
         for r in range(RELS):
             index = nbr_ref[at, r * FAN : (r + 1) * FAN]
-            for half in range(2):
-                total = jnp.zeros((rows, NODE_DEV), F32)
-                for k in range(FAN):
-                    hit = lanes == (index[:, k : k + 1] - half * NODE_DEV)
-                    total = total + jnp.where(hit, 1.0, 0.0)
-                if half == 0:
-                    count_buf[r, at, :] = total.astype(BF16)
-                else:
-                    halo_buf[r, at, :] = total.astype(BF16)
+            place = index & (NODE_DEV - 1)
+            code = jnp.where(index < NODE_DEV, 1.0, CODE)
+            total = jnp.zeros((rows, NODE_DEV), F32)
+            for k in range(FAN):
+                hit = lanes == place[:, k : k + 1]
+                total = total + jnp.where(hit, code[:, k : k + 1], 0.0)
+            halo = jnp.floor(total * (1.0 / CODE))
+            halo_buf[r, at, :] = halo.astype(BF16)
+            count_buf[r, at, :] = (total - CODE * halo).astype(BF16)
         return 0
 
     lax.fori_loop(0, NODE_DEV // rows, chunk, 0)
@@ -369,7 +370,7 @@
     tall = ((RELS + 1) * H, HALF)
     core = lax.axis_index(NEAR).astype(jnp.int32).reshape(1)
     core, halo_send = lax.optimization_barrier((core, halo_send))
-    (outgoing,) = call(halo_body, [hbm((N_DOM, HALO_PEER, H), BF16)], [FROM_HBM, FROM_HBM], (), (halo_send[0].T, features))
+    (outgoing,) = call(halo_body, [((N_DOM, HALO_PEER, H), BF16)], [FROM_HBM, FROM_HBM], (), (halo_send[0].T, features))
     incoming = swap(outgoing, DOM)
     neighbours = nbr_index.reshape(NODE_DEV, RELS * FAN)
     two = (RELS, *square)

time: 132 us -> 132 us (level)
  Pallas kernels: 33.4 us -> 31.7 us
  waiting for transfers between devices: 25.7 us -> 27.4 us
    pallas_call x12, Pallas kernels: 30.8 us -> 29.1 us  [call(): pl.pallas_call(body, out_shape=made, grid=(1,), in_specs=ins, out_specs=b...]
    all_to_all x3, waiting for transfers between devices: 24.9 us -> 26.6 us  [swap(): return lax.all_to_all(x, axes, split_axis=0, concat_axis=0, tiled=True)]
  transfers between devices with their start and end apart: 10 -> 10, of which waited for: 4 -> 4; matrix products, arithmetic and copies ran while one was open for 2% -> 2% of each run, Pallas kernels for 14% -> 12%
where the time goes in v7:
time: 132 us
  blocking collectives  37.9 us (29%)
  Pallas kernels  31.7 us (24%)
  starting transfers between devices  28.9 us (22%)
  waiting for transfers between devices  27.4 us (21%)
  other arithmetic  2.64 us (2%)
  local copies, waits for them, and re-layouts  1.47 us (1%)
  between operations  1.46 us (1%)
    all_to_all x2, blocking collectives, swap(): return lax.all_to_all(x, axes, split_axis=0, concat_axis=0, tiled=True)  37.9 us
    pallas_call x12, Pallas kernels, call(): pl.pallas_call(body, out_shape=made, grid=(1,), in_specs=ins, out_specs=b...  29.1 us
    all_to_all x3, waiting for transfers between devices, swap(): return lax.all_to_all(x, axes, split_axis=0, concat_axis=0, tiled=True)  26.6 us
    all_to_all x3, starting transfers between devices, swap(): return lax.all_to_all(x, axes, split_axis=0, concat_axis=0, tiled=True)  20.8 us
    ppermute x7, starting transfers between devices, core_swap(): return lax.ppermute(x, 'dom_3', [(0, 1), (1, 0)])  8.19 us
  transfers between devices with their start and end apart: 10, of which 4 were waited for; matrix products, arithmetic and copies ran while one was open for 2% of the time, Pallas kernels for 12%

profile of v7, /device:TPU:1, one launch (start us, length us, event | category | flops | bytes accessed | tf_op | source)
XLA Modules:
  0.0 131.5 jit_solution(5983519300141420661)
XLA Ops:
  0.6 2.5 %shard_map.95 = bf16[128,4,512]{2,1,0:T(4,128)(2,1)} custom-call(s32[4,128]{1,0:T(4,128)} %bitcast.16, bf16[512,512]{1,0:T(8,128)(2,1)} %features_ref.7), custom_call_target="tpu_custom_call" | custom-call | tf_op jit(solution)/shard_map/pallas_call | solution.py:93
  3.1 11.5 %all-to-all-start = ((bf16[128,4,512]{2,1,0:T(4,128)(2,1)}), bf16[128,4,512]{2,1,0:T(4,128)(2,1)S(1)}, u32[]{:S(2)}, u32[]{:S(2)}) async-start(bf16[128,4,512]{2,1,0:T(4,128)(2,1)} %shard_map.95), calls=%async_computation | async-start | bytes 1048576 | tf_op jit(solution)/shard_map/all_to_all | solution.py:37
  14.8 5.5 %shard_map.94 = (bf16[2,512,512]{2,1,0:T(8,128)(2,1)}, f32[2,512,512]{2,1,0:T(8,128)}, f32[512,512]{1,0:T(8,128)}) custom-call(bf16[512,512]{1,0:T(8,128)(2,1)} %features_ref.7, bf16[3,512,512]{2,1,0:T(8,128)(2,1)} %w_ref.3, s32[512,16]{1,0:T(8,128)S(1)} %copy.12.nbr_ref), custom_call_target="tpu_custom_call" | custom-call | tf_op jit(solution)/shard_map/pallas_call | solution.py:93
  20.3 8.0 %all-to-all-done = bf16[128,4,512]{2,1,0:T(4,128)(2,1)S(1)} async-done(((bf16[128,4,512]{2,1,0:T(4,128)(2,1)}), bf16[128,4,512]{2,1,0:T(4,128)(2,1)S(1)}, u32[]{:S(2)}, u32[]{:S(2)}) %all-to-all-start) | async-done | bytes 524320 | tf_op jit(solution)/shard_map/all_to_all | solution.py:37
  28.4 4.4 %shard_map.96 = (bf16[2,512,512]{2,1,0:T(8,128)(2,1)}, bf16[512,512]{1,0:T(8,128)(2,1)S(1)}, bf16[64,8,512]{2,1,0:T(8,128)(2,1)}) custom-call(s32[8]{0:T(128)S(1)} %copy-done.2, bf16[2,512,512]{2,1,0:T(8,128)(2,1)} %get-tuple-element.44.count_ref, bf16[512,512]{1,0:T(8,128)(2,1)S(1)} %reshape.29.halo_ref, f32[2,512,512]{2,1,0:T(8,128)} %get-tuple-element.46.own_sum_ref, ...), custom_call_target="tpu_custom_call" | custom-call | tf_op jit(solution)/shard_map/pallas_call | solution.py:93
  32.8 4.6 %all-to-all-start.1 = ((bf16[64,8,512]{2,1,0:T(8,128)(2,1)}), bf16[64,8,512]{2,1,0:T(8,128)(2,1)S(1)}, u32[]{:S(2)}, u32[]{:S(2)}) async-start(bf16[64,8,512]{2,1,0:T(8,128)(2,1)} %get-tuple-element.49), calls=%async_computation.1 | async-start | bytes 1048576 | tf_op jit(solution)/shard_map/all_to_all | solution.py:37
  38.1 4.4 %shard_map.97 = (f32[512,512]{1,0:T(8,128)}, f32[8,128]{1,0:T(8,128)S(1)}, f32[512,128]{1,0:T(8,128)S(1)}, bf16[512,1024]{1,0:T(8,128)(2,1)S(1)}) custom-call(s32[1]{0:T(128)S(6)} %copy.14.count_ref, bf16[512,512]{1,0:T(8,128)(2,1)S(1)} %get-tuple-element.48.embed_ref, s32[16,2,256]{2,1,0:T(2,128)} %ends_ref.1, bf16[512,512]{1,0:T(8,128)(2,1)} %features_ref.7, ...), custom_call_target="tpu_custom_call" | custom-call | tf_op jit(solution)/shard_map/pallas_call | solution.py:93
  42.5 6.8 %all-to-all-done.1 = bf16[64,8,512]{2,1,0:T(8,128)(2,1)S(1)} async-done(((bf16[64,8,512]{2,1,0:T(8,128)(2,1)}), bf16[64,8,512]{2,1,0:T(8,128)(2,1)S(1)}, u32[]{:S(2)}, u32[]{:S(2)}) %all-to-all-start.1) | async-done | bytes 524320 | tf_op jit(solution)/shard_map/all_to_all | solution.py:37
  49.3 2.6 %collective-permute-start = (bf16[512,512]{1,0:T(8,128)(2,1)S(1)}, bf16[512,512]{1,0:T(8,128)(2,1)S(1)}, u32[]{:S(2)}, u32[]{:S(2)}) collective-permute-start(bf16[512,512]{1,0:T(8,128)(2,1)S(1)} %bitcast.10), channel_id=1, source_target_pairs={{0,1},{1,0},{2,3},{3,2},{4,5},{5,4},{6,7},{7,6},{8,9},{9,8},{10,11... | collective-permute-start | bytes 1572872 | tf_op jit(solution)/shard_map/ppermute | solution.py:41
  51.9 1.8 %shard_map.98 = (bf16[512,512]{1,0:T(8,128)(2,1)S(1)}, f32[512,512]{1,0:T(8,128)S(1)}, f32[8,128]{1,0:T(8,128)S(1)}) custom-call(bf16[512,512]{1,0:T(8,128)(2,1)S(1)} %get-tuple-element.48.embed_ref, bf16[512,512]{1,0:T(8,128)(2,1)S(1)} %bitcast.11, bf16[512,1024]{1,0:T(8,128)(2,1)S(1)} %get-tuple-element.53.spread_ref, ...), custom_call_target="tpu_custom_call" | custom-call | tf_op jit(solution)/shard_map/pallas_call | solution.py:93
  53.7 1.8 %shard_map.99 = (bf16[512,512]{1,0:T(8,128)(2,1)S(1)}, bf16[512,512]{1,0:T(8,128)(2,1)S(1)}, f32[8,128]{1,0:T(8,128)S(1)}) custom-call(bf16[512,512]{1,0:T(8,128)(2,1)S(1)} %get-tuple-element.48.embed_ref, bf16[512,512]{1,0:T(8,128)(2,1)S(1)} %collective-permute-done.rows_ref, bf16[512,1024]{1,0:T(8,128)(2,1)S(1)} %get-tuple-element.53.spread_ref, ...), custom_call_target="tpu_custom_call" | custom-call | tf_op jit(solution)/shard_map/pallas_call | solution.py:93
  55.6 0.4 collective-permute-start.2
  56.0 1.9 %shard_map.100.grad_ref = f32[512,512]{1,0:T(8,128)S(1)} custom-call(bf16[512,512]{1,0:T(8,128)(2,1)S(1)} %get-tuple-element.59.near_weight_ref, bf16[512,512]{1,0:T(8,128)(2,1)S(1)} %bitcast.12, bf16[512,512]{1,0:T(8,128)(2,1)S(1)} %get-tuple-element.60.weight_ref, bf16[512,512]{1,0:T(8,128)(2,1)S(1)} %collective-permute-done.rows_ref, ...), custom_call_target="tpu_custom_call" | custom-call | tf_op jit(solution)/shard_map/pallas_call | solution.py:93
  58.0 1.1 shard_map.101
  59.1 2.9 %shard_map.102 = (f32[1536,256]{1,0:T(8,128)S(1)}, f32[1536,256]{1,0:T(8,128)S(1)}, bf16[16,1536]{1,0:T(8,128)(2,1)S(1)}) custom-call(s32[8]{0:T(128)S(1)} %copy-done.2, s32[1]{0:T(128)} %bitcast.core_ref, f32[512,512]{1,0:T(8,128)S(1)} %shard_map.100.grad_ref, bf16[512,512]{1,0:T(8,128)(2,1)} %features_ref.7, bf16[2,512,512]{2,1,0:T(8,128)(2,1)} %get-tuple-element.50.means_ref), custom_call_target="tpu_custom_call" | custom-call | tf_op jit(solution)/shard_map/pallas_call | solution.py:93
  62.0 1.1 copy-done.1
  63.2 0.3 collective-permute-start.3
  63.4 4.6 %all-to-all-start.2 = ((bf16[64,8,640]{2,1,0:T(8,128)(2,1)}), bf16[64,8,640]{2,1,0:T(8,128)(2,1)S(1)}, u32[]{:S(2)}, u32[]{:S(2)}) async-start(bf16[64,8,640]{2,1,0:T(8,128)(2,1)} %shard_map.101), calls=%async_computation.2 | async-start | bytes 1310720 | tf_op jit(solution)/shard_map/all_to_all | solution.py:37
  68.1 0.3 collective-permute-start.4
  68.4 2.1 %add.3.known_ref = f32[1536,256]{1,0:T(8,128)S(1)} add(f32[1536,256]{1,0:T(8,128)} %copy-done.1, f32[1536,256]{1,0:T(8,128)} %collective-permute-done.3) | non-fusion elementwise | flops 393216 | bytes 4718592 | tf_op jit(solution)/shard_map/add | solution.py:442
  70.5 11.8 %all-to-all-done.2.arrived_ref = bf16[64,8,640]{2,1,0:T(8,128)(2,1)S(1)} async-done(((bf16[64,8,640]{2,1,0:T(8,128)(2,1)}), bf16[64,8,640]{2,1,0:T(8,128)(2,1)S(1)}, u32[]{:S(2)}, u32[]{:S(2)}) %all-to-all-start.2) | async-done | bytes 655392 | tf_op jit(solution)/shard_map/all_to_all | solution.py:37
  82.3 0.7 shard_map.103
  83.0 1.6 %collective-permute-start.5 = (bf16[16,256]{1,0:T(8,128)(2,1)S(1)}, bf16[16,256]{1,0:T(8,128)(2,1)S(1)}, u32[]{:S(2)}, u32[]{:S(2)}) collective-permute-start(bf16[16,256]{1,0:T(8,128)(2,1)S(1)} %get-tuple-element.74), channel_id=1, source_target_pairs={{0,1},{1,0},{2,3},{3,2},{4,5},{5,4},{6,7},{7,6},{8,9},{9,8},{10,11... | collective-permute-start | bytes 24584 | tf_op jit(solution)/shard_map/ppermute | solution.py:41
  84.6 0.8 collective-permute-done.5.other_row_ref
  85.4 0.6 shard_map.104
  86.2 19.4 %all_to_all.25 = f16[64,24,256]{2,1,0:T(8,128)(2,1)S(1)} all-to-all(f16[64,24,256]{2,1,0:T(8,128)(2,1)S(1)} %bitcast.14), channel_id=1, replica_groups=mesh['dom_0'=4,'dom_1'=4,'dom_2'=4,'dom_3'=2] {'dom_0','dom_1','dom_2'}, dimensions={0} | all-to-all | bytes 1572864 | tf_op jit(solution)/shard_map/all_to_all | solution.py:37
  105.8 18.5 %all_to_all.26 = f16[64,24,256]{2,1,0:T(8,128)(2,1)S(1)} all-to-all(f16[64,24,256]{2,1,0:T(8,128)(2,1)S(1)} %broadcast_in_dim.3), channel_id=1, replica_groups=mesh['dom_0'=4,'dom_1'=4,'dom_2'=4,'dom_3'=2] {'dom_0','dom_1','dom_2'}, dimensions={0} | all-to-all | bytes 1572864 | tf_op jit(solution)/shard_map/all_to_all | solution.py:37
  124.3 2.9 %collective-permute-start.6 = (f16[1536,256]{1,0:T(8,128)(2,1)S(1)}, f16[1536,256]{1,0:T(8,128)(2,1)S(1)}, u32[]{:S(2)}, u32[]{:S(2)}) collective-permute-start(f16[1536,256]{1,0:T(8,128)(2,1)S(1)} %bitcast.13), channel_id=1, source_target_pairs={{0,1},{1,0},{2,3},{3,2},{4,5},{5,4},{6,7},{7,6},{8,9},{9,8},{10,11... | collective-permute-start | bytes 2359304 | tf_op jit(solution)/shard_map/ppermute | solution.py:41
  127.2 1.5 %shard_map.107 = bf16[512,512]{1,0:T(8,128)(2,1)} custom-call(s32[8]{0:T(128)S(1)} %copy-done.2, f32[8,512]{1,0:T(8,128)S(1)} %get-tuple-element.82.total_ref, f32[512,512]{1,0:T(8,128)S(1)} %shard_map.100.grad_ref), custom_call_target="tpu_custom_call" | custom-call | tf_op jit(solution)/shard_map/pallas_call | solution.py:93
  128.7 0.2 bitcast_convert_fusion.half_ref
  128.8 1.3 shard_map.105
  130.3 1.3 shard_map.106
  (21 shorter events, 0.8 us)
Async XLA Ops:
  0.6 14.0 %copy-start.3 = (s32[512,2,8]{0,2,1:T(8,128)S(1)}, s32[512,2,8]{0,2,1:T(8,128)}, u32[]{:S(2)}) copy-start(s32[512,2,8]{0,2,1:T(8,128)} %param.10) | copy-start | bytes 98308
  3.1 25.1 %all-to-all-start = ((bf16[128,4,512]{2,1,0:T(4,128)(2,1)}), bf16[128,4,512]{2,1,0:T(4,128)(2,1)S(1)}, u32[]{:S(2)}, u32[]{:S(2)}) async-start(bf16[128,4,512]{2,1,0:T(4,128)(2,1)} %shard_map.95), calls=%async_computation | async-start | bytes 1048576 | tf_op jit(solution)/shard_map/all_to_all | solution.py:37
  14.8 13.6 %copy-start = (bf16[3,512,512]{2,1,0:T(8,128)(2,1)S(1)}, bf16[3,512,512]{2,1,0:T(8,128)(2,1)}, u32[]{:S(2)}) copy-start(bf16[3,512,512]{2,1,0:T(8,128)(2,1)} %w_ref.3) | copy-start | bytes 4718596
  14.8 13.6 %copy-start.2 = (s32[8]{0:T(128)S(1)}, s32[8]{0:T(128)}, u32[]{:S(2)}) copy-start(s32[8]{0:T(128)} %neg_ids_ref.7) | copy-start | bytes 100
  32.8 16.5 %all-to-all-start.1 = ((bf16[64,8,512]{2,1,0:T(8,128)(2,1)}), bf16[64,8,512]{2,1,0:T(8,128)(2,1)S(1)}, u32[]{:S(2)}, u32[]{:S(2)}) async-start(bf16[64,8,512]{2,1,0:T(8,128)(2,1)} %get-tuple-element.49), calls=%async_computation.1 | async-start | bytes 1048576 | tf_op jit(solution)/shard_map/all_to_all | solution.py:37
  49.3 4.4 %collective-permute-start = (bf16[512,512]{1,0:T(8,128)(2,1)S(1)}, bf16[512,512]{1,0:T(8,128)(2,1)S(1)}, u32[]{:S(2)}, u32[]{:S(2)}) collective-permute-start(bf16[512,512]{1,0:T(8,128)(2,1)S(1)} %bitcast.10), channel_id=1, source_target_pairs={{0,1},{1,0},{2,3},{3,2},{4,5},{5,4},{6,7},{7,6},{8,9},{9,8},{10,11... | collective-permute-start | bytes 1572872 | tf_op jit(solution)/shard_map/ppermute | solution.py:41
  55.5 2.5 %collective-permute-start.1 = (bf16[512,512]{1,0:T(8,128)(2,1)S(1)}, bf16[512,512]{1,0:T(8,128)(2,1)S(1)}, u32[]{:S(2)}, u32[]{:S(2)}) collective-permute-start(bf16[512,512]{1,0:T(8,128)(2,1)S(1)} %get-tuple-element.58), channel_id=1, source_target_pairs={{0,1},{1,0},{2,3},{3,2},{4,5},{5,4},{6,7},{7,6},{8,9},{9,8},{10,11... | collective-permute-start | bytes 1572872 | tf_op jit(solution)/shard_map/ppermute | solution.py:41
  55.6 2.4 %collective-permute-start.2 = (f32[8,128]{1,0:T(8,128)S(1)}, f32[8,128]{1,0:T(8,128)S(1)}, u32[]{:S(2)}, u32[]{:S(2)}) collective-permute-start(f32[8,128]{1,0:T(8,128)S(1)} %get-tuple-element.63.own_note_ref), channel_id=1, source_target_pairs={{0,1},{1,0},{2,3},{3,2},{4,5},{5,4},{6,7},{7,6},{8,9},{9,8},{10,11... | collective-permute-start | bytes 12296 | tf_op jit(solution)/shard_map/ppermute | solution.py:41
  62.0 1.1 copy-start.1
  63.2 5.2 %collective-permute-start.3 = (f32[1536,256]{1,0:T(8,128)S(1)}, f32[1536,256]{1,0:T(8,128)}, u32[]{:S(2)}, u32[]{:S(2)}) collective-permute-start(f32[1536,256]{1,0:T(8,128)S(1)} %get-tuple-element.68), channel_id=1, source_target_pairs={{0,1},{1,0},{2,3},{3,2},{4,5},{5,4},{6,7},{7,6},{8,9},{9,8},{10,11... | collective-permute-start | bytes 4718600 | tf_op jit(solution)/shard_map/ppermute | solution.py:41
  63.4 18.9 %all-to-all-start.2 = ((bf16[64,8,640]{2,1,0:T(8,128)(2,1)}), bf16[64,8,640]{2,1,0:T(8,128)(2,1)S(1)}, u32[]{:S(2)}, u32[]{:S(2)}) async-start(bf16[64,8,640]{2,1,0:T(8,128)(2,1)} %shard_map.101), calls=%async_computation.2 | async-start | bytes 1310720 | tf_op jit(solution)/shard_map/all_to_all | solution.py:37
  68.1 2.4 %collective-permute-start.4 = (bf16[16,1536]{1,0:T(8,128)(2,1)S(1)}, bf16[16,1536]{1,0:T(8,128)(2,1)S(1)}, u32[]{:S(2)}, u32[]{:S(2)}) collective-permute-start(bf16[16,1536]{1,0:T(8,128)(2,1)S(1)} %get-tuple-element.69.own_chosen_ref), channel_id=1, source_target_pairs={{0,1},{1,0},{2,3},{3,2},{4,5},{5,4},{6,7},{7,6},{8,9},{9,8},{10,11... | collective-permute-start | bytes 147464 | tf_op jit(solution)/shard_map/ppermute | solution.py:41
  83.0 2.4 %collective-permute-start.5 = (bf16[16,256]{1,0:T(8,128)(2,1)S(1)}, bf16[16,256]{1,0:T(8,128)(2,1)S(1)}, u32[]{:S(2)}, u32[]{:S(2)}) collective-permute-start(bf16[16,256]{1,0:T(8,128)(2,1)S(1)} %get-tuple-element.74), channel_id=1, source_target_pairs={{0,1},{1,0},{2,3},{3,2},{4,5},{5,4},{6,7},{7,6},{8,9},{9,8},{10,11... | collective-permute-start | bytes 24584 | tf_op jit(solution)/shard_map/ppermute | solution.py:41
  124.3 5.9 %collective-permute-start.6 = (f16[1536,256]{1,0:T(8,128)(2,1)S(1)}, f16[1536,256]{1,0:T(8,128)(2,1)S(1)}, u32[]{:S(2)}, u32[]{:S(2)}) collective-permute-start(f16[1536,256]{1,0:T(8,128)(2,1)S(1)} %bitcast.13), channel_id=1, source_target_pairs={{0,1},{1,0},{2,3},{3,2},{4,5},{5,4},{6,7},{7,6},{8,9},{9,8},{10,11... | collective-permute-start | bytes 2359304 | tf_op jit(solution)/shard_map/ppermute | solution.py:41

commit v8 on v7

--- a/solution.py
+++ b/solution.py
@@ -227,8 +227,9 @@
     for r in range(RELS):
         widest = jnp.maximum(widest, largest(mean_buf[r].astype(F32)))
     count = tiles.astype(F32)
+    reach = largest(embed.astype(F32)) * count * (TILE / NEG)
     known = widest * NODE_DEV * largest(base)
-    note_ref[...] = notes_of((loss, count, 0.0, known, widest * TILE * count, NEG_DEV * widest, 0.0))
+    note_ref[...] = notes_of((loss, count, 0.0, known, widest * TILE * count, NEG_DEV * widest, reach))
 
 
 def scored(embed, rows, sources, spread):
@@ -250,8 +251,7 @@
     lane = lax.broadcasted_iota(jnp.int32, note.shape, 1)
     tallest = largest(rows.astype(F32))
     note = jnp.where(lane == 0, note + loss, note)
-    note = jnp.where(lane == 2, jnp.maximum(note, note[:, 3:4] + note[:, 4:5] * tallest), note)
-    note_ref[...] = jnp.where(lane == 6, jnp.maximum(note, largest(part)), note)
+    note_ref[...] = jnp.where(lane == 2, jnp.maximum(note, note[:, 3:4] + note[:, 4:5] * tallest), note)
 
 
 def rest_body(near_weight_ref, near_rows_ref, weight_ref, rows_ref, sources_ref, base_ref, grad_ref):

time: 132 us -> 132 us (level)
  no operation moved by 1% of the time
where the time goes in v8:
time: 132 us; the launch traced here: 131 us
  blocking collectives  37.9 us (29%)
  Pallas kernels  31.5 us (24%)
  starting transfers between devices  29 us (22%)
  waiting for transfers between devices  27.4 us (21%)
  other arithmetic  2.64 us (2%)
  between operations  1.48 us (1%)
  local copies, waits for them, and re-layouts  1.47 us (1%)
    all_to_all x2, blocking collectives, swap(): return lax.all_to_all(x, axes, split_axis=0, concat_axis=0, tiled=True)  37.9 us
    pallas_call x12, Pallas kernels, call(): pl.pallas_call(body, out_shape=made, grid=(1,), in_specs=ins, out_specs=b...  29 us
    all_to_all x3, waiting for transfers between devices, swap(): return lax.all_to_all(x, axes, split_axis=0, concat_axis=0, tiled=True)  26.6 us
    all_to_all x3, starting transfers between devices, swap(): return lax.all_to_all(x, axes, split_axis=0, concat_axis=0, tiled=True)  20.8 us
    ppermute x7, starting transfers between devices, core_swap(): return lax.ppermute(x, 'dom_3', [(0, 1), (1, 0)])  8.24 us
  transfers between devices with their start and end apart: 10, of which 4 were waited for; matrix products, arithmetic and copies ran while one was open for 2% of the time, Pallas kernels for 12%

profile of v8, /device:TPU:1, one launch (start us, length us, event | category | flops | bytes accessed | tf_op | source)
XLA Modules:
  0.0 131.4 jit_solution(2910731240312123884)
XLA Ops:
  0.6 2.5 %shard_map.95 = bf16[128,4,512]{2,1,0:T(4,128)(2,1)} custom-call(s32[4,128]{1,0:T(4,128)} %bitcast.16, bf16[512,512]{1,0:T(8,128)(2,1)} %features_ref.7), custom_call_target="tpu_custom_call" | custom-call | tf_op jit(solution)/shard_map/pallas_call | solution.py:93
  3.1 11.5 %all-to-all-start = ((bf16[128,4,512]{2,1,0:T(4,128)(2,1)}), bf16[128,4,512]{2,1,0:T(4,128)(2,1)S(1)}, u32[]{:S(2)}, u32[]{:S(2)}) async-start(bf16[128,4,512]{2,1,0:T(4,128)(2,1)} %shard_map.95), calls=%async_computation | async-start | bytes 1048576 | tf_op jit(solution)/shard_map/all_to_all | solution.py:37
  14.8 5.5 %shard_map.94 = (bf16[2,512,512]{2,1,0:T(8,128)(2,1)}, f32[2,512,512]{2,1,0:T(8,128)}, f32[512,512]{1,0:T(8,128)}) custom-call(bf16[512,512]{1,0:T(8,128)(2,1)} %features_ref.7, bf16[3,512,512]{2,1,0:T(8,128)(2,1)} %w_ref.3, s32[512,16]{1,0:T(8,128)S(1)} %copy.12.nbr_ref), custom_call_target="tpu_custom_call" | custom-call | tf_op jit(solution)/shard_map/pallas_call | solution.py:93
  20.3 8.0 %all-to-all-done = bf16[128,4,512]{2,1,0:T(4,128)(2,1)S(1)} async-done(((bf16[128,4,512]{2,1,0:T(4,128)(2,1)}), bf16[128,4,512]{2,1,0:T(4,128)(2,1)S(1)}, u32[]{:S(2)}, u32[]{:S(2)}) %all-to-all-start) | async-done | bytes 524320 | tf_op jit(solution)/shard_map/all_to_all | solution.py:37
  28.4 4.4 %shard_map.96 = (bf16[2,512,512]{2,1,0:T(8,128)(2,1)}, bf16[512,512]{1,0:T(8,128)(2,1)S(1)}, bf16[64,8,512]{2,1,0:T(8,128)(2,1)}) custom-call(s32[8]{0:T(128)S(1)} %copy-done.2, bf16[2,512,512]{2,1,0:T(8,128)(2,1)} %get-tuple-element.44.count_ref, bf16[512,512]{1,0:T(8,128)(2,1)S(1)} %reshape.29.halo_ref, f32[2,512,512]{2,1,0:T(8,128)} %get-tuple-element.46.own_sum_ref, ...), custom_call_target="tpu_custom_call" | custom-call | tf_op jit(solution)/shard_map/pallas_call | solution.py:93
  32.8 4.6 %all-to-all-start.1 = ((bf16[64,8,512]{2,1,0:T(8,128)(2,1)}), bf16[64,8,512]{2,1,0:T(8,128)(2,1)S(1)}, u32[]{:S(2)}, u32[]{:S(2)}) async-start(bf16[64,8,512]{2,1,0:T(8,128)(2,1)} %get-tuple-element.49), calls=%async_computation.1 | async-start | bytes 1048576 | tf_op jit(solution)/shard_map/all_to_all | solution.py:37
  38.1 4.4 %shard_map.97 = (f32[512,512]{1,0:T(8,128)}, f32[8,128]{1,0:T(8,128)S(1)}, f32[512,128]{1,0:T(8,128)S(1)}, bf16[512,1024]{1,0:T(8,128)(2,1)S(1)}) custom-call(s32[1]{0:T(128)S(6)} %copy.14.count_ref, bf16[512,512]{1,0:T(8,128)(2,1)S(1)} %get-tuple-element.48.embed_ref, s32[16,2,256]{2,1,0:T(2,128)} %ends_ref.1, bf16[512,512]{1,0:T(8,128)(2,1)} %features_ref.7, ...), custom_call_target="tpu_custom_call" | custom-call | tf_op jit(solution)/shard_map/pallas_call | solution.py:93
  42.5 6.8 %all-to-all-done.1 = bf16[64,8,512]{2,1,0:T(8,128)(2,1)S(1)} async-done(((bf16[64,8,512]{2,1,0:T(8,128)(2,1)}), bf16[64,8,512]{2,1,0:T(8,128)(2,1)S(1)}, u32[]{:S(2)}, u32[]{:S(2)}) %all-to-all-start.1) | async-done | bytes 524320 | tf_op jit(solution)/shard_map/all_to_all | solution.py:37
  49.3 2.6 %collective-permute-start = (bf16[512,512]{1,0:T(8,128)(2,1)S(1)}, bf16[512,512]{1,0:T(8,128)(2,1)S(1)}, u32[]{:S(2)}, u32[]{:S(2)}) collective-permute-start(bf16[512,512]{1,0:T(8,128)(2,1)S(1)} %bitcast.10), channel_id=1, source_target_pairs={{0,1},{1,0},{2,3},{3,2},{4,5},{5,4},{6,7},{7,6},{8,9},{9,8},{10,11... | collective-permute-start | bytes 1572872 | tf_op jit(solution)/shard_map/ppermute | solution.py:41
  51.9 1.7 %shard_map.98 = (bf16[512,512]{1,0:T(8,128)(2,1)S(1)}, f32[512,512]{1,0:T(8,128)S(1)}, f32[8,128]{1,0:T(8,128)S(1)}) custom-call(bf16[512,512]{1,0:T(8,128)(2,1)S(1)} %get-tuple-element.48.embed_ref, bf16[512,512]{1,0:T(8,128)(2,1)S(1)} %bitcast.11, bf16[512,1024]{1,0:T(8,128)(2,1)S(1)} %get-tuple-element.53.spread_ref, ...), custom_call_target="tpu_custom_call" | custom-call | tf_op jit(solution)/shard_map/pallas_call | solution.py:93
  53.6 1.7 %shard_map.99 = (bf16[512,512]{1,0:T(8,128)(2,1)S(1)}, bf16[512,512]{1,0:T(8,128)(2,1)S(1)}, f32[8,128]{1,0:T(8,128)S(1)}) custom-call(bf16[512,512]{1,0:T(8,128)(2,1)S(1)} %get-tuple-element.48.embed_ref, bf16[512,512]{1,0:T(8,128)(2,1)S(1)} %collective-permute-done.rows_ref, bf16[512,1024]{1,0:T(8,128)(2,1)S(1)} %get-tuple-element.53.spread_ref, ...), custom_call_target="tpu_custom_call" | custom-call | tf_op jit(solution)/shard_map/pallas_call | solution.py:93
  55.4 0.2 collective-permute-start.1
  55.6 0.4 collective-permute-start.2
  56.0 1.9 %shard_map.100.grad_ref = f32[512,512]{1,0:T(8,128)S(1)} custom-call(bf16[512,512]{1,0:T(8,128)(2,1)S(1)} %get-tuple-element.59.near_weight_ref, bf16[512,512]{1,0:T(8,128)(2,1)S(1)} %bitcast.12, bf16[512,512]{1,0:T(8,128)(2,1)S(1)} %get-tuple-element.60.weight_ref, bf16[512,512]{1,0:T(8,128)(2,1)S(1)} %collective-permute-done.rows_ref, ...), custom_call_target="tpu_custom_call" | custom-call | tf_op jit(solution)/shard_map/pallas_call | solution.py:93
  57.9 1.1 shard_map.101
  59.1 2.9 %shard_map.102 = (f32[1536,256]{1,0:T(8,128)S(1)}, f32[1536,256]{1,0:T(8,128)S(1)}, bf16[16,1536]{1,0:T(8,128)(2,1)S(1)}) custom-call(s32[8]{0:T(128)S(1)} %copy-done.2, s32[1]{0:T(128)} %bitcast.core_ref, f32[512,512]{1,0:T(8,128)S(1)} %shard_map.100.grad_ref, bf16[512,512]{1,0:T(8,128)(2,1)} %features_ref.7, bf16[2,512,512]{2,1,0:T(8,128)(2,1)} %get-tuple-element.50.means_ref), custom_call_target="tpu_custom_call" | custom-call | tf_op jit(solution)/shard_map/pallas_call | solution.py:93
  61.9 1.1 copy-done.1
  63.1 0.3 collective-permute-start.3
  63.3 4.6 %all-to-all-start.2 = ((bf16[64,8,640]{2,1,0:T(8,128)(2,1)}), bf16[64,8,640]{2,1,0:T(8,128)(2,1)S(1)}, u32[]{:S(2)}, u32[]{:S(2)}) async-start(bf16[64,8,640]{2,1,0:T(8,128)(2,1)} %shard_map.101), calls=%async_computation.2 | async-start | bytes 1310720 | tf_op jit(solution)/shard_map/all_to_all | solution.py:37
  68.0 0.3 collective-permute-start.4
  68.3 2.1 %add.3.known_ref = f32[1536,256]{1,0:T(8,128)S(1)} add(f32[1536,256]{1,0:T(8,128)} %copy-done.1, f32[1536,256]{1,0:T(8,128)} %collective-permute-done.3) | non-fusion elementwise | flops 393216 | bytes 4718592 | tf_op jit(solution)/shard_map/add | solution.py:442
  70.4 11.8 %all-to-all-done.2.arrived_ref = bf16[64,8,640]{2,1,0:T(8,128)(2,1)S(1)} async-done(((bf16[64,8,640]{2,1,0:T(8,128)(2,1)}), bf16[64,8,640]{2,1,0:T(8,128)(2,1)S(1)}, u32[]{:S(2)}, u32[]{:S(2)}) %all-to-all-start.2) | async-done | bytes 655392 | tf_op jit(solution)/shard_map/all_to_all | solution.py:37
  82.3 0.7 shard_map.103
  82.9 1.6 %collective-permute-start.5 = (bf16[16,256]{1,0:T(8,128)(2,1)S(1)}, bf16[16,256]{1,0:T(8,128)(2,1)S(1)}, u32[]{:S(2)}, u32[]{:S(2)}) collective-permute-start(bf16[16,256]{1,0:T(8,128)(2,1)S(1)} %get-tuple-element.74), channel_id=1, source_target_pairs={{0,1},{1,0},{2,3},{3,2},{4,5},{5,4},{6,7},{7,6},{8,9},{9,8},{10,11... | collective-permute-start | bytes 24584 | tf_op jit(solution)/shard_map/ppermute | solution.py:41
  84.5 0.8 collective-permute-done.5.other_row_ref
  85.4 0.6 shard_map.104
  86.1 19.4 %all_to_all.25 = f16[64,24,256]{2,1,0:T(8,128)(2,1)S(1)} all-to-all(f16[64,24,256]{2,1,0:T(8,128)(2,1)S(1)} %bitcast.14), channel_id=1, replica_groups=mesh['dom_0'=4,'dom_1'=4,'dom_2'=4,'dom_3'=2] {'dom_0','dom_1','dom_2'}, dimensions={0} | all-to-all | bytes 1572864 | tf_op jit(solution)/shard_map/all_to_all | solution.py:37
  105.7 18.5 %all_to_all.26 = f16[64,24,256]{2,1,0:T(8,128)(2,1)S(1)} all-to-all(f16[64,24,256]{2,1,0:T(8,128)(2,1)S(1)} %broadcast_in_dim.3), channel_id=1, replica_groups=mesh['dom_0'=4,'dom_1'=4,'dom_2'=4,'dom_3'=2] {'dom_0','dom_1','dom_2'}, dimensions={0} | all-to-all | bytes 1572864 | tf_op jit(solution)/shard_map/all_to_all | solution.py:37
  124.2 2.9 %collective-permute-start.6 = (f16[1536,256]{1,0:T(8,128)(2,1)S(1)}, f16[1536,256]{1,0:T(8,128)(2,1)S(1)}, u32[]{:S(2)}, u32[]{:S(2)}) collective-permute-start(f16[1536,256]{1,0:T(8,128)(2,1)S(1)} %bitcast.13), channel_id=1, source_target_pairs={{0,1},{1,0},{2,3},{3,2},{4,5},{5,4},{6,7},{7,6},{8,9},{9,8},{10,11... | collective-permute-start | bytes 2359304 | tf_op jit(solution)/shard_map/ppermute | solution.py:41
  127.1 1.5 %shard_map.107 = bf16[512,512]{1,0:T(8,128)(2,1)} custom-call(s32[8]{0:T(128)S(1)} %copy-done.2, f32[8,512]{1,0:T(8,128)S(1)} %get-tuple-element.82.total_ref, f32[512,512]{1,0:T(8,128)S(1)} %shard_map.100.grad_ref), custom_call_target="tpu_custom_call" | custom-call | tf_op jit(solution)/shard_map/pallas_call | solution.py:93
  128.8 1.3 shard_map.105
  130.2 1.3 shard_map.106
  (21 shorter events, 0.9 us)
Async XLA Ops:
  0.6 14.0 %copy-start.3 = (s32[512,2,8]{0,2,1:T(8,128)S(1)}, s32[512,2,8]{0,2,1:T(8,128)}, u32[]{:S(2)}) copy-start(s32[512,2,8]{0,2,1:T(8,128)} %param.10) | copy-start | bytes 98308
  3.1 25.1 %all-to-all-start = ((bf16[128,4,512]{2,1,0:T(4,128)(2,1)}), bf16[128,4,512]{2,1,0:T(4,128)(2,1)S(1)}, u32[]{:S(2)}, u32[]{:S(2)}) async-start(bf16[128,4,512]{2,1,0:T(4,128)(2,1)} %shard_map.95), calls=%async_computation | async-start | bytes 1048576 | tf_op jit(solution)/shard_map/all_to_all | solution.py:37
  14.8 13.6 %copy-start = (bf16[3,512,512]{2,1,0:T(8,128)(2,1)S(1)}, bf16[3,512,512]{2,1,0:T(8,128)(2,1)}, u32[]{:S(2)}) copy-start(bf16[3,512,512]{2,1,0:T(8,128)(2,1)} %w_ref.3) | copy-start | bytes 4718596
  14.8 13.6 %copy-start.2 = (s32[8]{0:T(128)S(1)}, s32[8]{0:T(128)}, u32[]{:S(2)}) copy-start(s32[8]{0:T(128)} %neg_ids_ref.7) | copy-start | bytes 100
  32.8 16.5 %all-to-all-start.1 = ((bf16[64,8,512]{2,1,0:T(8,128)(2,1)}), bf16[64,8,512]{2,1,0:T(8,128)(2,1)S(1)}, u32[]{:S(2)}, u32[]{:S(2)}) async-start(bf16[64,8,512]{2,1,0:T(8,128)(2,1)} %get-tuple-element.49), calls=%async_computation.1 | async-start | bytes 1048576 | tf_op jit(solution)/shard_map/all_to_all | solution.py:37
  49.3 4.3 %collective-permute-start = (bf16[512,512]{1,0:T(8,128)(2,1)S(1)}, bf16[512,512]{1,0:T(8,128)(2,1)S(1)}, u32[]{:S(2)}, u32[]{:S(2)}) collective-permute-start(bf16[512,512]{1,0:T(8,128)(2,1)S(1)} %bitcast.10), channel_id=1, source_target_pairs={{0,1},{1,0},{2,3},{3,2},{4,5},{5,4},{6,7},{7,6},{8,9},{9,8},{10,11... | collective-permute-start | bytes 1572872 | tf_op jit(solution)/shard_map/ppermute | solution.py:41
  55.4 2.5 %collective-permute-start.1 = (bf16[512,512]{1,0:T(8,128)(2,1)S(1)}, bf16[512,512]{1,0:T(8,128)(2,1)S(1)}, u32[]{:S(2)}, u32[]{:S(2)}) collective-permute-start(bf16[512,512]{1,0:T(8,128)(2,1)S(1)} %get-tuple-element.58), channel_id=1, source_target_pairs={{0,1},{1,0},{2,3},{3,2},{4,5},{5,4},{6,7},{7,6},{8,9},{9,8},{10,11... | collective-permute-start | bytes 1572872 | tf_op jit(solution)/shard_map/ppermute | solution.py:41
  55.6 2.3 %collective-permute-start.2 = (f32[8,128]{1,0:T(8,128)S(1)}, f32[8,128]{1,0:T(8,128)S(1)}, u32[]{:S(2)}, u32[]{:S(2)}) collective-permute-start(f32[8,128]{1,0:T(8,128)S(1)} %get-tuple-element.63.own_note_ref), channel_id=1, source_target_pairs={{0,1},{1,0},{2,3},{3,2},{4,5},{5,4},{6,7},{7,6},{8,9},{9,8},{10,11... | collective-permute-start | bytes 12296 | tf_op jit(solution)/shard_map/ppermute | solution.py:41
  61.9 1.1 copy-start.1
  63.1 5.2 %collective-permute-start.3 = (f32[1536,256]{1,0:T(8,128)S(1)}, f32[1536,256]{1,0:T(8,128)}, u32[]{:S(2)}, u32[]{:S(2)}) collective-permute-start(f32[1536,256]{1,0:T(8,128)S(1)} %get-tuple-element.68), channel_id=1, source_target_pairs={{0,1},{1,0},{2,3},{3,2},{4,5},{5,4},{6,7},{7,6},{8,9},{9,8},{10,11... | collective-permute-start | bytes 4718600 | tf_op jit(solution)/shard_map/ppermute | solution.py:41
  63.3 18.9 %all-to-all-start.2 = ((bf16[64,8,640]{2,1,0:T(8,128)(2,1)}), bf16[64,8,640]{2,1,0:T(8,128)(2,1)S(1)}, u32[]{:S(2)}, u32[]{:S(2)}) async-start(bf16[64,8,640]{2,1,0:T(8,128)(2,1)} %shard_map.101), calls=%async_computation.2 | async-start | bytes 1310720 | tf_op jit(solution)/shard_map/all_to_all | solution.py:37
  68.0 2.4 %collective-permute-start.4 = (bf16[16,1536]{1,0:T(8,128)(2,1)S(1)}, bf16[16,1536]{1,0:T(8,128)(2,1)S(1)}, u32[]{:S(2)}, u32[]{:S(2)}) collective-permute-start(bf16[16,1536]{1,0:T(8,128)(2,1)S(1)} %get-tuple-element.69.own_chosen_ref), channel_id=1, source_target_pairs={{0,1},{1,0},{2,3},{3,2},{4,5},{5,4},{6,7},{7,6},{8,9},{9,8},{10,11... | collective-permute-start | bytes 147464 | tf_op jit(solution)/shard_map/ppermute | solution.py:41
  82.9 2.4 %collective-permute-start.5 = (bf16[16,256]{1,0:T(8,128)(2,1)S(1)}, bf16[16,256]{1,0:T(8,128)(2,1)S(1)}, u32[]{:S(2)}, u32[]{:S(2)}) collective-permute-start(bf16[16,256]{1,0:T(8,128)(2,1)S(1)} %get-tuple-element.74), channel_id=1, source_target_pairs={{0,1},{1,0},{2,3},{3,2},{4,5},{5,4},{6,7},{7,6},{8,9},{9,8},{10,11... | collective-permute-start | bytes 24584 | tf_op jit(solution)/shard_map/ppermute | solution.py:41
  124.2 5.9 %collective-permute-start.6 = (f16[1536,256]{1,0:T(8,128)(2,1)S(1)}, f16[1536,256]{1,0:T(8,128)(2,1)S(1)}, u32[]{:S(2)}, u32[]{:S(2)}) collective-permute-start(f16[1536,256]{1,0:T(8,128)(2,1)S(1)} %bitcast.13), channel_id=1, source_target_pairs={{0,1},{1,0},{2,3},{3,2},{4,5},{5,4},{6,7},{7,6},{8,9},{9,8},{10,11... | collective-permute-start | bytes 2359304 | tf_op jit(solution)/shard_map/ppermute | solution.py:41

commit v9 on v8

--- a/solution.py
+++ b/solution.py
@@ -109,7 +109,7 @@
         out_ref[:, k, :] = lax.dot_general(hit, own, TN, preferred_element_type=F32).astype(BF16)
 
 
-def counts_body(features_ref, w_ref, nbr_ref, halo_count_ref, own_sum_ref, pre_ref, own_buf, w_buf, halo_buf, count_buf, sum_buf, pre_buf, sems):
+def counts_body(tiles_ref, features_ref, w_ref, nbr_ref, halo_count_ref, own_sum_ref, pre_ref, own_buf, w_buf, halo_buf, count_buf, sum_buf, pre_buf, sems):
     copy = pltpu.make_async_copy
     fetch_own = copy(features_ref, own_buf, sems.at[0])
     fetch_w = copy(w_ref.at[0], w_buf, sems.at[1])
@@ -377,9 +377,9 @@
     halo_count, own_sum, pre = call(
         counts_body,
         [(two, BF16, BY_HAND), (two, F32, BY_HAND), (square, F32, BY_HAND)],
-        [BY_HAND, BY_HAND, vmem()],
+        [smem(), BY_HAND, BY_HAND, vmem()],
         [pltpu.VMEM(square, BF16)] * 2 + [pltpu.VMEM(two, BF16)] * 2 + [pltpu.VMEM(two, F32), pltpu.VMEM(square, F32), pltpu.SemaphoreType.DMA((6,))],
-        (features, weights, neighbours),
+        (tile_count, features, weights, neighbours),
     )
     means, embed, picked = call(
         layer_body,

time: 132 us -> 132 us (level)
  no operation moved by 1% of the time
where the time goes in v9:
time: 132 us; the launch traced here: 131 us
  blocking collectives  37.9 us (29%)
  Pallas kernels  31.5 us (24%)
  starting transfers between devices  29 us (22%)
  waiting for transfers between devices  27.4 us (21%)
  other arithmetic  2.64 us (2%)
  between operations  1.48 us (1%)
  local copies, waits for them, and re-layouts  1.47 us (1%)
    all_to_all x2, blocking collectives, swap(): return lax.all_to_all(x, axes, split_axis=0, concat_axis=0, tiled=True)  37.9 us
    pallas_call x12, Pallas kernels, call(): pl.pallas_call(body, out_shape=made, grid=(1,), in_specs=ins, out_specs=b...  29 us
    all_to_all x3, waiting for transfers between devices, swap(): return lax.all_to_all(x, axes, split_axis=0, concat_axis=0, tiled=True)  26.6 us
    all_to_all x3, starting transfers between devices, swap(): return lax.all_to_all(x, axes, split_axis=0, concat_axis=0, tiled=True)  20.8 us
    ppermute x7, starting transfers between devices, core_swap(): return lax.ppermute(x, 'dom_3', [(0, 1), (1, 0)])  8.24 us
  transfers between devices with their start and end apart: 10, of which 4 were waited for; matrix products, arithmetic and copies ran while one was open for 2% of the time, Pallas kernels for 12%

profile of v9, /device:TPU:1, one launch (start us, length us, event | category | flops | bytes accessed | tf_op | source)
XLA Modules:
  0.0 131.4 jit_solution(16228295689990150851)
XLA Ops:
  0.6 2.5 %shard_map.95 = bf16[128,4,512]{2,1,0:T(4,128)(2,1)} custom-call(s32[4,128]{1,0:T(4,128)} %bitcast.16, bf16[512,512]{1,0:T(8,128)(2,1)} %features_ref.7), custom_call_target="tpu_custom_call" | custom-call | tf_op jit(solution)/shard_map/pallas_call | solution.py:93
  3.1 11.5 %all-to-all-start = ((bf16[128,4,512]{2,1,0:T(4,128)(2,1)}), bf16[128,4,512]{2,1,0:T(4,128)(2,1)S(1)}, u32[]{:S(2)}, u32[]{:S(2)}) async-start(bf16[128,4,512]{2,1,0:T(4,128)(2,1)} %shard_map.95), calls=%async_computation | async-start | bytes 1048576 | tf_op jit(solution)/shard_map/all_to_all | solution.py:37
  15.4 5.5 %shard_map.94 = (bf16[2,512,512]{2,1,0:T(8,128)(2,1)}, f32[2,512,512]{2,1,0:T(8,128)}, f32[512,512]{1,0:T(8,128)}) custom-call(s32[1]{0:T(128)S(6)} %copy.14.tiles_ref.count_ref, bf16[512,512]{1,0:T(8,128)(2,1)} %features_ref.7, bf16[3,512,512]{2,1,0:T(8,128)(2,1)} %w_ref.3, s32[512,16]{1,0:T(8,128)S(1)} %copy.12.nbr_ref), custom_call_target="tpu_custom_call" | custom-call | tf_op jit(solution)/shard_map/pallas_call | solution.py:93
  20.9 7.3 %all-to-all-done = bf16[128,4,512]{2,1,0:T(4,128)(2,1)S(1)} async-done(((bf16[128,4,512]{2,1,0:T(4,128)(2,1)}), bf16[128,4,512]{2,1,0:T(4,128)(2,1)S(1)}, u32[]{:S(2)}, u32[]{:S(2)}) %all-to-all-start) | async-done | bytes 524320 | tf_op jit(solution)/shard_map/all_to_all | solution.py:37
  28.4 4.4 %shard_map.96 = (bf16[2,512,512]{2,1,0:T(8,128)(2,1)}, bf16[512,512]{1,0:T(8,128)(2,1)S(1)}, bf16[64,8,512]{2,1,0:T(8,128)(2,1)}) custom-call(s32[8]{0:T(128)S(1)} %copy-done.2, bf16[2,512,512]{2,1,0:T(8,128)(2,1)} %get-tuple-element.44.count_ref, bf16[512,512]{1,0:T(8,128)(2,1)S(1)} %reshape.29.halo_ref, f32[2,512,512]{2,1,0:T(8,128)} %get-tuple-element.46.own_sum_ref, ...), custom_call_target="tpu_custom_call" | custom-call | tf_op jit(solution)/shard_map/pallas_call | solution.py:93
  32.8 4.6 %all-to-all-start.1 = ((bf16[64,8,512]{2,1,0:T(8,128)(2,1)}), bf16[64,8,512]{2,1,0:T(8,128)(2,1)S(1)}, u32[]{:S(2)}, u32[]{:S(2)}) async-start(bf16[64,8,512]{2,1,0:T(8,128)(2,1)} %get-tuple-element.49), calls=%async_computation.1 | async-start | bytes 1048576 | tf_op jit(solution)/shard_map/all_to_all | solution.py:37
  37.5 4.4 %shard_map.97 = (f32[512,512]{1,0:T(8,128)}, f32[8,128]{1,0:T(8,128)S(1)}, f32[512,128]{1,0:T(8,128)S(1)}, bf16[512,1024]{1,0:T(8,128)(2,1)S(1)}) custom-call(s32[1]{0:T(128)S(6)} %copy.14.tiles_ref.count_ref, bf16[512,512]{1,0:T(8,128)(2,1)S(1)} %get-tuple-element.48.embed_ref, s32[16,2,256]{2,1,0:T(2,128)} %ends_ref.1, bf16[512,512]{1,0:T(8,128)(2,1)} %features_ref.7, ...), custom_call_target="tpu_custom_call" | custom-call | tf_op jit(solution)/shard_map/pallas_call | solution.py:93
  41.9 7.4 %all-to-all-done.1 = bf16[64,8,512]{2,1,0:T(8,128)(2,1)S(1)} async-done(((bf16[64,8,512]{2,1,0:T(8,128)(2,1)}), bf16[64,8,512]{2,1,0:T(8,128)(2,1)S(1)}, u32[]{:S(2)}, u32[]{:S(2)}) %all-to-all-start.1) | async-done | bytes 524320 | tf_op jit(solution)/shard_map/all_to_all | solution.py:37
  49.3 2.6 %collective-permute-start = (bf16[512,512]{1,0:T(8,128)(2,1)S(1)}, bf16[512,512]{1,0:T(8,128)(2,1)S(1)}, u32[]{:S(2)}, u32[]{:S(2)}) collective-permute-start(bf16[512,512]{1,0:T(8,128)(2,1)S(1)} %bitcast.10), channel_id=1, source_target_pairs={{0,1},{1,0},{2,3},{3,2},{4,5},{5,4},{6,7},{7,6},{8,9},{9,8},{10,11... | collective-permute-start | bytes 1572872 | tf_op jit(solution)/shard_map/ppermute | solution.py:41
  51.9 1.7 %shard_map.98 = (bf16[512,512]{1,0:T(8,128)(2,1)S(1)}, f32[512,512]{1,0:T(8,128)S(1)}, f32[8,128]{1,0:T(8,128)S(1)}) custom-call(bf16[512,512]{1,0:T(8,128)(2,1)S(1)} %get-tuple-element.48.embed_ref, bf16[512,512]{1,0:T(8,128)(2,1)S(1)} %bitcast.11, bf16[512,1024]{1,0:T(8,128)(2,1)S(1)} %get-tuple-element.53.spread_ref, ...), custom_call_target="tpu_custom_call" | custom-call | tf_op jit(solution)/shard_map/pallas_call | solution.py:93
  53.6 1.7 %shard_map.99 = (bf16[512,512]{1,0:T(8,128)(2,1)S(1)}, bf16[512,512]{1,0:T(8,128)(2,1)S(1)}, f32[8,128]{1,0:T(8,128)S(1)}) custom-call(bf16[512,512]{1,0:T(8,128)(2,1)S(1)} %get-tuple-element.48.embed_ref, bf16[512,512]{1,0:T(8,128)(2,1)S(1)} %collective-permute-done.rows_ref, bf16[512,1024]{1,0:T(8,128)(2,1)S(1)} %get-tuple-element.53.spread_ref, ...), custom_call_target="tpu_custom_call" | custom-call | tf_op jit(solution)/shard_map/pallas_call | solution.py:93
  55.4 0.2 collective-permute-start.1
  55.6 0.4 collective-permute-start.2
  56.0 1.9 %shard_map.100.grad_ref = f32[512,512]{1,0:T(8,128)S(1)} custom-call(bf16[512,512]{1,0:T(8,128)(2,1)S(1)} %get-tuple-element.59.near_weight_ref, bf16[512,512]{1,0:T(8,128)(2,1)S(1)} %bitcast.12, bf16[512,512]{1,0:T(8,128)(2,1)S(1)} %get-tuple-element.60.weight_ref, bf16[512,512]{1,0:T(8,128)(2,1)S(1)} %collective-permute-done.rows_ref, ...), custom_call_target="tpu_custom_call" | custom-call | tf_op jit(solution)/shard_map/pallas_call | solution.py:93
  57.9 1.1 shard_map.101
  59.1 2.9 %shard_map.102 = (f32[1536,256]{1,0:T(8,128)S(1)}, f32[1536,256]{1,0:T(8,128)S(1)}, bf16[16,1536]{1,0:T(8,128)(2,1)S(1)}) custom-call(s32[8]{0:T(128)S(1)} %copy-done.2, s32[1]{0:T(128)} %bitcast.core_ref, f32[512,512]{1,0:T(8,128)S(1)} %shard_map.100.grad_ref, bf16[512,512]{1,0:T(8,128)(2,1)} %features_ref.7, bf16[2,512,512]{2,1,0:T(8,128)(2,1)} %get-tuple-element.50.means_ref), custom_call_target="tpu_custom_call" | custom-call | tf_op jit(solution)/shard_map/pallas_call | solution.py:93
  61.9 1.1 copy-done.1
  63.1 0.3 collective-permute-start.3
  63.3 4.6 %all-to-all-start.2 = ((bf16[64,8,640]{2,1,0:T(8,128)(2,1)}), bf16[64,8,640]{2,1,0:T(8,128)(2,1)S(1)}, u32[]{:S(2)}, u32[]{:S(2)}) async-start(bf16[64,8,640]{2,1,0:T(8,128)(2,1)} %shard_map.101), calls=%async_computation.2 | async-start | bytes 1310720 | tf_op jit(solution)/shard_map/all_to_all | solution.py:37
  68.0 0.3 collective-permute-start.4
  68.3 2.1 %add.3.known_ref = f32[1536,256]{1,0:T(8,128)S(1)} add(f32[1536,256]{1,0:T(8,128)} %copy-done.1, f32[1536,256]{1,0:T(8,128)} %collective-permute-done.3) | non-fusion elementwise | flops 393216 | bytes 4718592 | tf_op jit(solution)/shard_map/add | solution.py:442
  70.4 11.8 %all-to-all-done.2.arrived_ref = bf16[64,8,640]{2,1,0:T(8,128)(2,1)S(1)} async-done(((bf16[64,8,640]{2,1,0:T(8,128)(2,1)}), bf16[64,8,640]{2,1,0:T(8,128)(2,1)S(1)}, u32[]{:S(2)}, u32[]{:S(2)}) %all-to-all-start.2) | async-done | bytes 655392 | tf_op jit(solution)/shard_map/all_to_all | solution.py:37
  82.2 0.7 shard_map.103
  82.9 1.6 %collective-permute-start.5 = (bf16[16,256]{1,0:T(8,128)(2,1)S(1)}, bf16[16,256]{1,0:T(8,128)(2,1)S(1)}, u32[]{:S(2)}, u32[]{:S(2)}) collective-permute-start(bf16[16,256]{1,0:T(8,128)(2,1)S(1)} %get-tuple-element.74), channel_id=1, source_target_pairs={{0,1},{1,0},{2,3},{3,2},{4,5},{5,4},{6,7},{7,6},{8,9},{9,8},{10,11... | collective-permute-start | bytes 24584 | tf_op jit(solution)/shard_map/ppermute | solution.py:41
  84.5 0.8 collective-permute-done.5.other_row_ref
  85.4 0.6 shard_map.104
  86.1 19.4 %all_to_all.25 = f16[64,24,256]{2,1,0:T(8,128)(2,1)S(1)} all-to-all(f16[64,24,256]{2,1,0:T(8,128)(2,1)S(1)} %bitcast.14), channel_id=1, replica_groups=mesh['dom_0'=4,'dom_1'=4,'dom_2'=4,'dom_3'=2] {'dom_0','dom_1','dom_2'}, dimensions={0} | all-to-all | bytes 1572864 | tf_op jit(solution)/shard_map/all_to_all | solution.py:37
  105.7 18.5 %all_to_all.26 = f16[64,24,256]{2,1,0:T(8,128)(2,1)S(1)} all-to-all(f16[64,24,256]{2,1,0:T(8,128)(2,1)S(1)} %broadcast_in_dim.3), channel_id=1, replica_groups=mesh['dom_0'=4,'dom_1'=4,'dom_2'=4,'dom_3'=2] {'dom_0','dom_1','dom_2'}, dimensions={0} | all-to-all | bytes 1572864 | tf_op jit(solution)/shard_map/all_to_all | solution.py:37
  124.2 2.9 %collective-permute-start.6 = (f16[1536,256]{1,0:T(8,128)(2,1)S(1)}, f16[1536,256]{1,0:T(8,128)(2,1)S(1)}, u32[]{:S(2)}, u32[]{:S(2)}) collective-permute-start(f16[1536,256]{1,0:T(8,128)(2,1)S(1)} %bitcast.13), channel_id=1, source_target_pairs={{0,1},{1,0},{2,3},{3,2},{4,5},{5,4},{6,7},{7,6},{8,9},{9,8},{10,11... | collective-permute-start | bytes 2359304 | tf_op jit(solution)/shard_map/ppermute | solution.py:41
  127.1 1.5 %shard_map.107 = bf16[512,512]{1,0:T(8,128)(2,1)} custom-call(s32[8]{0:T(128)S(1)} %copy-done.2, f32[8,512]{1,0:T(8,128)S(1)} %get-tuple-element.82.total_ref, f32[512,512]{1,0:T(8,128)S(1)} %shard_map.100.grad_ref), custom_call_target="tpu_custom_call" | custom-call | tf_op jit(solution)/shard_map/pallas_call | solution.py:93
  128.8 1.3 shard_map.105
  130.2 1.3 shard_map.106
  (21 shorter events, 0.9 us)
Async XLA Ops:
  0.6 14.6 %copy-start.3 = (s32[512,2,8]{0,2,1:T(8,128)S(1)}, s32[512,2,8]{0,2,1:T(8,128)}, u32[]{:S(2)}) copy-start(s32[512,2,8]{0,2,1:T(8,128)} %param.10) | copy-start | bytes 98308
  3.1 25.1 %all-to-all-start = ((bf16[128,4,512]{2,1,0:T(4,128)(2,1)}), bf16[128,4,512]{2,1,0:T(4,128)(2,1)S(1)}, u32[]{:S(2)}, u32[]{:S(2)}) async-start(bf16[128,4,512]{2,1,0:T(4,128)(2,1)} %shard_map.95), calls=%async_computation | async-start | bytes 1048576 | tf_op jit(solution)/shard_map/all_to_all | solution.py:37
  15.4 13.0 %copy-start = (bf16[3,512,512]{2,1,0:T(8,128)(2,1)S(1)}, bf16[3,512,512]{2,1,0:T(8,128)(2,1)}, u32[]{:S(2)}) copy-start(bf16[3,512,512]{2,1,0:T(8,128)(2,1)} %w_ref.3) | copy-start | bytes 4718596
  15.4 13.0 %copy-start.2 = (s32[8]{0:T(128)S(1)}, s32[8]{0:T(128)}, u32[]{:S(2)}) copy-start(s32[8]{0:T(128)} %neg_ids_ref.7) | copy-start | bytes 100
  32.8 16.5 %all-to-all-start.1 = ((bf16[64,8,512]{2,1,0:T(8,128)(2,1)}), bf16[64,8,512]{2,1,0:T(8,128)(2,1)S(1)}, u32[]{:S(2)}, u32[]{:S(2)}) async-start(bf16[64,8,512]{2,1,0:T(8,128)(2,1)} %get-tuple-element.49), calls=%async_computation.1 | async-start | bytes 1048576 | tf_op jit(solution)/shard_map/all_to_all | solution.py:37
  49.3 4.3 %collective-permute-start = (bf16[512,512]{1,0:T(8,128)(2,1)S(1)}, bf16[512,512]{1,0:T(8,128)(2,1)S(1)}, u32[]{:S(2)}, u32[]{:S(2)}) collective-permute-start(bf16[512,512]{1,0:T(8,128)(2,1)S(1)} %bitcast.10), channel_id=1, source_target_pairs={{0,1},{1,0},{2,3},{3,2},{4,5},{5,4},{6,7},{7,6},{8,9},{9,8},{10,11... | collective-permute-start | bytes 1572872 | tf_op jit(solution)/shard_map/ppermute | solution.py:41
  55.4 2.5 %collective-permute-start.1 = (bf16[512,512]{1,0:T(8,128)(2,1)S(1)}, bf16[512,512]{1,0:T(8,128)(2,1)S(1)}, u32[]{:S(2)}, u32[]{:S(2)}) collective-permute-start(bf16[512,512]{1,0:T(8,128)(2,1)S(1)} %get-tuple-element.58), channel_id=1, source_target_pairs={{0,1},{1,0},{2,3},{3,2},{4,5},{5,4},{6,7},{7,6},{8,9},{9,8},{10,11... | collective-permute-start | bytes 1572872 | tf_op jit(solution)/shard_map/ppermute | solution.py:41
  55.6 2.3 %collective-permute-start.2 = (f32[8,128]{1,0:T(8,128)S(1)}, f32[8,128]{1,0:T(8,128)S(1)}, u32[]{:S(2)}, u32[]{:S(2)}) collective-permute-start(f32[8,128]{1,0:T(8,128)S(1)} %get-tuple-element.63.own_note_ref), channel_id=1, source_target_pairs={{0,1},{1,0},{2,3},{3,2},{4,5},{5,4},{6,7},{7,6},{8,9},{9,8},{10,11... | collective-permute-start | bytes 12296 | tf_op jit(solution)/shard_map/ppermute | solution.py:41
  61.9 1.1 copy-start.1
  63.1 5.2 %collective-permute-start.3 = (f32[1536,256]{1,0:T(8,128)S(1)}, f32[1536,256]{1,0:T(8,128)}, u32[]{:S(2)}, u32[]{:S(2)}) collective-permute-start(f32[1536,256]{1,0:T(8,128)S(1)} %get-tuple-element.68), channel_id=1, source_target_pairs={{0,1},{1,0},{2,3},{3,2},{4,5},{5,4},{6,7},{7,6},{8,9},{9,8},{10,11... | collective-permute-start | bytes 4718600 | tf_op jit(solution)/shard_map/ppermute | solution.py:41
  63.3 18.9 %all-to-all-start.2 = ((bf16[64,8,640]{2,1,0:T(8,128)(2,1)}), bf16[64,8,640]{2,1,0:T(8,128)(2,1)S(1)}, u32[]{:S(2)}, u32[]{:S(2)}) async-start(bf16[64,8,640]{2,1,0:T(8,128)(2,1)} %shard_map.101), calls=%async_computation.2 | async-start | bytes 1310720 | tf_op jit(solution)/shard_map/all_to_all | solution.py:37
  68.0 2.4 %collective-permute-start.4 = (bf16[16,1536]{1,0:T(8,128)(2,1)S(1)}, bf16[16,1536]{1,0:T(8,128)(2,1)S(1)}, u32[]{:S(2)}, u32[]{:S(2)}) collective-permute-start(bf16[16,1536]{1,0:T(8,128)(2,1)S(1)} %get-tuple-element.69.own_chosen_ref), channel_id=1, source_target_pairs={{0,1},{1,0},{2,3},{3,2},{4,5},{5,4},{6,7},{7,6},{8,9},{9,8},{10,11... | collective-permute-start | bytes 147464 | tf_op jit(solution)/shard_map/ppermute | solution.py:41
  82.9 2.4 %collective-permute-start.5 = (bf16[16,256]{1,0:T(8,128)(2,1)S(1)}, bf16[16,256]{1,0:T(8,128)(2,1)S(1)}, u32[]{:S(2)}, u32[]{:S(2)}) collective-permute-start(bf16[16,256]{1,0:T(8,128)(2,1)S(1)} %get-tuple-element.74), channel_id=1, source_target_pairs={{0,1},{1,0},{2,3},{3,2},{4,5},{5,4},{6,7},{7,6},{8,9},{9,8},{10,11... | collective-permute-start | bytes 24584 | tf_op jit(solution)/shard_map/ppermute | solution.py:41
  124.2 5.9 %collective-permute-start.6 = (f16[1536,256]{1,0:T(8,128)(2,1)S(1)}, f16[1536,256]{1,0:T(8,128)(2,1)S(1)}, u32[]{:S(2)}, u32[]{:S(2)}) collective-permute-start(f16[1536,256]{1,0:T(8,128)(2,1)S(1)} %bitcast.13), channel_id=1, source_target_pairs={{0,1},{1,0},{2,3},{3,2},{4,5},{5,4},{6,7},{7,6},{8,9},{9,8},{10,11... | collective-permute-start | bytes 2359304 | tf_op jit(solution)/shard_map/ppermute | solution.py:41

commit v10 on v8

--- a/solution.py
+++ b/solution.py
@@ -320,11 +320,18 @@
     other_ref[...] = row_ref[:, half_at(1 - core_ref[0])].astype(BF16)
 
 
-def pre_body(neg_ids_ref, total_ref, grad_ref, pre_ref, sum_ref):
+def pre_body(neg_ids_ref, total_ref, grad_ref, pre_ref, sum_ref, round_ref, sems):
     sum_ref[...] = grad_ref[...]
     for i in range(NEG_DEV):
         sum_ref[pl.ds(neg_ids_ref[i], 1), :] += total_ref[i : i + 1, :]
-    pre_ref[...] = sum_ref[...].astype(BF16)
+    leave = []
+    for part in range(4):
+        at = pl.ds(part * N_DOM, N_DOM)
+        round_ref[at, :] = sum_ref[at, :].astype(BF16)
+        leave.append(pltpu.make_async_copy(round_ref.at[at], pre_ref.at[at], sems.at[part]))
+        leave[part].start()
+    for one in leave:
+        one.wait()
 
 
 def update_body(known_ref, own_chosen_ref, other_chosen_ref, own_row_ref, other_row_ref, note_ref, out_ref, factor_ref):
@@ -451,9 +458,9 @@
     other_row = core_swap(send_row)
     (pre_grad,) = call(
         pre_body,
-        [hbm(square, BF16)],
+        [(square, BF16, BY_HAND)],
         [smem(), vmem(), vmem()],
-        [pltpu.VMEM(square, F32)],
+        [pltpu.VMEM(square, F32), pltpu.VMEM(square, BF16), pltpu.SemaphoreType.DMA((4,))],
         (neg_ids, total, grad),
     )
     partial, factor = call(

time: 132 us -> 132 us (level)
  no operation moved by 1% of the time
where the time goes in v10:
time: 132 us; the launch traced here: 131 us
  blocking collectives  37.9 us (29%)
  Pallas kernels  31.5 us (24%)
  starting transfers between devices  29 us (22%)
  waiting for transfers between devices  27.4 us (21%)
  other arithmetic  2.64 us (2%)
  between operations  1.49 us (1%)
  local copies, waits for them, and re-layouts  1.47 us (1%)
    all_to_all x2, blocking collectives, swap(): return lax.all_to_all(x, axes, split_axis=0, concat_axis=0, tiled=True)  37.9 us
    pallas_call x12, Pallas kernels, call(): pl.pallas_call(body, out_shape=made, grid=(1,), in_specs=ins, out_specs=b...  29 us
    all_to_all x3, waiting for transfers between devices, swap(): return lax.all_to_all(x, axes, split_axis=0, concat_axis=0, tiled=True)  26.6 us
    all_to_all x3, starting transfers between devices, swap(): return lax.all_to_all(x, axes, split_axis=0, concat_axis=0, tiled=True)  20.8 us
    ppermute x7, starting transfers between devices, core_swap(): return lax.ppermute(x, 'dom_3', [(0, 1), (1, 0)])  8.24 us
  transfers between devices with their start and end apart: 10, of which 4 were waited for; matrix products, arithmetic and copies ran while one was open for 2% of the time, Pallas kernels for 12%

profile of v10, /device:TPU:1, one launch (start us, length us, event | category | flops | bytes accessed | tf_op | source)
XLA Modules:
  0.0 131.4 jit_solution(13506570210593557730)
XLA Ops:
  0.6 2.5 %shard_map.95 = bf16[128,4,512]{2,1,0:T(4,128)(2,1)} custom-call(s32[4,128]{1,0:T(4,128)} %bitcast.16, bf16[512,512]{1,0:T(8,128)(2,1)} %features_ref.7), custom_call_target="tpu_custom_call" | custom-call | tf_op jit(solution)/shard_map/pallas_call | solution.py:93
  3.1 11.5 %all-to-all-start = ((bf16[128,4,512]{2,1,0:T(4,128)(2,1)}), bf16[128,4,512]{2,1,0:T(4,128)(2,1)S(1)}, u32[]{:S(2)}, u32[]{:S(2)}) async-start(bf16[128,4,512]{2,1,0:T(4,128)(2,1)} %shard_map.95), calls=%async_computation | async-start | bytes 1048576 | tf_op jit(solution)/shard_map/all_to_all | solution.py:37
  14.8 5.5 %shard_map.94 = (bf16[2,512,512]{2,1,0:T(8,128)(2,1)}, f32[2,512,512]{2,1,0:T(8,128)}, f32[512,512]{1,0:T(8,128)}) custom-call(bf16[512,512]{1,0:T(8,128)(2,1)} %features_ref.7, bf16[3,512,512]{2,1,0:T(8,128)(2,1)} %w_ref.3, s32[512,16]{1,0:T(8,128)S(1)} %copy.12.nbr_ref), custom_call_target="tpu_custom_call" | custom-call | tf_op jit(solution)/shard_map/pallas_call | solution.py:93
  20.3 8.0 %all-to-all-done = bf16[128,4,512]{2,1,0:T(4,128)(2,1)S(1)} async-done(((bf16[128,4,512]{2,1,0:T(4,128)(2,1)}), bf16[128,4,512]{2,1,0:T(4,128)(2,1)S(1)}, u32[]{:S(2)}, u32[]{:S(2)}) %all-to-all-start) | async-done | bytes 524320 | tf_op jit(solution)/shard_map/all_to_all | solution.py:37
  28.4 4.4 %shard_map.96 = (bf16[2,512,512]{2,1,0:T(8,128)(2,1)}, bf16[512,512]{1,0:T(8,128)(2,1)S(1)}, bf16[64,8,512]{2,1,0:T(8,128)(2,1)}) custom-call(s32[8]{0:T(128)S(1)} %copy-done.2, bf16[2,512,512]{2,1,0:T(8,128)(2,1)} %get-tuple-element.44.count_ref, bf16[512,512]{1,0:T(8,128)(2,1)S(1)} %reshape.29.halo_ref, f32[2,512,512]{2,1,0:T(8,128)} %get-tuple-element.46.own_sum_ref, ...), custom_call_target="tpu_custom_call" | custom-call | tf_op jit(solution)/shard_map/pallas_call | solution.py:93
  32.8 4.6 %all-to-all-start.1 = ((bf16[64,8,512]{2,1,0:T(8,128)(2,1)}), bf16[64,8,512]{2,1,0:T(8,128)(2,1)S(1)}, u32[]{:S(2)}, u32[]{:S(2)}) async-start(bf16[64,8,512]{2,1,0:T(8,128)(2,1)} %get-tuple-element.49), calls=%async_computation.1 | async-start | bytes 1048576 | tf_op jit(solution)/shard_map/all_to_all | solution.py:37
  38.1 4.4 %shard_map.97 = (f32[512,512]{1,0:T(8,128)}, f32[8,128]{1,0:T(8,128)S(1)}, f32[512,128]{1,0:T(8,128)S(1)}, bf16[512,1024]{1,0:T(8,128)(2,1)S(1)}) custom-call(s32[1]{0:T(128)S(6)} %copy.14.count_ref, bf16[512,512]{1,0:T(8,128)(2,1)S(1)} %get-tuple-element.48.embed_ref, s32[16,2,256]{2,1,0:T(2,128)} %ends_ref.1, bf16[512,512]{1,0:T(8,128)(2,1)} %features_ref.7, ...), custom_call_target="tpu_custom_call" | custom-call | tf_op jit(solution)/shard_map/pallas_call | solution.py:93
  42.5 6.8 %all-to-all-done.1 = bf16[64,8,512]{2,1,0:T(8,128)(2,1)S(1)} async-done(((bf16[64,8,512]{2,1,0:T(8,128)(2,1)}), bf16[64,8,512]{2,1,0:T(8,128)(2,1)S(1)}, u32[]{:S(2)}, u32[]{:S(2)}) %all-to-all-start.1) | async-done | bytes 524320 | tf_op jit(solution)/shard_map/all_to_all | solution.py:37
  49.3 2.6 %collective-permute-start = (bf16[512,512]{1,0:T(8,128)(2,1)S(1)}, bf16[512,512]{1,0:T(8,128)(2,1)S(1)}, u32[]{:S(2)}, u32[]{:S(2)}) collective-permute-start(bf16[512,512]{1,0:T(8,128)(2,1)S(1)} %bitcast.10), channel_id=1, source_target_pairs={{0,1},{1,0},{2,3},{3,2},{4,5},{5,4},{6,7},{7,6},{8,9},{9,8},{10,11... | collective-permute-start | bytes 1572872 | tf_op jit(solution)/shard_map/ppermute | solution.py:41
  51.9 1.7 %shard_map.98 = (bf16[512,512]{1,0:T(8,128)(2,1)S(1)}, f32[512,512]{1,0:T(8,128)S(1)}, f32[8,128]{1,0:T(8,128)S(1)}) custom-call(bf16[512,512]{1,0:T(8,128)(2,1)S(1)} %get-tuple-element.48.embed_ref, bf16[512,512]{1,0:T(8,128)(2,1)S(1)} %bitcast.11, bf16[512,1024]{1,0:T(8,128)(2,1)S(1)} %get-tuple-element.53.spread_ref, ...), custom_call_target="tpu_custom_call" | custom-call | tf_op jit(solution)/shard_map/pallas_call | solution.py:93
  53.6 1.7 %shard_map.99 = (bf16[512,512]{1,0:T(8,128)(2,1)S(1)}, bf16[512,512]{1,0:T(8,128)(2,1)S(1)}, f32[8,128]{1,0:T(8,128)S(1)}) custom-call(bf16[512,512]{1,0:T(8,128)(2,1)S(1)} %get-tuple-element.48.embed_ref, bf16[512,512]{1,0:T(8,128)(2,1)S(1)} %collective-permute-done.rows_ref, bf16[512,1024]{1,0:T(8,128)(2,1)S(1)} %get-tuple-element.53.spread_ref, ...), custom_call_target="tpu_custom_call" | custom-call | tf_op jit(solution)/shard_map/pallas_call | solution.py:93
  55.4 0.2 collective-permute-start.1
  55.6 0.4 collective-permute-start.2
  56.0 1.9 %shard_map.100.grad_ref = f32[512,512]{1,0:T(8,128)S(1)} custom-call(bf16[512,512]{1,0:T(8,128)(2,1)S(1)} %get-tuple-element.59.near_weight_ref, bf16[512,512]{1,0:T(8,128)(2,1)S(1)} %bitcast.12, bf16[512,512]{1,0:T(8,128)(2,1)S(1)} %get-tuple-element.60.weight_ref, bf16[512,512]{1,0:T(8,128)(2,1)S(1)} %collective-permute-done.rows_ref, ...), custom_call_target="tpu_custom_call" | custom-call | tf_op jit(solution)/shard_map/pallas_call | solution.py:93
  57.9 1.1 shard_map.101
  59.1 2.9 %shard_map.102 = (f32[1536,256]{1,0:T(8,128)S(1)}, f32[1536,256]{1,0:T(8,128)S(1)}, bf16[16,1536]{1,0:T(8,128)(2,1)S(1)}) custom-call(s32[8]{0:T(128)S(1)} %copy-done.2, s32[1]{0:T(128)} %bitcast.core_ref, f32[512,512]{1,0:T(8,128)S(1)} %shard_map.100.grad_ref, bf16[512,512]{1,0:T(8,128)(2,1)} %features_ref.7, bf16[2,512,512]{2,1,0:T(8,128)(2,1)} %get-tuple-element.50.means_ref), custom_call_target="tpu_custom_call" | custom-call | tf_op jit(solution)/shard_map/pallas_call | solution.py:93
  61.9 1.1 copy-done.1
  63.1 0.3 collective-permute-start.3
  63.3 4.6 %all-to-all-start.2 = ((bf16[64,8,640]{2,1,0:T(8,128)(2,1)}), bf16[64,8,640]{2,1,0:T(8,128)(2,1)S(1)}, u32[]{:S(2)}, u32[]{:S(2)}) async-start(bf16[64,8,640]{2,1,0:T(8,128)(2,1)} %shard_map.101), calls=%async_computation.2 | async-start | bytes 1310720 | tf_op jit(solution)/shard_map/all_to_all | solution.py:37
  68.0 0.3 collective-permute-start.4
  68.3 2.1 %add.3.known_ref = f32[1536,256]{1,0:T(8,128)S(1)} add(f32[1536,256]{1,0:T(8,128)} %copy-done.1, f32[1536,256]{1,0:T(8,128)} %collective-permute-done.3) | non-fusion elementwise | flops 393216 | bytes 4718592 | tf_op jit(solution)/shard_map/add | solution.py:449
  70.4 11.8 %all-to-all-done.2.arrived_ref = bf16[64,8,640]{2,1,0:T(8,128)(2,1)S(1)} async-done(((bf16[64,8,640]{2,1,0:T(8,128)(2,1)}), bf16[64,8,640]{2,1,0:T(8,128)(2,1)S(1)}, u32[]{:S(2)}, u32[]{:S(2)}) %all-to-all-start.2) | async-done | bytes 655392 | tf_op jit(solution)/shard_map/all_to_all | solution.py:37
  82.3 0.7 shard_map.103
  82.9 1.6 %collective-permute-start.5 = (bf16[16,256]{1,0:T(8,128)(2,1)S(1)}, bf16[16,256]{1,0:T(8,128)(2,1)S(1)}, u32[]{:S(2)}, u32[]{:S(2)}) collective-permute-start(bf16[16,256]{1,0:T(8,128)(2,1)S(1)} %get-tuple-element.74), channel_id=1, source_target_pairs={{0,1},{1,0},{2,3},{3,2},{4,5},{5,4},{6,7},{7,6},{8,9},{9,8},{10,11... | collective-permute-start | bytes 24584 | tf_op jit(solution)/shard_map/ppermute | solution.py:41
  84.5 0.8 collective-permute-done.5.other_row_ref
  85.4 0.6 shard_map.104
  86.1 19.4 %all_to_all.25 = f16[64,24,256]{2,1,0:T(8,128)(2,1)S(1)} all-to-all(f16[64,24,256]{2,1,0:T(8,128)(2,1)S(1)} %bitcast.14), channel_id=1, replica_groups=mesh['dom_0'=4,'dom_1'=4,'dom_2'=4,'dom_3'=2] {'dom_0','dom_1','dom_2'}, dimensions={0} | all-to-all | bytes 1572864 | tf_op jit(solution)/shard_map/all_to_all | solution.py:37
  105.7 18.5 %all_to_all.26 = f16[64,24,256]{2,1,0:T(8,128)(2,1)S(1)} all-to-all(f16[64,24,256]{2,1,0:T(8,128)(2,1)S(1)} %broadcast_in_dim.3), channel_id=1, replica_groups=mesh['dom_0'=4,'dom_1'=4,'dom_2'=4,'dom_3'=2] {'dom_0','dom_1','dom_2'}, dimensions={0} | all-to-all | bytes 1572864 | tf_op jit(solution)/shard_map/all_to_all | solution.py:37
  124.2 2.9 %collective-permute-start.6 = (f16[1536,256]{1,0:T(8,128)(2,1)S(1)}, f16[1536,256]{1,0:T(8,128)(2,1)S(1)}, u32[]{:S(2)}, u32[]{:S(2)}) collective-permute-start(f16[1536,256]{1,0:T(8,128)(2,1)S(1)} %bitcast.13), channel_id=1, source_target_pairs={{0,1},{1,0},{2,3},{3,2},{4,5},{5,4},{6,7},{7,6},{8,9},{9,8},{10,11... | collective-permute-start | bytes 2359304 | tf_op jit(solution)/shard_map/ppermute | solution.py:41
  127.1 1.5 %shard_map.107 = bf16[512,512]{1,0:T(8,128)(2,1)} custom-call(s32[8]{0:T(128)S(1)} %copy-done.2, f32[8,512]{1,0:T(8,128)S(1)} %get-tuple-element.82.total_ref, f32[512,512]{1,0:T(8,128)S(1)} %shard_map.100.grad_ref), custom_call_target="tpu_custom_call" | custom-call | tf_op jit(solution)/shard_map/pallas_call | solution.py:93
  128.8 1.3 shard_map.105
  130.2 1.3 shard_map.106
  (21 shorter events, 0.9 us)
Async XLA Ops:
  0.6 14.0 %copy-start.3 = (s32[512,2,8]{0,2,1:T(8,128)S(1)}, s32[512,2,8]{0,2,1:T(8,128)}, u32[]{:S(2)}) copy-start(s32[512,2,8]{0,2,1:T(8,128)} %param.10) | copy-start | bytes 98308
  3.1 25.1 %all-to-all-start = ((bf16[128,4,512]{2,1,0:T(4,128)(2,1)}), bf16[128,4,512]{2,1,0:T(4,128)(2,1)S(1)}, u32[]{:S(2)}, u32[]{:S(2)}) async-start(bf16[128,4,512]{2,1,0:T(4,128)(2,1)} %shard_map.95), calls=%async_computation | async-start | bytes 1048576 | tf_op jit(solution)/shard_map/all_to_all | solution.py:37
  14.8 13.6 %copy-start = (bf16[3,512,512]{2,1,0:T(8,128)(2,1)S(1)}, bf16[3,512,512]{2,1,0:T(8,128)(2,1)}, u32[]{:S(2)}) copy-start(bf16[3,512,512]{2,1,0:T(8,128)(2,1)} %w_ref.3) | copy-start | bytes 4718596
  14.8 13.6 %copy-start.2 = (s32[8]{0:T(128)S(1)}, s32[8]{0:T(128)}, u32[]{:S(2)}) copy-start(s32[8]{0:T(128)} %neg_ids_ref.7) | copy-start | bytes 100
  32.8 16.5 %all-to-all-start.1 = ((bf16[64,8,512]{2,1,0:T(8,128)(2,1)}), bf16[64,8,512]{2,1,0:T(8,128)(2,1)S(1)}, u32[]{:S(2)}, u32[]{:S(2)}) async-start(bf16[64,8,512]{2,1,0:T(8,128)(2,1)} %get-tuple-element.49), calls=%async_computation.1 | async-start | bytes 1048576 | tf_op jit(solution)/shard_map/all_to_all | solution.py:37
  49.3 4.3 %collective-permute-start = (bf16[512,512]{1,0:T(8,128)(2,1)S(1)}, bf16[512,512]{1,0:T(8,128)(2,1)S(1)}, u32[]{:S(2)}, u32[]{:S(2)}) collective-permute-start(bf16[512,512]{1,0:T(8,128)(2,1)S(1)} %bitcast.10), channel_id=1, source_target_pairs={{0,1},{1,0},{2,3},{3,2},{4,5},{5,4},{6,7},{7,6},{8,9},{9,8},{10,11... | collective-permute-start | bytes 1572872 | tf_op jit(solution)/shard_map/ppermute | solution.py:41
  55.4 2.5 %collective-permute-start.1 = (bf16[512,512]{1,0:T(8,128)(2,1)S(1)}, bf16[512,512]{1,0:T(8,128)(2,1)S(1)}, u32[]{:S(2)}, u32[]{:S(2)}) collective-permute-start(bf16[512,512]{1,0:T(8,128)(2,1)S(1)} %get-tuple-element.58), channel_id=1, source_target_pairs={{0,1},{1,0},{2,3},{3,2},{4,5},{5,4},{6,7},{7,6},{8,9},{9,8},{10,11... | collective-permute-start | bytes 1572872 | tf_op jit(solution)/shard_map/ppermute | solution.py:41
  55.6 2.3 %collective-permute-start.2 = (f32[8,128]{1,0:T(8,128)S(1)}, f32[8,128]{1,0:T(8,128)S(1)}, u32[]{:S(2)}, u32[]{:S(2)}) collective-permute-start(f32[8,128]{1,0:T(8,128)S(1)} %get-tuple-element.63.own_note_ref), channel_id=1, source_target_pairs={{0,1},{1,0},{2,3},{3,2},{4,5},{5,4},{6,7},{7,6},{8,9},{9,8},{10,11... | collective-permute-start | bytes 12296 | tf_op jit(solution)/shard_map/ppermute | solution.py:41
  61.9 1.1 copy-start.1
  63.1 5.2 %collective-permute-start.3 = (f32[1536,256]{1,0:T(8,128)S(1)}, f32[1536,256]{1,0:T(8,128)}, u32[]{:S(2)}, u32[]{:S(2)}) collective-permute-start(f32[1536,256]{1,0:T(8,128)S(1)} %get-tuple-element.68), channel_id=1, source_target_pairs={{0,1},{1,0},{2,3},{3,2},{4,5},{5,4},{6,7},{7,6},{8,9},{9,8},{10,11... | collective-permute-start | bytes 4718600 | tf_op jit(solution)/shard_map/ppermute | solution.py:41
  63.3 18.9 %all-to-all-start.2 = ((bf16[64,8,640]{2,1,0:T(8,128)(2,1)}), bf16[64,8,640]{2,1,0:T(8,128)(2,1)S(1)}, u32[]{:S(2)}, u32[]{:S(2)}) async-start(bf16[64,8,640]{2,1,0:T(8,128)(2,1)} %shard_map.101), calls=%async_computation.2 | async-start | bytes 1310720 | tf_op jit(solution)/shard_map/all_to_all | solution.py:37
  68.0 2.4 %collective-permute-start.4 = (bf16[16,1536]{1,0:T(8,128)(2,1)S(1)}, bf16[16,1536]{1,0:T(8,128)(2,1)S(1)}, u32[]{:S(2)}, u32[]{:S(2)}) collective-permute-start(bf16[16,1536]{1,0:T(8,128)(2,1)S(1)} %get-tuple-element.69.own_chosen_ref), channel_id=1, source_target_pairs={{0,1},{1,0},{2,3},{3,2},{4,5},{5,4},{6,7},{7,6},{8,9},{9,8},{10,11... | collective-permute-start | bytes 147464 | tf_op jit(solution)/shard_map/ppermute | solution.py:41
  82.9 2.4 %collective-permute-start.5 = (bf16[16,256]{1,0:T(8,128)(2,1)S(1)}, bf16[16,256]{1,0:T(8,128)(2,1)S(1)}, u32[]{:S(2)}, u32[]{:S(2)}) collective-permute-start(bf16[16,256]{1,0:T(8,128)(2,1)S(1)} %get-tuple-element.74), channel_id=1, source_target_pairs={{0,1},{1,0},{2,3},{3,2},{4,5},{5,4},{6,7},{7,6},{8,9},{9,8},{10,11... | collective-permute-start | bytes 24584 | tf_op jit(solution)/shard_map/ppermute | solution.py:41
  124.2 5.9 %collective-permute-start.6 = (f16[1536,256]{1,0:T(8,128)(2,1)S(1)}, f16[1536,256]{1,0:T(8,128)(2,1)S(1)}, u32[]{:S(2)}, u32[]{:S(2)}) collective-permute-start(f16[1536,256]{1,0:T(8,128)(2,1)S(1)} %bitcast.13), channel_id=1, source_target_pairs={{0,1},{1,0},{2,3},{3,2},{4,5},{5,4},{6,7},{7,6},{8,9},{9,8},{10,11... | collective-permute-start | bytes 2359304 | tf_op jit(solution)/shard_map/ppermute | solution.py:41
